TPU v7x, 128 devices: a whole 4x4x4 slice. The times are simulated.
128 devices in a mesh: gx: 4 (over x), gy: 8 (over y, core), gz: 4 (over z).
Axes of the slice: x: 4, y: 4, z: 4, core: 2. Of those that a mesh axis runs over, the one named last changes fastest.
Arguments:
- labels: int32 [128, 512, 512], P('gx', 'gy', 'gz'), may hold values from 0 to 7
- conductivity: float32 [7, 8], replicated, may hold values from -0.08 to 2, as said below
- right_side: float32 [128, 512, 512], P('gx', 'gy', 'gz'), may hold values from -18 to 18
Outputs:
- solution: float32 [128, 512, 512], P('gx', 'gy', 'gz')
Inputs may be any that keep to these rules, and one draw needn't show every extreme that they name: `conductivity`: rows 0 to 2 are positive, rows 3 to 5 have magnitude at most 0.08, row 6 is at least 0.5.
All inputs are finite; a program needn't handle non-finite values.
Results may differ from a plain program's by a relative error of at most 0.0001.
Values sent between devices are 32-bit elements; how exact they have to be, the bound alone decides.
No kernel may reach another device: no remote copies, remote signals or barrier semaphores. Data moves between devices by JAX's collectives and lax.ppermute only.
A program may use at most 128 MiB of HBM per device.

v0:
```python
import functools

import jax
import jax.numpy as jnp
from jax import lax
from jax.sharding import Mesh
from jax.sharding import PartitionSpec as P

ITERS = 3
GX_GY_GZ = ("gx", "gy_0", "gy_1", "gz")
GY = ("gy_0", "gy_1")


def with_halo(cells, sides, width):
    for axis, dim in sides:
        count = lax.axis_size(axis)
        ends = count - 1
        head = lax.slice_in_dim(cells, 0, width, axis=dim)
        tail = lax.slice_in_dim(cells, cells.shape[dim] - width, cells.shape[dim], axis=dim)
        cells = jnp.concatenate(
            [
                lax.ppermute(tail, axis, [(i, (i + 1) % count) for i in range(ends)]),
                cells,
                lax.ppermute(head, axis, [((i + 1) % count, i) for i in range(ends)]),
            ],
            axis=dim,
        )
    return cells


def by_axis(shard, axes):
    return functools.reduce(lax.psum, axes, shard)


def neighbour_value(arr, shift_x, shift_y, shift_z, cell_grid):
    size_x, size_y, size_z = cell_grid
    return arr[
        ...,
        1 + shift_x : 1 + shift_x + size_x,
        1 + shift_y : 1 + shift_y + size_y,
        1 + shift_z : 1 + shift_z + size_z,
    ]


def stencil_apply(padded_value, padded_sigma, self_coefficient):
    cell_grid = self_coefficient.shape
    value_entry = neighbour_value(padded_value, 0, 0, 0, cell_grid)
    total_flux = self_coefficient * value_entry
    for axis in range(3):
        for sign in (-1, 1):
            stencil_offset = [0, 0, 0]
            stencil_offset[axis] = sign
            face_flux = 0.5 * (
                neighbour_value(padded_sigma[axis], 0, 0, 0, cell_grid)
                + neighbour_value(
                    padded_sigma[axis],
                    stencil_offset[0],
                    stencil_offset[1],
                    stencil_offset[2],
                    cell_grid,
                )
            )
            total_flux = total_flux + face_flux * (
                value_entry
                - neighbour_value(
                    padded_value, stencil_offset[0], stencil_offset[1], stencil_offset[2], cell_grid
                )
            )
    for first, second, comp in ((0, 1, 3), (0, 2, 4), (1, 2, 5)):
        for sign_a in (-1, 1):
            for sign_b in (-1, 1):
                stencil_offset = [0, 0, 0]
                stencil_offset[first] = sign_a
                stencil_offset[second] = sign_b
                cross_term = (
                    0.25
                    * sign_a
                    * sign_b
                    * (
                        neighbour_value(padded_sigma[comp], 0, 0, 0, cell_grid)
                        + neighbour_value(
                            padded_sigma[comp],
                            stencil_offset[0],
                            stencil_offset[1],
                            stencil_offset[2],
                            cell_grid,
                        )
                    )
                )
                total_flux = total_flux - cross_term * neighbour_value(
                    padded_value, stencil_offset[0], stencil_offset[1], stencil_offset[2], cell_grid
                )
    return total_flux


def diagonal_of(padded_sigma, self_coefficient):
    cell_grid = self_coefficient.shape
    total_flux = self_coefficient
    for axis in range(3):
        for sign in (-1, 1):
            stencil_offset = [0, 0, 0]
            stencil_offset[axis] = sign
            total_flux = total_flux + 0.5 * (
                neighbour_value(padded_sigma[axis], 0, 0, 0, cell_grid)
                + neighbour_value(
                    padded_sigma[axis],
                    stencil_offset[0],
                    stencil_offset[1],
                    stencil_offset[2],
                    cell_grid,
                )
            )
    return total_flux


def lookup(shifted, conductivity):
    total_flux = jnp.zeros((7,) + shifted.shape, jnp.float32)
    for label in range(conductivity.shape[1]):
        hit = (shifted == label + 1).astype(jnp.float32)
        total_flux = total_flux + hit[None] * conductivity[:, label][:, None, None, None]
    return total_flux


def apply_operator(field, padded_sigma, self_coefficient):
    field_pad = with_halo(field, (("gx", 0), (GY, 1), ("gz", 2)), 1)
    return stencil_apply(field_pad, padded_sigma, self_coefficient)


def local(labels, conductivity, right_side):
    shifted = labels + 1
    shifted_pad = with_halo(shifted, (("gx", 0), (GY, 1), ("gz", 2)), 1)
    table_pad = lookup(shifted_pad, conductivity)
    padded_sigma = table_pad[:6]
    self_coefficient = table_pad[6, 1:-1, 1:-1, 1:-1]
    diag = diagonal_of(padded_sigma, self_coefficient)
    solution = jnp.zeros_like(right_side)
    residual = right_side
    precond = residual / diag
    applied = apply_operator(precond, padded_sigma, self_coefficient)
    gamma_old = jnp.float32(1.0)
    alpha_old = jnp.float32(1.0)
    direction = precond
    for step in range(ITERS):
        gamma, delta = (
            by_axis(jnp.sum(residual * precond), GX_GY_GZ),
            by_axis(jnp.sum(applied * precond), GX_GY_GZ),
        )
        if step + 1 < ITERS:
            scaled = applied / diag
            product = apply_operator(scaled, padded_sigma, self_coefficient)
        if step == 0:
            alpha = gamma / delta
            direction = precond
            along_z = product
            along_q = scaled
            along_s = applied
        else:
            ratio = gamma / gamma_old
            alpha = gamma / (delta - ratio * gamma / alpha_old)
            direction = precond + ratio * direction
            if step + 1 < ITERS:
                along_z = product + ratio * along_z
                along_q = scaled + ratio * along_q
                along_s = applied + ratio * along_s
        solution = solution + alpha * direction
        if step + 1 < ITERS:
            residual = residual - alpha * along_s
            precond = precond - alpha * along_q
            applied = applied - alpha * along_z
        gamma_old = gamma
        alpha_old = alpha
    return solution


def solution(mesh):
    finer = Mesh(
        mesh.devices.reshape(mesh.shape["gx"], 4, 2, mesh.shape["gz"]), ("gx", "gy_0", "gy_1", "gz")
    )
    in_specs = (P("gx", GY, "gz"), P(), P("gx", GY, "gz"))
    out_specs = P("gx", GY, "gz")
    return jax.shard_map(local, mesh=finer, in_specs=in_specs, out_specs=out_specs, check_vma=False)
```

profile of v0, /device:TPU:1, one launch (start us, length us, event | category | flops | bytes accessed | tf_op | source)
XLA Modules:
  0.0 380.2 jit_solution(2394452676744524515)
XLA Ops:
  1.3 3.9 %collective-permute-start = (s32[1,64,128]{2,1,0:T(8,128)S(1)}, s32[1,64,128]{2,1,0:T(8,128)S(1)}, u32[]{:S(2)}, u32[]{:S(2)}) collective-permute-start(s32[1,64,128]{2,1,0:T(8,128)S(1)} %get-tuple-element.101), channel_id=1, source_target_pairs={{0,32},{32,64},{64,96},{1,33},{33,65},{65,97},{2,34},{34,66},{66,9... | collective-permute-start | bytes 98312 | tf_op jit(solution)/shard_map/ppermute | solution.py:22
  10.1 5.2 %collective-permute-start.2 = (s32[34,1,128]{2,0,1:T(8,128)S(1)}, s32[34,1,128]{2,0,1:T(8,128)S(1)}, u32[]{:S(2)}, u32[]{:S(2)}) collective-permute-start(s32[34,1,128]{2,0,1:T(8,128)S(1)} %copy.91), channel_id=1, source_target_pairs={{0,4},{4,8},{8,12},{12,16},{16,20},{20,24},{24,28},{1,5},{5,9},{9,... | collective-permute-start | bytes 52232 | tf_op jit(solution)/shard_map/ppermute | solution.py:22
  25.4 4.2 %collective-permute-start.4 = (s32[34,66,1]{1,0,2:T(8,128)S(1)}, s32[34,66,1]{1,0,2:T(8,128)S(1)}, u32[]{:S(2)}, u32[]{:S(2)}) collective-permute-start(s32[34,66,1]{1,0,2:T(8,128)S(1)} %copy.67), channel_id=1, source_target_pairs={{0,1},{1,2},{2,3},{4,5},{5,6},{6,7},{8,9},{9,10},{10,11},{12,13},{... | collective-permute-start | bytes 26936 | tf_op jit(solution)/shard_map/ppermute | solution.py:22
  36.7 7.6 %compare_convert_fusion.6 = (f32[34,66,130]{1,2,0:T(8,128)}, f32[34,66,130]{1,2,0:T(8,128)}, f32[34,66,130]{1,2,0:T(8,128)}, f32[34,66,130]{1,2,0:T(8,128)}, f32...) fusion(s32[34,66,130]{1,2,0:T(8,128)} %get-tuple-element.53), kind=kLoop, calls=%fused_computation.20 | loop fusion | flops 4084080 | bytes 9335040 | tf_op jit(solution)/shard_map/convert_element_type | solution.py:119
  70.4 16.9 %multiply_add_fusion = f32[7,34,66,130]{3,2,1,0:T(8,128)} fusion(f32[7]{0:T(128)S(1)} %get-tuple-element.15, f32[34,66,130]{2,1,0:T(8,128)} %copy.78, f32[7]{0:T(128)S(1)} %get-tuple-element.16, f32[34,66,130]{2,1,0:T(8,128)} %copy.77, f32[7]{0:T(128)S(1)} %get-tuple-element.10, f32[34,66,130]{2,1,0:T(8,128)} %copy.76, f32[7]{0:T(128)S(1)} %get-tuple-element.11, ...), kind=kLoop, calls=%fused_computation | loop fusion | flops 30630600 | bytes 17503424 | tf_op jit(solution)/shard_map/add | solution.py:120
  87.3 10.0 %slice_bitcast_fusion.2 = (f32[34,66,130]{2,1,0:T(8,128)S(1)}, f32[34,66,130]{2,1,0:T(8,128)}, f32[34,66,130]{2,1,0:T(8,128)}, f32[34,66,130]{2,1,0:T(8,128)}, f...) fusion(f32[7,34,66,130]{3,2,1,0:T(8,128)} %multiply_add_fusion), kind=kLoop, calls=%fused_computation.3 | loop fusion | bytes 14002560 | tf_op jit(solution)/shard_map/squeeze | solution.py:80
  97.3 12.8 %fusion.104 = (f32[32,64,128]{2,1,0:T(8,128)S(1)}, f32[32,64,128]{2,1,0:T(8,128)}, f32[32,64,128]{2,1,0:T(8,128)}, f32[32,64,128]{2,1,0:T(8,128)}, f32[32,64,128...) fusion(f32[32,64,128]{2,1,0:T(8,128)} %param.5, ...), kind=kLoop, calls=%fused_computation.239 | loop fusion | flops 4980736 | bytes 19922944 | tf_op jit(solution)/shard_map/div | solution.py:138
  118.0 5.8 %collective-permute-start.8 = (f32[34,1,128]{2,1,0:T(1,128)S(1)}, f32[34,1,128]{2,1,0:T(1,128)S(1)}, u32[]{:S(2)}, u32[]{:S(2)}) collective-permute-start(f32[34,1,128]{2,1,0:T(1,128)S(1)} %get-tuple-element.91), channel_id=1, source_target_pairs={{0,4},{4,8},{8,12},{12,16},{16,20},{20,24},{24,28},{1,5},{5,9},{9,... | collective-permute-start | bytes 52232 | tf_op jit(solution)/shard_map/ppermute | solution.py:22
  137.4 5.2 %collective-permute-start.10 = (f32[34,66,1]{1,2,0:T(1,128)}, f32[34,66,1]{1,2,0:T(1,128)}, u32[]{:S(2)}, u32[]{:S(2)}) collective-permute-start(f32[34,66,1]{1,2,0:T(1,128)} %copy.79), channel_id=1, source_target_pairs={{0,1},{1,2},{2,3},{4,5},{5,6},{6,7},{8,9},{9,10},{10,11},{12,13},{... | collective-permute-start | bytes 26936 | tf_op jit(solution)/shard_map/ppermute | solution.py:22
  153.9 10.2 %multiply_reduce_fusion.3 = (f32[]{:T(128)}, f32[]{:T(128)}, f32[32,64,128]{2,1,0:T(8,128)S(1)}) fusion(f32[32,64,128]{2,1,0:T(8,128)S(1)} %get-tuple-element.44, f32[32,64,128]{2,1,0:T(8,128)} %param.5, f32[34,66,129]{2,1,0:T(8,128)S(1)} %get-tuple-element.80, f32[34,66,130]{2,1,0:T(8,128)S(1)} %copy-done, f32[34,66,129]{2,1,0:T(8,128)S(1)} %get-tuple-element.79, ...), kind=kLoop, calls=%fused_computation.214 | loop fusion | flops 19136512 | bytes 43057160 | tf_op jit(solution)/shard_map/reduce_sum | solution.py:146
  172.5 3.8 %collective-permute-start.14 = (f32[34,1,128]{2,1,0:T(1,128)}, f32[34,1,128]{2,1,0:T(1,128)}, u32[]{:S(2)}, u32[]{:S(2)}) collective-permute-start(f32[34,1,128]{2,1,0:T(1,128)} %get-tuple-element.87), channel_id=1, source_target_pairs={{0,4},{4,8},{8,12},{12,16},{16,20},{20,24},{24,28},{1,5},{5,9},{9,... | collective-permute-start | bytes 52232 | tf_op jit(solution)/shard_map/ppermute | solution.py:22
  178.3 6.7 %all-reduce.8 = (f32[]{:T(128)}, f32[]{:T(128)}) all-reduce(f32[]{:T(128)} %get-tuple-element.8, f32[]{:T(128)} %get-tuple-element.7), channel_id=1, replica_groups=mesh['gx'=4,'gy_0'=4,'gy_1'=2,'gz'=4] {'gx'}, use_global_device_ids=true, to_apply=%region_1.0 | all-reduce | flops 2 | bytes 16 | tf_op jit(solution)/shard_map/psum | solution.py:32
  185.0 8.6 %all-reduce.5 = (f32[]{:T(128)}, f32[]{:T(128)}) all-reduce(f32[]{:T(128)} %get-tuple-element.33, f32[]{:T(128)} %get-tuple-element.34), channel_id=1, replica_groups=mesh['gx'=4,'gy_0'=4,'gy_1'=2,'gz'=4] {'gy_0'}, use_global_device_ids=true, to_apply=%region_2.0 | all-reduce | flops 2 | bytes 16 | tf_op jit(solution)/shard_map/psum | solution.py:32
  193.6 7.6 %all-reduce.11 = (f32[]{:T(128)}, f32[]{:T(128)}) all-reduce(f32[]{:T(128)} %get-tuple-element.27, f32[]{:T(128)} %get-tuple-element.28), channel_id=1, replica_groups=mesh['gx'=4,'gy_0'=4,'gy_1'=2,'gz'=4] {'gy_1'}, use_global_device_ids=true, to_apply=%region_3.0 | all-reduce | flops 2 | bytes 16 | tf_op jit(solution)/shard_map/psum | solution.py:32
  201.2 10.4 %all-reduce.2 = (f32[]{:T(128)}, f32[]{:T(128)}) all-reduce(f32[]{:T(128)} %get-tuple-element.39, f32[]{:T(128)} %get-tuple-element.40), channel_id=1, replica_groups=mesh['gx'=4,'gy_0'=4,'gy_1'=2,'gz'=4] {'gz'}, use_global_device_ids=true, to_apply=%region_4.0 | all-reduce | flops 2 | bytes 16 | tf_op jit(solution)/shard_map/psum | solution.py:32
  222.2 4.6 %collective-permute-start.16 = (f32[34,66,1]{1,2,0:T(1,128)}, f32[34,66,1]{1,2,0:T(1,128)}, u32[]{:S(2)}, u32[]{:S(2)}) collective-permute-start(f32[34,66,1]{1,2,0:T(1,128)} %copy.83), channel_id=1, source_target_pairs={{0,1},{1,2},{2,3},{4,5},{5,6},{6,7},{8,9},{9,10},{10,11},{12,13},{... | collective-permute-start | bytes 26936 | tf_op jit(solution)/shard_map/ppermute | solution.py:22
  234.6 4.1 %maximum_maximum_fusion.1 = (f32[34,66,129]{2,1,0:T(8,128)S(1)}, f32[34,66,129]{2,1,0:T(8,128)S(1)}) fusion(f32[34,1,128]{2,1,0:T(1,128)} %collective-permute-done.15, f32[1,64,128]{2,1,0:T(8,128)} %copy-done.26, f32[32,64,128]{2,1,0:T(8,128)} %copy-done.6, f32[1,64,128]{2,1,0:T(8,128)} %copy-done.24, f32[34,1,128]{2,1,0:T(1,128)} %collective-permute-done.14, ...), kind=kLoop, calls=%fused_computation.9 | loop fusion | flops 2894760 | bytes 3482688 | tf_op jit(solution)/shard_map/concatenate | solution.py:20
  239.4 9.7 %fusion.101 = (f32[32,64,128]{2,1,0:T(8,128)S(1)}, f32[32,64,128]{2,1,0:T(8,128)S(1)}) fusion(f32[32,64,128]{2,1,0:T(8,128)S(1)} %copy-done.16, f32[32,64,128]{2,1,0:T(8,128)S(1)} %copy-done.10, f32[]{:T(128)S(6)} %div.31, f32[34,66,129]{2,1,0:T(8,128)S(1)} %get-tuple-element.78, f32[34,66,130]{2,1,0:T(8,128)S(1)} %copy-done.1, ...), kind=kLoop, calls=%fused_computation.218 | loop fusion | flops 18874368 | bytes 45154308 | tf_op jit(solution)/shard_map/div | solution.py:149
  249.8 4.2 %collective-permute-start.18 = (f32[1,64,128]{2,1,0:T(8,128)}, f32[1,64,128]{2,1,0:T(8,128)}, u32[]{:S(2)}, u32[]{:S(2)}) collective-permute-start(f32[1,64,128]{2,1,0:T(8,128)} %get-tuple-element.95), channel_id=1, source_target_pairs={{0,32},{32,64},{64,96},{1,33},{33,65},{65,97},{2,34},{34,66},{66,9... | collective-permute-start | bytes 98312 | tf_op jit(solution)/shard_map/ppermute | solution.py:22
  256.6 8.6 %all-reduce.7 = (f32[]{:T(128)}, f32[]{:T(128)}) all-reduce(f32[]{:T(128)} %get-tuple-element.6, f32[]{:T(128)} %get-tuple-element.5), channel_id=1, replica_groups=mesh['gx'=4,'gy_0'=4,'gy_1'=2,'gz'=4] {'gx'}, use_global_device_ids=true, to_apply=%region_11.0 | all-reduce | flops 2 | bytes 16 | tf_op jit(solution)/shard_map/psum | solution.py:32
  265.2 6.7 %all-reduce.4 = (f32[]{:T(128)}, f32[]{:T(128)}) all-reduce(f32[]{:T(128)} %get-tuple-element.31, f32[]{:T(128)} %get-tuple-element.32), channel_id=1, replica_groups=mesh['gx'=4,'gy_0'=4,'gy_1'=2,'gz'=4] {'gy_0'}, use_global_device_ids=true, to_apply=%region_12.0 | all-reduce | flops 2 | bytes 16 | tf_op jit(solution)/shard_map/psum | solution.py:32
  271.9 10.1 %all-reduce.10 = (f32[]{:T(128)}, f32[]{:T(128)}) all-reduce(f32[]{:T(128)} %get-tuple-element.25, f32[]{:T(128)} %get-tuple-element.26), channel_id=1, replica_groups=mesh['gx'=4,'gy_0'=4,'gy_1'=2,'gz'=4] {'gy_1'}, use_global_device_ids=true, to_apply=%region_13.0 | all-reduce | flops 2 | bytes 16 | tf_op jit(solution)/shard_map/psum | solution.py:32
  281.9 6.8 %all-reduce.1 = (f32[]{:T(128)}, f32[]{:T(128)}) all-reduce(f32[]{:T(128)} %get-tuple-element.37, f32[]{:T(128)} %get-tuple-element.38), channel_id=1, replica_groups=mesh['gx'=4,'gy_0'=4,'gy_1'=2,'gz'=4] {'gz'}, use_global_device_ids=true, to_apply=%region_14.0 | all-reduce | flops 2 | bytes 16 | tf_op jit(solution)/shard_map/psum | solution.py:32
  294.1 5.7 %collective-permute-start.20 = (f32[34,1,128]{2,1,0:T(1,128)S(1)}, f32[34,1,128]{2,1,0:T(1,128)S(1)}, u32[]{:S(2)}, u32[]{:S(2)}) collective-permute-start(f32[34,1,128]{2,1,0:T(1,128)S(1)} %get-tuple-element.83), channel_id=1, source_target_pairs={{0,4},{4,8},{8,12},{12,16},{16,20},{20,24},{24,28},{1,5},{5,9},{9,... | collective-permute-start | bytes 52232 | tf_op jit(solution)/shard_map/ppermute | solution.py:22
  302.1 3.8 %multiply_reduce_fusion = f32[]{:T(128)} fusion(f32[32,64,128]{2,1,0:T(8,128)} %copy-done.9, f32[32,64,128]{2,1,0:T(8,128)} %param.5, f32[]{:T(128)S(6)} %div.33, f32[]{:T(128)S(6)} %div.35, f32[]{:T(128)S(6)} %div.31, f32[32,64,128]{2,1,0:T(8,128)} %copy-done.17, f32[32,64,128]{2,1,0:T(8,128)} %copy-done.6, f32[32,64,128]{2,1,0:T(8,128)} %get-tuple-element.45, ...), kind=kLoop, calls=%fused_computation.207 | loop fusion | flops 4456447 | bytes 6291472 | tf_op jit(solution)/shard_map/reduce_sum | solution.py:145
  314.7 4.7 %collective-permute-start.22 = (f32[34,66,1]{1,2,0:T(1,128)}, f32[34,66,1]{1,2,0:T(1,128)}, u32[]{:S(2)}, u32[]{:S(2)}) collective-permute-start(f32[34,66,1]{1,2,0:T(1,128)} %copy.87), channel_id=1, source_target_pairs={{0,1},{1,2},{2,3},{4,5},{5,6},{6,7},{8,9},{9,10},{10,11},{12,13},{... | collective-permute-start | bytes 26936 | tf_op jit(solution)/shard_map/ppermute | solution.py:22
  327.2 4.1 %maximum_maximum_fusion.2 = (f32[34,66,129]{2,1,0:T(8,128)S(1)}, f32[34,66,129]{2,1,0:T(8,128)S(1)}) fusion(f32[34,1,128]{2,1,0:T(1,128)} %copy-done.35, f32[1,64,128]{2,1,0:T(8,128)} %collective-permute-done.19, f32[32,64,128]{2,1,0:T(8,128)} %copy-done.12, f32[1,64,128]{2,1,0:T(8,128)} %collective-permute-done.18, f32[34,1,128]{2,1,0:T(1,128)} %copy-done.33, ...), kind=kLoop, calls=%fused_computation.11 | loop fusion | flops 2894760 | bytes 3482688 | tf_op jit(solution)/shard_map/concatenate | solution.py:20
  332.0 10.9 %fusion.5 = f32[]{:T(128)} fusion(f32[34,66,129]{2,1,0:T(8,128)S(1)} %get-tuple-element.76, f32[34,66,129]{2,1,0:T(8,128)S(1)} %get-tuple-element.75, f32[34,65,128]{2,1,0:T(8,128)} %get-tuple-element.82, f32[34,65,128]{2,1,0:T(8,128)} %get-tuple-element.81, f32[32,64,128]{2,1,0:T(8,128)} %get-tuple-element.51, f32[32,64,128]{2,1,0:T(8,128)S(1)} %copy-done.14, ...), kind=kLoop, calls=%fused_computation.38 | loop fusion | flops 22020096 | bytes 46202896 | tf_op jit(solution)/shard_map/reduce_sum | solution.py:146
  342.9 6.7 %all-reduce.6 = (f32[]{:T(128)}, f32[]{:T(128)}) all-reduce(f32[]{:T(128)} %multiply_reduce_fusion, f32[]{:T(128)} %fusion.5), channel_id=1, replica_groups=mesh['gx'=4,'gy_0'=4,'gy_1'=2,'gz'=4] {'gx'}, use_global_device_ids=true, to_apply=%region_21.0 | all-reduce | flops 2 | bytes 16 | tf_op jit(solution)/shard_map/psum | solution.py:32
  349.6 6.7 %all-reduce.3 = (f32[]{:T(128)}, f32[]{:T(128)}) all-reduce(f32[]{:T(128)} %get-tuple-element.29, f32[]{:T(128)} %get-tuple-element.30), channel_id=1, replica_groups=mesh['gx'=4,'gy_0'=4,'gy_1'=2,'gz'=4] {'gy_0'}, use_global_device_ids=true, to_apply=%region_22.0 | all-reduce | flops 2 | bytes 16 | tf_op jit(solution)/shard_map/psum | solution.py:32
  356.3 8.7 %all-reduce.9 = (f32[]{:T(128)}, f32[]{:T(128)}) all-reduce(f32[]{:T(128)} %get-tuple-element.23, f32[]{:T(128)} %get-tuple-element.24), channel_id=1, replica_groups=mesh['gx'=4,'gy_0'=4,'gy_1'=2,'gz'=4] {'gy_1'}, use_global_device_ids=true, to_apply=%region_23.0 | all-reduce | flops 2 | bytes 16 | tf_op jit(solution)/shard_map/psum | solution.py:32
  365.1 7.6 %all-reduce = (f32[]{:T(128)}, f32[]{:T(128)}) all-reduce(f32[]{:T(128)} %get-tuple-element.35, f32[]{:T(128)} %get-tuple-element.36), channel_id=1, replica_groups=mesh['gx'=4,'gy_0'=4,'gy_1'=2,'gz'=4] {'gz'}, use_global_device_ids=true, to_apply=%region_24.0 | all-reduce | flops 2 | bytes 16 | tf_op jit(solution)/shard_map/psum | solution.py:32
  (167 shorter events, 137.6 us)
Async XLA Ops:
  1.3 5.2 %collective-permute-start = (s32[1,64,128]{2,1,0:T(8,128)S(1)}, s32[1,64,128]{2,1,0:T(8,128)S(1)}, u32[]{:S(2)}, u32[]{:S(2)}) collective-permute-start(s32[1,64,128]{2,1,0:T(8,128)S(1)} %get-tuple-element.101), channel_id=1, source_target_pairs={{0,32},{32,64},{64,96},{1,33},{33,65},{65,97},{2,34},{34,66},{66,9... | collective-permute-start | bytes 98312 | tf_op jit(solution)/shard_map/ppermute | solution.py:22
  5.3 4.7 %collective-permute-start.1 = (s32[1,64,128]{2,1,0:T(8,128)S(1)}, s32[1,64,128]{2,1,0:T(8,128)S(1)}, u32[]{:S(2)}, u32[]{:S(2)}) collective-permute-start(s32[1,64,128]{2,1,0:T(8,128)S(1)} %get-tuple-element.102), channel_id=1, source_target_pairs={{32,0},{64,32},{96,64},{33,1},{65,33},{97,65},{34,2},{66,34},{98,6... | collective-permute-start | bytes 98312 | tf_op jit(solution)/shard_map/ppermute | solution.py:24
  10.1 8.0 %collective-permute-start.2 = (s32[34,1,128]{2,0,1:T(8,128)S(1)}, s32[34,1,128]{2,0,1:T(8,128)S(1)}, u32[]{:S(2)}, u32[]{:S(2)}) collective-permute-start(s32[34,1,128]{2,0,1:T(8,128)S(1)} %copy.91), channel_id=1, source_target_pairs={{0,4},{4,8},{8,12},{12,16},{16,20},{20,24},{24,28},{1,5},{5,9},{9,... | collective-permute-start | bytes 52232 | tf_op jit(solution)/shard_map/ppermute | solution.py:22
  15.3 5.1 %collective-permute-start.3 = (s32[34,1,128]{2,0,1:T(8,128)S(1)}, s32[34,1,128]{2,0,1:T(8,128)S(1)}, u32[]{:S(2)}, u32[]{:S(2)}) collective-permute-start(s32[34,1,128]{2,0,1:T(8,128)S(1)} %copy.92), channel_id=1, source_target_pairs={{4,0},{8,4},{12,8},{16,12},{20,16},{24,20},{28,24},{5,1},{9,5},{13... | collective-permute-start | bytes 52232 | tf_op jit(solution)/shard_map/ppermute | solution.py:24
  22.5 8.0 %copy-start.18 = (s32[34,1,128]{1,2,0:T(8,128)S(1)}, s32[34,1,128]{1,2,0:T(8,128)}, u32[]{:S(2)}) copy-start(s32[34,1,128]{1,2,0:T(8,128)} %copy.64) | copy-start | bytes 52228
  22.5 8.0 %copy-start.19 = (s32[34,1,128]{1,2,0:T(8,128)S(1)}, s32[34,1,128]{1,2,0:T(8,128)}, u32[]{:S(2)}) copy-start(s32[34,1,128]{1,2,0:T(8,128)} %copy.66) | copy-start | bytes 52228
  24.0 5.9 %collective-permute-start.5 = (s32[34,66,1]{1,0,2:T(8,128)S(1)}, s32[34,66,1]{1,0,2:T(8,128)S(1)}, u32[]{:S(2)}, u32[]{:S(2)}) collective-permute-start(s32[34,66,1]{1,0,2:T(8,128)S(1)} %copy.68), channel_id=1, source_target_pairs={{1,0},{2,1},{3,2},{5,4},{6,5},{7,6},{9,8},{10,9},{11,10},{13,12},{... | collective-permute-start | bytes 26936 | tf_op jit(solution)/shard_map/ppermute | solution.py:24
  25.4 5.1 %collective-permute-start.4 = (s32[34,66,1]{1,0,2:T(8,128)S(1)}, s32[34,66,1]{1,0,2:T(8,128)S(1)}, u32[]{:S(2)}, u32[]{:S(2)}) collective-permute-start(s32[34,66,1]{1,0,2:T(8,128)S(1)} %copy.67), channel_id=1, source_target_pairs={{0,1},{1,2},{2,3},{4,5},{5,6},{6,7},{8,9},{9,10},{10,11},{12,13},{... | collective-permute-start | bytes 26936 | tf_op jit(solution)/shard_map/ppermute | solution.py:22
  110.1 4.4 %collective-permute-start.6 = (f32[1,64,128]{2,1,0:T(8,128)S(1)}, f32[1,64,128]{2,1,0:T(8,128)S(1)}, u32[]{:S(2)}, u32[]{:S(2)}) collective-permute-start(f32[1,64,128]{2,1,0:T(8,128)S(1)} %get-tuple-element.99), channel_id=1, source_target_pairs={{0,32},{32,64},{64,96},{1,33},{33,65},{65,97},{2,34},{34,66},{66,9... | collective-permute-start | bytes 98312 | tf_op jit(solution)/shard_map/ppermute | solution.py:22
  113.2 4.7 %collective-permute-start.7 = (f32[1,64,128]{2,1,0:T(8,128)S(1)}, f32[1,64,128]{2,1,0:T(8,128)S(1)}, u32[]{:S(2)}, u32[]{:S(2)}) collective-permute-start(f32[1,64,128]{2,1,0:T(8,128)S(1)} %get-tuple-element.100), channel_id=1, source_target_pairs={{32,0},{64,32},{96,64},{33,1},{65,33},{97,65},{34,2},{66,34},{98,6... | collective-permute-start | bytes 98312 | tf_op jit(solution)/shard_map/ppermute | solution.py:24
  114.5 14.3 %copy-start.28 = (f32[1,64,128]{2,1,0:T(8,128)}, f32[1,64,128]{2,1,0:T(8,128)S(1)}, u32[]{:S(2)}) copy-start(f32[1,64,128]{2,1,0:T(8,128)S(1)} %collective-permute-done.6) | copy-start | bytes 98308
  117.9 10.9 %copy-start.30 = (f32[1,64,128]{2,1,0:T(8,128)}, f32[1,64,128]{2,1,0:T(8,128)S(1)}, u32[]{:S(2)}) copy-start(f32[1,64,128]{2,1,0:T(8,128)S(1)} %collective-permute-done.7) | copy-start | bytes 98308
  118.0 7.7 %collective-permute-start.8 = (f32[34,1,128]{2,1,0:T(1,128)S(1)}, f32[34,1,128]{2,1,0:T(1,128)S(1)}, u32[]{:S(2)}, u32[]{:S(2)}) collective-permute-start(f32[34,1,128]{2,1,0:T(1,128)S(1)} %get-tuple-element.91), channel_id=1, source_target_pairs={{0,4},{4,8},{8,12},{12,16},{16,20},{20,24},{24,28},{1,5},{5,9},{9,... | collective-permute-start | bytes 52232 | tf_op jit(solution)/shard_map/ppermute | solution.py:22
  123.7 5.1 %collective-permute-start.9 = (f32[34,1,128]{2,1,0:T(1,128)S(1)}, f32[34,1,128]{2,1,0:T(1,128)S(1)}, u32[]{:S(2)}, u32[]{:S(2)}) collective-permute-start(f32[34,1,128]{2,1,0:T(1,128)S(1)} %get-tuple-element.92), channel_id=1, source_target_pairs={{4,0},{8,4},{12,8},{16,12},{20,16},{24,20},{28,24},{5,1},{9,5},{13... | collective-permute-start | bytes 52232 | tf_op jit(solution)/shard_map/ppermute | solution.py:24
  136.1 11.3 %collective-permute-start.11 = (f32[34,66,1]{1,2,0:T(1,128)}, f32[34,66,1]{1,2,0:T(1,128)}, u32[]{:S(2)}, u32[]{:S(2)}) collective-permute-start(f32[34,66,1]{1,2,0:T(1,128)} %copy.81), channel_id=1, source_target_pairs={{1,0},{2,1},{3,2},{5,4},{6,5},{7,6},{9,8},{10,9},{11,10},{13,12},{... | collective-permute-start | bytes 26936 | tf_op jit(solution)/shard_map/ppermute | solution.py:24
  137.4 7.7 %collective-permute-start.10 = (f32[34,66,1]{1,2,0:T(1,128)}, f32[34,66,1]{1,2,0:T(1,128)}, u32[]{:S(2)}, u32[]{:S(2)}) collective-permute-start(f32[34,66,1]{1,2,0:T(1,128)} %copy.79), channel_id=1, source_target_pairs={{0,1},{1,2},{2,3},{4,5},{5,6},{6,7},{8,9},{9,10},{10,11},{12,13},{... | collective-permute-start | bytes 26936 | tf_op jit(solution)/shard_map/ppermute | solution.py:22
  153.9 10.2 %copy-start.15 = (f32[32,64,128]{2,1,0:T(8,128)S(1)}, f32[32,64,128]{2,1,0:T(8,128)}, u32[]{:S(2)}) copy-start(f32[32,64,128]{2,1,0:T(8,128)} %get-tuple-element.45) | copy-start | bytes 3145732
  164.1 8.4 %copy-start.9 = (f32[32,64,128]{2,1,0:T(8,128)}, f32[32,64,128]{2,1,0:T(8,128)S(1)}, u32[]{:S(2)}) copy-start(f32[32,64,128]{2,1,0:T(8,128)S(1)} %get-tuple-element.43) | copy-start | bytes 3145732
  164.3 7.5 %copy-start.6 = (f32[32,64,128]{2,1,0:T(8,128)}, f32[32,64,128]{2,1,0:T(8,128)S(1)}, u32[]{:S(2)}) copy-start(f32[32,64,128]{2,1,0:T(8,128)S(1)} %div.32) | copy-start | bytes 3145732
  164.4 4.1 %collective-permute-start.12 = (f32[1,64,128]{2,1,0:T(8,128)S(1)}, f32[1,64,128]{2,1,0:T(8,128)S(1)}, u32[]{:S(2)}, u32[]{:S(2)}) collective-permute-start(f32[1,64,128]{2,1,0:T(8,128)S(1)} %get-tuple-element.97), channel_id=1, source_target_pairs={{0,32},{32,64},{64,96},{1,33},{33,65},{65,97},{2,34},{34,66},{66,9... | collective-permute-start | bytes 98312 | tf_op jit(solution)/shard_map/ppermute | solution.py:22
  167.2 4.7 %collective-permute-start.13 = (f32[1,64,128]{2,1,0:T(8,128)S(1)}, f32[1,64,128]{2,1,0:T(8,128)S(1)}, u32[]{:S(2)}, u32[]{:S(2)}) collective-permute-start(f32[1,64,128]{2,1,0:T(8,128)S(1)} %get-tuple-element.98), channel_id=1, source_target_pairs={{32,0},{64,32},{96,64},{33,1},{65,33},{97,65},{34,2},{66,34},{98,6... | collective-permute-start | bytes 98312 | tf_op jit(solution)/shard_map/ppermute | solution.py:24
  172.5 40.4 %collective-permute-start.14 = (f32[34,1,128]{2,1,0:T(1,128)}, f32[34,1,128]{2,1,0:T(1,128)}, u32[]{:S(2)}, u32[]{:S(2)}) collective-permute-start(f32[34,1,128]{2,1,0:T(1,128)} %get-tuple-element.87), channel_id=1, source_target_pairs={{0,4},{4,8},{8,12},{12,16},{16,20},{20,24},{24,28},{1,5},{5,9},{9,... | collective-permute-start | bytes 52232 | tf_op jit(solution)/shard_map/ppermute | solution.py:22
  176.4 36.6 %collective-permute-start.15 = (f32[34,1,128]{2,1,0:T(1,128)}, f32[34,1,128]{2,1,0:T(1,128)}, u32[]{:S(2)}, u32[]{:S(2)}) collective-permute-start(f32[34,1,128]{2,1,0:T(1,128)} %get-tuple-element.88), channel_id=1, source_target_pairs={{4,0},{8,4},{12,8},{16,12},{20,16},{24,20},{28,24},{5,1},{9,5},{13... | collective-permute-start | bytes 52232 | tf_op jit(solution)/shard_map/ppermute | solution.py:24
  220.9 11.4 %collective-permute-start.17 = (f32[34,66,1]{1,2,0:T(1,128)}, f32[34,66,1]{1,2,0:T(1,128)}, u32[]{:S(2)}, u32[]{:S(2)}) collective-permute-start(f32[34,66,1]{1,2,0:T(1,128)} %copy.85), channel_id=1, source_target_pairs={{1,0},{2,1},{3,2},{5,4},{6,5},{7,6},{9,8},{10,9},{11,10},{13,12},{... | collective-permute-start | bytes 26936 | tf_op jit(solution)/shard_map/ppermute | solution.py:24
  222.2 7.8 %collective-permute-start.16 = (f32[34,66,1]{1,2,0:T(1,128)}, f32[34,66,1]{1,2,0:T(1,128)}, u32[]{:S(2)}, u32[]{:S(2)}) collective-permute-start(f32[34,66,1]{1,2,0:T(1,128)} %copy.83), channel_id=1, source_target_pairs={{0,1},{1,2},{2,3},{4,5},{5,6},{6,7},{8,9},{9,10},{10,11},{12,13},{... | collective-permute-start | bytes 26936 | tf_op jit(solution)/shard_map/ppermute | solution.py:22
  239.4 15.9 %copy-start.23 = (f32[32,64,128]{2,1,0:T(8,128)S(1)}, f32[32,64,128]{2,1,0:T(8,128)}, u32[]{:S(2)}) copy-start(f32[32,64,128]{2,1,0:T(8,128)} %param.5) | copy-start | bytes 3145732
  249.8 43.2 %collective-permute-start.18 = (f32[1,64,128]{2,1,0:T(8,128)}, f32[1,64,128]{2,1,0:T(8,128)}, u32[]{:S(2)}, u32[]{:S(2)}) collective-permute-start(f32[1,64,128]{2,1,0:T(8,128)} %get-tuple-element.95), channel_id=1, source_target_pairs={{0,32},{32,64},{64,96},{1,33},{33,65},{65,97},{2,34},{34,66},{66,9... | collective-permute-start | bytes 98312 | tf_op jit(solution)/shard_map/ppermute | solution.py:22
  254.0 39.0 %collective-permute-start.19 = (f32[1,64,128]{2,1,0:T(8,128)}, f32[1,64,128]{2,1,0:T(8,128)}, u32[]{:S(2)}, u32[]{:S(2)}) collective-permute-start(f32[1,64,128]{2,1,0:T(8,128)} %get-tuple-element.96), channel_id=1, source_target_pairs={{32,0},{64,32},{96,64},{33,1},{65,33},{97,65},{34,2},{66,34},{98,6... | collective-permute-start | bytes 98312 | tf_op jit(solution)/shard_map/ppermute | solution.py:24
  294.1 11.8 %collective-permute-start.20 = (f32[34,1,128]{2,1,0:T(1,128)S(1)}, f32[34,1,128]{2,1,0:T(1,128)S(1)}, u32[]{:S(2)}, u32[]{:S(2)}) collective-permute-start(f32[34,1,128]{2,1,0:T(1,128)S(1)} %get-tuple-element.83), channel_id=1, source_target_pairs={{0,4},{4,8},{8,12},{12,16},{16,20},{20,24},{24,28},{1,5},{5,9},{9,... | collective-permute-start | bytes 52232 | tf_op jit(solution)/shard_map/ppermute | solution.py:22
  299.8 6.1 %collective-permute-start.21 = (f32[34,1,128]{2,1,0:T(1,128)S(1)}, f32[34,1,128]{2,1,0:T(1,128)S(1)}, u32[]{:S(2)}, u32[]{:S(2)}) collective-permute-start(f32[34,1,128]{2,1,0:T(1,128)S(1)} %get-tuple-element.84), channel_id=1, source_target_pairs={{4,0},{8,4},{12,8},{16,12},{20,16},{24,20},{28,24},{5,1},{9,5},{13... | collective-permute-start | bytes 52232 | tf_op jit(solution)/shard_map/ppermute | solution.py:24
  313.4 11.5 %collective-permute-start.23 = (f32[34,66,1]{1,2,0:T(1,128)}, f32[34,66,1]{1,2,0:T(1,128)}, u32[]{:S(2)}, u32[]{:S(2)}) collective-permute-start(f32[34,66,1]{1,2,0:T(1,128)} %copy.89), channel_id=1, source_target_pairs={{1,0},{2,1},{3,2},{5,4},{6,5},{7,6},{9,8},{10,9},{11,10},{13,12},{... | collective-permute-start | bytes 26936 | tf_op jit(solution)/shard_map/ppermute | solution.py:24
  314.7 8.0 %collective-permute-start.22 = (f32[34,66,1]{1,2,0:T(1,128)}, f32[34,66,1]{1,2,0:T(1,128)}, u32[]{:S(2)}, u32[]{:S(2)}) collective-permute-start(f32[34,66,1]{1,2,0:T(1,128)} %copy.87), channel_id=1, source_target_pairs={{0,1},{1,2},{2,3},{4,5},{5,6},{6,7},{8,9},{9,10},{10,11},{12,13},{... | collective-permute-start | bytes 26936 | tf_op jit(solution)/shard_map/ppermute | solution.py:22
  (29 other events, 126.9 us)
where the time goes:
time: 384 us; the launch traced here: 380 us
  other arithmetic  109 us (28%)
  blocking collectives  95.2 us (25%)
  local copies, waits for them, and re-layouts  80.6 us (21%)
  starting transfers between devices  71.7 us (19%)
  waiting for transfers between devices  14 us (4%)
  between operations  10.1 us (3%)
    psum x12, blocking collectives, by_axis(): return functools.reduce(lax.psum, axes, shard)  95.2 us
    ppermute x12, starting transfers between devices, with_halo(): lax.ppermute(tail, axis, [(i, (i + 1) % count) for i in range(ends)])  53.2 us
    convert_element_type x8, local copies, waits for them, and re-layouts, lookup(): hit = (shifted == label + 1).astype(jnp.float32)  28.8 us
    concatenate x10, other arithmetic, with_halo(): jnp.concatenate([lax.ppermute(tail, axis, [(i, (i + 1) % count) for i in...  23.5 us
    reduce_sum x3, other arithmetic, local(): jnp.sum(applied * precond)  22.3 us
    ppermute x12, starting transfers between devices, with_halo(): lax.ppermute(head, axis, [((i + 1) % count, i) for i in range(ends)])  18.5 us
    add x1, other arithmetic, lookup(): total_flux + hit[None] * conductivity[:, label][:, None, None, None]  16.9 us
    ppermute x12, waiting for transfers between devices, with_halo(): lax.ppermute(head, axis, [((i + 1) % count, i) for i in range(ends)])  13.4 us
  transfers between devices with their start and end apart: 24, of which 6 were waited for; matrix products, arithmetic and copies ran while one was open for 6% of the time, Pallas kernels for 0%

commit v1 on v0

v1 whole, which is shorter than its diff:
```python
import jax
import jax.numpy as jnp
from jax import lax
from jax.experimental import pallas as pl
from jax.experimental.pallas import tpu as pltpu
from jax.sharding import PartitionSpec as P

LABELS = 8
ALL = ("gx", "gy", "gz")
NX, NY, NZ = 32, 64, 128
XP, RW = NX + 8, NY + 16
OWN = slice(8, 8 + NY)
F32 = jnp.float32


def ring(arr, axis, step):
    count = lax.axis_size(axis)
    return lax.ppermute(arr, axis, [(i, (i + step) % count) for i in range(count)])


def iota(shape, dim):
    return lax.broadcasted_iota(jnp.int32, shape, dim)


def pack_rows(lab0, lab7, b0, b7, xu0, xu7, xl0, xl7, up, down):
    low = iota((8, 128), 0) < 4

    def put(xp, lab_first, lab_last, b_first, b_last):
        up[xp] = jnp.where(low, b_first, pltpu.roll(lab_first, 4, 0))
        down[xp] = jnp.where(low, pltpu.roll(lab_last, 4, 0), b_last)

    def own(x, carry):
        put(x + 4, lab0[x].astype(F32), lab7[x].astype(F32), b0[x], b7[x])
        return carry

    lax.fori_loop(0, NX, own, 0)
    zero = jnp.zeros((8, 128), F32)
    for k in range(4):
        bk = (xl0[k - 1], xl7[k - 1]) if k else (zero, zero)
        put(k, xl0[3 + k], xl7[3 + k], *bk)
        bk = (xu0[k], xu7[k]) if k < 3 else (zero, zero)
        put(36 + k, xu0[3 + k], xu7[3 + k], *bk)


def rows_lab(yu, yd, xp):
    low = iota((8, 128), 0) < 4
    return pltpu.roll(jnp.where(low, yd[xp], yu[xp]), 4, 0)


def rows_b(yu, yd, xp):
    low = iota((8, 128), 0) < 4
    return jnp.where(low, yu[xp], yd[xp])


def pack_lanes(lab, b, xu, xl, yu, yd, up, down, acc_lab, acc_b):
    group = iota((RW, 128), 1) // 8

    def put(xp, lab_own, b_own):
        k = xp % 16
        g = xp // 16
        lab8 = rows_lab(yu, yd, xp)
        b8 = rows_b(yu, yd, xp)
        hit = group == k
        shift = 8 * k + 4
        full = jnp.concatenate([lab8, lab_own, lab8], 0)
        acc_lab[g] = jnp.where(hit, pltpu.roll(full, shift, 1), acc_lab[g])
        full = jnp.concatenate([b8, b_own, b8], 0)
        acc_b[g] = jnp.where(hit, pltpu.roll(full, shift, 1), acc_b[g])

    acc_lab[...] = jnp.zeros((3, RW, 128), F32)
    acc_b[...] = jnp.zeros((3, RW, 128), F32)

    def own(x, carry):
        put(x + 4, lab[x].astype(F32), b[x])
        return carry

    lax.fori_loop(0, NX, own, 0)
    zero = jnp.zeros((NY, 128), F32)
    for k in range(4):
        put(k, xl[3 + k], xl[k - 1] if k else zero)
        put(36 + k, xu[3 + k], xu[k] if k < 3 else zero)
    first = iota((RW, 128), 1) % 8 < 4
    for g in range(3):
        down[g] = jnp.where(first, acc_lab[g], pltpu.roll(acc_b[g], 4, 1))
        up[g] = jnp.where(first, pltpu.roll(acc_b[g], 124, 1), acc_lab[g])


def sweeps(
    cond, lab, b, xu, xl, yu, yd, zu_own, zd_own, zu, zd,
    w0o, w1o, w2o, mom,
    s0, s1, s2, s3, s4, s5, inv, mid, v0, v1, v2, dz, ac, u3, u4, u5,
    q0, q1, q2, q3, q4, q5, qinv, qmid, qv0, qv1, qv2, qdz, qac, p3, p4, p5,
    wide, patch_v, patch_q, row_v, row_q,
):
    sig = (s0, s1, s2, s3, s4, s5)
    qsig = (q0, q1, q2, q3, q4, q5)
    gx, gy, gz = (lax.axis_index(a) for a in ALL)
    not_first_x = (gx > 0).astype(F32)
    not_last_x = (gx < lax.axis_size("gx") - 1).astype(F32)
    not_first_y = (gy > 0).astype(F32)
    not_last_y = (gy < lax.axis_size("gy") - 1).astype(F32)
    not_first_z = (gz > 0).astype(F32)
    not_last_z = (gz < lax.axis_size("gz") - 1).astype(F32)

    sub8 = iota((8, 128), 0)
    tables = []
    for c in range(7):
        t = jnp.zeros((8, 128), F32)
        scale = 0.5 if c < 3 else (0.25 if c < 6 else 1.0)
        for l in range(LABELS):
            t = jnp.where(sub8 == l, cond[c, l] * scale, t)
        tables.append(t)

    mass = sum(cond[6, l] for l in range(LABELS))
    faces = sum(cond[c, l] for c in range(3) for l in range(LABELS)) * 2.0
    theta = jnp.full((1, 128), faces, F32) / jnp.full((1, 128), faces + mass, F32)

    def look(c, idx):
        return jnp.take_along_axis(tables[c], idx, axis=0, mode="promise_in_bounds")

    def entries(idx, on):
        vals = [look(c, idx) for c in range(7)]
        if on is not None:
            vals = [v * on for v in vals]
        centre = vals[6] + 2.0 * (vals[0] + vals[1] + vals[2])
        return vals[:6], centre

    row_on = jnp.where(sub8 < 4, not_last_y, not_first_y)

    def table_plane(xp, labels_of, b_own, on):
        for g in range(8):
            vals, centre = entries(labels_of(g), on)
            at = pl.ds(8 + 8 * g, 8)
            for c in range(6):
                sig[c][xp, at] = vals[c]
            inv[xp, at] = centre
        vals, centre = entries(
            rows_lab(yu, yd, xp).astype(jnp.int32), row_on if on is None else row_on * on
        )
        b8 = rows_b(yu, yd, xp)
        for at in (pl.ds(0, 8), pl.ds(72, 8)):
            for c in range(6):
                sig[c][xp, at] = vals[c]
            inv[xp, at] = centre
            v0[xp, at] = b8
        v0[xp, OWN] = b_own

    def own_plane(x, carry):
        table_plane(x + 4, lambda g: lab[x, pl.ds(8 * g, 8)], b[x], None)
        return carry

    lax.fori_loop(0, NX, own_plane, 0)
    zero = jnp.zeros((NY, 128), F32)

    def low_plane(k, carry):
        table_plane(
            k,
            lambda g: xl[3 + k, pl.ds(8 * g, 8)].astype(jnp.int32),
            xl[jnp.maximum(k - 1, 0)],
            not_first_x,
        )
        return carry

    def high_plane(k, carry):
        table_plane(
            36 + k,
            lambda g: xu[3 + k, pl.ds(8 * g, 8)].astype(jnp.int32),
            xu[jnp.minimum(k, 2)],
            not_last_x,
        )
        return carry

    lax.fori_loop(0, 4, low_plane, 0)
    lax.fori_loop(0, 4, high_plane, 0)

    first = iota((RW, 128), 1) % 8 < 4
    wide[...] = jnp.zeros((128, 128), F32)
    lane = iota((8, 128), 1)
    lane_on = jnp.where(
        lane < 8, not_first_y, jnp.where(lane >= 72, not_last_y, 1.0)
    )
    low_on = jnp.where(sub8 < 4, not_first_z, 1.0) * lane_on
    high_on = jnp.where(sub8 < 4, 1.0, not_last_z) * lane_on

    def turned(arr):
        wide[pl.ds(0, RW)] = arr
        return wide[...].T

    for g in range(3):
        count = 16 if g < 2 else 8
        base = 16 * g
        parts = (
            (0, low_on, turned(jnp.where(first, zd[g], zu_own[g])),
             turned(jnp.where(first, zu_own[g], zd[g]))),
            (8, high_on, turned(jnp.where(first, zd_own[g], zu[g])),
             turned(jnp.where(first, zu[g], zd_own[g]))),
        )
        for off, on, labs, bs in parts:
            for k in range(count):
                xp = base + k
                here = on
                if xp < 4:
                    here = on * not_first_x
                if xp >= 36:
                    here = on * not_last_x
                idx = jnp.clip(labs[8 * k : 8 * k + 8].astype(jnp.int32), 0, LABELS - 1)
                vals, centre = entries(idx, here)
                for c in range(6):
                    qsig[c][xp, pl.ds(off, 8)] = vals[c]
                qinv[xp, pl.ds(off, 8)] = centre
                qv0[xp, pl.ds(off, 8)] = pltpu.roll(bs[8 * k : 8 * k + 8], 4, 0)

    def set_patch(patch, rows):
        patch[...] = rows[...].T[:RW]

    lane_main = iota((RW, 128), 1)

    def z_sides(value, patch, xp, at=None):
        p = patch[...] if at is None else patch[at]
        p = pltpu.roll(p, 127 - 2 * xp, 1)
        ln = iota(value.shape, 1)
        left = jnp.where(ln == 0, p, pltpu.roll(value, 1, 1))
        right = jnp.where(ln == 127, p, pltpu.roll(value, 127, 1))
        return left, right

    row_v[...] = jnp.zeros((128, 128), F32)
    row_q[...] = jnp.zeros((128, 128), F32)

    def q_diag(xp, carry):
        c = qinv[xp]
        f1 = q1[xp]
        f2 = q2[xp]
        total = c + (q0[xp + 1] + q0[xp - 1])
        total = total + (pltpu.roll(f1, 1, 1) + pltpu.roll(f1, 127, 1))
        total = total + (pltpu.roll(f2, 1, 0) + pltpu.roll(f2, 15, 0))
        r = jnp.where(c > 0, 1.0 / jnp.where(c > 0, total, 1.0), 0.0)
        qinv[xp] = r
        qmid[xp] = theta * total
        w = qv0[xp] * r
        qv0[xp] = w
        row_q[pl.ds(2 * xp + 1, 1)] = f2[3:4]
        row_q[pl.ds(2 * xp, 1)] = f2[12:13]
        row_v[pl.ds(2 * xp + 1, 1)] = w[3:4]
        row_v[pl.ds(2 * xp, 1)] = w[12:13]
        return carry

    lax.fori_loop(1, XP - 1, q_diag, 0)
    set_patch(patch_q, row_q)
    set_patch(patch_v, row_v)

    def diag_rows(xp, at, size):
        c = inv[xp, pl.ds(at, size)]
        left, right = z_sides(s2[xp, pl.ds(at, size)], patch_q, xp, pl.ds(at, size))
        total = c + (s0[xp + 1, pl.ds(at, size)] + s0[xp - 1, pl.ds(at, size)])
        total = total + (s1[xp, pl.ds(at + 1, size)] + s1[xp, pl.ds(at - 1, size)])
        total = total + (left + right)
        r = jnp.where(c > 0, 1.0 / jnp.where(c > 0, total, 1.0), 0.0)
        rhs = v0[xp, pl.ds(at, size)]
        return r, rhs, rhs * r, theta * total

    def add(acc, value):
        total, lost = acc
        value = value - lost
        new = total + value
        return new, (new - total) - value

    def fold(value):
        return jnp.sum(value.reshape(-1, 8, 128), axis=0)

    def main_diag(xp, acc):
        r8, _, w8, m8 = diag_rows(xp, 71, 8)
        r1, _, w1_, m1 = diag_rows(xp, 1, 8)
        r, rhs, w, m = diag_rows(xp, 8, NY)
        mid[xp, pl.ds(71, 8)] = m8
        mid[xp, pl.ds(1, 8)] = m1
        mid[xp, OWN] = m
        inv[xp, pl.ds(71, 8)] = r8
        inv[xp, pl.ds(1, 8)] = r1
        inv[xp, OWN] = r
        v0[xp, pl.ds(71, 8)] = w8
        v0[xp, pl.ds(1, 8)] = w1_
        v0[xp, OWN] = w
        mine = jnp.logical_and(xp >= 4, xp < 36).astype(F32)
        return add(acc, fold(rhs * w) * mine)

    zero8 = jnp.zeros((8, 128), F32)
    none = (zero8, zero8)
    nu0 = lax.fori_loop(1, XP - 1, main_diag, none)

    def apply(v, w, qv, qw, lo, hi, last):
        def q_first(xp, carry):
            x = qv[xp]
            left = pltpu.roll(x, 1, 0)
            right = pltpu.roll(x, 15, 0)
            qdz[xp] = right - left
            qac[xp] = q2[xp] * (left + right)
            p3[xp] = q3[xp] * x
            p4[xp] = q4[xp] * x
            p5[xp] = q5[xp] * x
            return carry

        lax.fori_loop(lo - 1, hi + 1, q_first, 0)

        def q_second(xp, carry):
            def dy(x):
                return pltpu.roll(x, 127, 1) - pltpu.roll(x, 1, 1)

            x = qv[xp]
            u2 = q2[xp] * x
            q = (p4[xp + 1] - p4[xp - 1]) + dy(p5[xp])
            plus = u2 + q
            minus = u2 - q
            row_q[pl.ds(2 * xp + 1, 1)] = minus[3:4]
            row_q[pl.ds(2 * xp, 1)] = plus[12:13]
            if not last:
                f0 = q0[xp]
                xa, xb = qv[xp + 1], qv[xp - 1]
                r = (qac[xp] - qmid[xp] * x) + (f0 + q0[xp + 1]) * xa + (f0 + q0[xp - 1]) * xb
                u1 = q1[xp] * x
                t = p3[xp + 1] - p3[xp - 1]
                r = r + q1[xp] * (pltpu.roll(x, 127, 1) + pltpu.roll(x, 1, 1))
                r = r + pltpu.roll(u1 + t, 127, 1) + pltpu.roll(u1 - t, 1, 1)
                r = r + q3[xp] * dy(xa - xb)
                r = r + q4[xp] * (qdz[xp + 1] - qdz[xp - 1])
                r = r + q5[xp] * dy(qdz[xp])
                r = r + pltpu.roll(plus, 15, 0) + pltpu.roll(minus, 1, 0)
                out = r * qinv[xp]
                qw[xp] = out
                row_v[pl.ds(2 * xp + 1, 1)] = out[3:4]
                row_v[pl.ds(2 * xp, 1)] = out[12:13]
            return carry

        lax.fori_loop(lo, hi, q_second, 0)
        set_patch(patch_q, row_q)

        def first_pass(xp, carry):
            x = v[xp]
            left, right = z_sides(x, patch_v, xp)
            dz[xp] = right - left
            ac[xp] = s2[xp] * (left + right)
            u3[xp] = s3[xp] * x
            u4[xp] = s4[xp] * x
            u5[xp] = s5[xp] * x
            return carry

        lax.fori_loop(lo - 1, hi + 1, first_pass, 0)

        def rows_of(xp, at, size):
            here = pl.ds(at, size)
            nxt = pl.ds(at + 1, size)
            prv = pl.ds(at - 1, size)
            f0 = s0[xp, here]
            x = v[xp, here]
            r = ac[xp, here] - mid[xp, here] * x
            r = r + (f0 + s0[xp + 1, here]) * v[xp + 1, here]
            r = r + (f0 + s0[xp - 1, here]) * v[xp - 1, here]
            f1 = s1[xp, here]
            r = r + (f1 + s1[xp, nxt]) * v[xp, nxt]
            r = r + (f1 + s1[xp, prv]) * v[xp, prv]
            cross = (v[xp + 1, nxt] - v[xp - 1, nxt]) - (v[xp + 1, prv] - v[xp - 1, prv])
            r = r + s3[xp, here] * cross
            r = r + ((u3[xp + 1, nxt] - u3[xp - 1, nxt]) - (u3[xp + 1, prv] - u3[xp - 1, prv]))
            r = r + s4[xp, here] * (dz[xp + 1, here] - dz[xp - 1, here])
            r = r + s5[xp, here] * (dz[xp, nxt] - dz[xp, prv])
            u2 = s2[xp, here] * x
            q = (u4[xp + 1, here] - u4[xp - 1, here]) + (u5[xp, nxt] - u5[xp, prv])
            p = pltpu.roll(patch_q[here], 127 - 2 * xp, 1)
            ln = iota(q.shape, 1)
            r = r + jnp.where(ln == 127, p, pltpu.roll(u2 + q, 127, 1))
            r = r + jnp.where(ln == 0, p, pltpu.roll(u2 - q, 1, 1))
            return x, r

        def second_pass(xp, acc):
            if last:
                x, r = rows_of(xp, 8, NY)
                return (add(acc[0], fold(x * r)), acc[1])
            for at in (71, 1):
                _, r = rows_of(xp, at, 8)
                w[xp, pl.ds(at, 8)] = r * inv[xp, pl.ds(at, 8)]
            x, r = rows_of(xp, 8, NY)
            out = r * inv[xp, OWN]
            w[xp, OWN] = out
            mine = jnp.logical_and(xp >= 4, xp < 36).astype(F32)
            return add(acc[0], fold(x * r) * mine), add(acc[1], fold(out * r) * mine)

        out = lax.fori_loop(lo, hi, second_pass, (none, none))
        if not last:
            set_patch(patch_v, row_v)
        return out

    nu1, nu2 = apply(v0, v1, qv0, qv1, 2, XP - 2, False)
    nu3, nu4 = apply(v1, v2, qv1, qv2, 3, XP - 3, False)
    nu5, _ = apply(v2, None, qv2, None, 4, XP - 4, True)

    def store(x, carry):
        w0o[x] = v0[x + 4, OWN]
        w1o[x] = v1[x + 4, OWN]
        w2o[x] = v2[x + 4, OWN]
        return carry

    lax.fori_loop(0, NX, store, 0)
    line = jnp.zeros((1, 128), F32)
    at = iota((1, 128), 1)
    line = jnp.where(at == 6, theta, line)
    for k, (nu, _) in enumerate((nu0, nu1, nu2, nu3, nu4, nu5)):
        part = jnp.sum(jnp.sum(nu, axis=0, keepdims=True), axis=1, keepdims=True)
        line = jnp.where(at == k, part, line)
    mom[...] = jnp.broadcast_to(line, mom.shape)


def combine(mom, w0, w1, w2, out):
    total = jnp.sum(mom[...], axis=0, keepdims=True)
    at = iota((1, 128), 1)
    m = [jnp.sum(jnp.where(at == k, total, 0.0), axis=1, keepdims=True) for k in range(7)]
    rest = 1.0 - m[6] * (1.0 / mom.shape[0])
    a = [rest * m[k] - m[k + 1] for k in range(5)]
    tiny = 1e-7

    def ratio(p, q, limit):
        ok = q > limit
        return jnp.where(ok, p / jnp.where(ok, q, 1.0), 0.0)

    l10 = a[1] / a[0]
    l20 = a[2] / a[0]
    d1 = a[2] - l10 * a[1]
    e12 = a[3] - l10 * a[2]
    g1 = m[1] - l10 * m[0]
    l21 = ratio(e12, d1, tiny * a[2])
    d2 = a[4] - l20 * a[2] - l21 * e12
    g2 = m[2] - l20 * m[0] - l21 * g1
    c2 = ratio(g2, d2, tiny * a[4])
    c1 = ratio(g1, d1, tiny * a[2]) - l21 * c2
    c0 = (m[0] - a[1] * c1 - a[2] * c2) / a[0]

    def plane(x, carry):
        out[x] = c0 * w0[x] + c1 * w1[x] + c2 * w2[x]
        return carry

    lax.fori_loop(0, NX, plane, 0)


def vmem():
    return pl.BlockSpec(memory_space=pltpu.VMEM)


def local(labels, conductivity, right_side):
    xu_own = jnp.concatenate([right_side[:3], labels[:4].astype(F32)], 0)
    xl_own = jnp.concatenate([right_side[NX - 3 :], labels[NX - 4 :].astype(F32)], 0)
    xu = ring(xu_own, "gx", -1)
    xl = ring(xl_own, "gx", 1)

    def ends(planes):
        return [
            pl.BlockSpec((planes, 8, 128), lambda i: (0, 0, 0)),
            pl.BlockSpec((planes, 8, 128), lambda i: (0, 7, 0)),
        ]

    packet = jax.ShapeDtypeStruct((XP, 8, 128), F32)
    whole = pl.BlockSpec((XP, 8, 128), lambda i: (0, 0, 0))
    yu_own, yd_own = pl.pallas_call(
        pack_rows,
        grid=(1,),
        in_specs=ends(NX) + ends(NX) + ends(7) + ends(7),
        out_specs=[whole, whole],
        out_shape=[packet, packet],
        name="pack_rows",
    )(labels, labels, right_side, right_side, xu, xu, xl, xl)
    yu = ring(yu_own, "gy", -1)
    yd = ring(yd_own, "gy", 1)

    packet = jax.ShapeDtypeStruct((3, RW, 128), F32)
    zu_own, zd_own = pl.pallas_call(
        pack_lanes,
        in_specs=[vmem()] * 6,
        out_specs=[vmem()] * 2,
        out_shape=[packet, packet],
        scratch_shapes=[pltpu.VMEM((3, RW, 128), F32)] * 2,
        name="pack_lanes",
    )(labels, right_side, xu, xl, yu, yd)
    zu = ring(zu_own, "gz", -1)
    zd = ring(zd_own, "gz", 1)

    block = jax.ShapeDtypeStruct((NX, NY, NZ), F32)
    main = pltpu.VMEM((XP, RW, 128), F32)
    slab = pltpu.VMEM((XP, 16, 128), F32)
    w0, w1, w2, mom = pl.pallas_call(
        sweeps,
        in_specs=[pl.BlockSpec(memory_space=pltpu.SMEM)] + [vmem()] * 10,
        out_specs=[vmem()] * 4,
        out_shape=[block, block, block, jax.ShapeDtypeStruct((128, 128), F32)],
        scratch_shapes=[main] * 16
        + [slab] * 16
        + [pltpu.VMEM((128, 128), F32)]
        + [pltpu.VMEM((RW, 128), F32)] * 2
        + [pltpu.VMEM((128, 128), F32)] * 2,
        compiler_params=pltpu.CompilerParams(vmem_limit_bytes=48 * 1024 * 1024),
        name="sweeps",
    )(conductivity, labels, right_side, xu, xl, yu, yd, zu_own, zd_own, zu, zd)
    mom = lax.all_to_all(mom, ALL, 0, 0, tiled=True)
    return pl.pallas_call(
        combine,
        in_specs=[vmem()] * 4,
        out_specs=vmem(),
        out_shape=block,
        name="combine",
    )(mom, w0, w1, w2)


def solution(mesh):
    spec = P("gx", "gy", "gz")
    return jax.shard_map(
        local, mesh=mesh, in_specs=(spec, P(), spec), out_specs=spec, check_vma=False
    )
```

time: 384 us -> 112 us (0.29)
  other arithmetic: 109 us -> 1.02 us
  blocking collectives: 95.2 us -> 17.5 us
  local copies, waits for them, and re-layouts: 80.6 us -> 9.55 us
  starting transfers between devices: 71.7 us -> 10.2 us
  Pallas kernels: 0 us -> 57.2 us
  between operations: 10.1 us -> 0.08 us
    psum x12 -> x0, blocking collectives: 95.2 us -> none  [by_axis(): return functools.reduce(lax.psum, axes, shard)]
    ppermute x24 -> x6, starting transfers between devices: 71.7 us -> 10.2 us  [ring(): lax.ppermute(arr, axis, [(i, (i + step) % count) for i in range(count)])]
    pallas_call x0 -> x4, Pallas kernels: none -> 57.2 us  [the longest x1 46.1 us: local(): pl.pallas_call(sweeps, in_specs=[pl.BlockSpec(memory_space=pltpu.SMEM)] +...]
    convert_element_type x8 -> x0, local copies, waits for them, and re-layouts: 28.8 us -> none  [lookup(): hit = (shifted == label + 1).astype(jnp.float32)]
    reduce_sum x4 -> x0, other arithmetic: 26.1 us -> none  [the longest x3 22.3 us: local(): jnp.sum(applied * precond)]
    concatenate x10 -> x2, other arithmetic: 23.5 us -> 0.03 us  [the longest x1 0.02 us: local(): xu_own = jnp.concatenate([right_side[:3], labels[:4].astype(F32)], 0)]
    div x3 -> x0, other arithmetic: 22.8 us -> none  [the longest x1 12.8 us: local(): precond = residual / diag]
    add x3 -> x0, other arithmetic: 22 us -> none  [the longest x1 16.9 us: lookup(): total_flux + hit[None] * conductivity[:, label][:, None, None, None]]
  transfers between devices with their start and end apart: 24 -> 6, of which waited for: 6 -> 5; matrix products, arithmetic and copies ran while one was open for 6% -> 0% of each run, Pallas kernels for 0% -> 0%
where the time goes in v1:
time: 112 us; the launch traced here: 111 us
  Pallas kernels  57.2 us (51%)
  blocking collectives  17.5 us (16%)
  waiting for transfers between devices  15.7 us (14%)
  starting transfers between devices  10.2 us (9%)
  local copies, waits for them, and re-layouts  9.55 us (9%)
    pallas_call x1, Pallas kernels, local(): pl.pallas_call(sweeps, in_specs=[pl.BlockSpec(memory_space=pltpu.SMEM)] +...  46.1 us
    all_to_all x1, blocking collectives, local(): mom = lax.all_to_all(mom, ALL, 0, 0, tiled=True)  17.5 us
    ppermute x6, waiting for transfers between devices, ring(): lax.ppermute(arr, axis, [(i, (i + step) % count) for i in range(count)])  15.7 us
    ppermute x6, starting transfers between devices, ring(): lax.ppermute(arr, axis, [(i, (i + step) % count) for i in range(count)])  10.2 us
    unnamed x30, local copies, waits for them, and re-layouts  8.59 us
    pallas_call x1, Pallas kernels, local(): pl.pallas_call(pack_lanes, in_specs=[vmem()] * 6, out_specs=[vmem()] * 2,...  5.73 us
    pallas_call x1, Pallas kernels, local(): pl.pallas_call(combine, in_specs=[vmem()] * 4, out_specs=vmem(), out_shap...  3.31 us
  transfers between devices with their start and end apart: 6, of which 5 were waited for; matrix products, arithmetic and copies ran while one was open for 0% of the time, Pallas kernels for 0%

profile of v1, /device:TPU:1, one launch (start us, length us, event | category | flops | bytes accessed | tf_op | source)
XLA Modules:
  0.0 111.3 jit_solution(5545849853101087383)
XLA Ops:
  0.0 1.0 fusion
  1.0 1.0 slice_convert_fusion
  2.0 3.4 %collective-permute-start = (f32[7,64,128]{2,1,0:T(8,128)S(1)}, f32[7,64,128]{2,1,0:T(8,128)S(1)}, u32[]{:S(2)}, u32[]{:S(2)}) collective-permute-start(f32[7,64,128]{2,1,0:T(8,128)S(1)} %pad_maximum_fusion), channel_id=1, source_target_pairs={{0,96},{32,0},{64,32},{96,64},{1,97},{33,1},{65,33},{97,65},{2,98}... | collective-permute-start | bytes 688136 | tf_op jit(solution)/shard_map/ppermute | solution.py:18
  5.4 0.1 collective-permute-start.1
  5.4 4.2 %collective-permute-done.xu0.xu7.xu = f32[7,64,128]{2,1,0:T(8,128)S(1)} collective-permute-done((f32[7,64,128]{2,1,0:T(8,128)S(1)}, f32[7,64,128]{2,1,0:T(8,128)S(1)}, u32[]{:S(2)}, u32[]{:S(2)}) %collective-permute-start) | collective-permute-done | bytes 229408 | tf_op jit(solution)/shard_map/ppermute | solution.py:18
  9.6 3.2 %collective-permute-done.1.xl0.xl7.xl = f32[7,64,128]{2,1,0:T(8,128)S(1)} collective-permute-done((f32[7,64,128]{2,1,0:T(8,128)S(1)}, f32[7,64,128]{2,1,0:T(8,128)S(1)}, u32[]{:S(2)}, u32[]{:S(2)}) %collective-permute-start.1) | collective-permute-done | bytes 229408 | tf_op jit(solution)/shard_map/ppermute | solution.py:18
  12.9 0.0 copy-done.1
  12.9 0.7 copy-done.3
  13.5 2.1 %pack_rows.1 = (f32[40,8,128]{2,1,0:T(8,128)}, f32[40,8,128]{2,1,0:T(8,128)}) custom-call(s32[32,64,128]{2,1,0:T(8,128)} %lab.3, s32[32,64,128]{2,1,0:T(8,128)} %lab.3, f32[32,64,128]{2,1,0:T(8,128)} %b.3, f32[32,64,128]{2,1,0:T(8,128)} %b.3, f32[7,64,128]{2,1,0:T(8,128)} %copy-done.1, f32[7,64,128]{2,1,0:T(8,128)} %copy-done.1, f32[7,64,128]{2,1,0:T(8,128)} %copy-done.3, ...), custom_call_target="tpu_custom_call" | custom-call | tf_op jit(solution)/shard_map/pack_rows/pallas_call | solution.py:460
  15.6 1.8 %collective-permute-start.2 = (f32[40,8,128]{2,1,0:T(8,128)}, f32[40,8,128]{2,1,0:T(8,128)S(1)}, u32[]{:S(2)}, u32[]{:S(2)}) collective-permute-start(f32[40,8,128]{2,1,0:T(8,128)} %get-tuple-element.13), channel_id=1, source_target_pairs={{0,28},{4,0},{8,4},{12,8},{16,12},{20,16},{24,20},{28,24},{1,29},{... | collective-permute-start | bytes 491528 | tf_op jit(solution)/shard_map/ppermute | solution.py:18
  17.4 1.2 %collective-permute-start.3 = (f32[40,8,128]{2,1,0:T(8,128)}, f32[40,8,128]{2,1,0:T(8,128)S(1)}, u32[]{:S(2)}, u32[]{:S(2)}) collective-permute-start(f32[40,8,128]{2,1,0:T(8,128)} %get-tuple-element.14), channel_id=1, source_target_pairs={{0,4},{4,8},{8,12},{12,16},{16,20},{20,24},{24,28},{28,0},{1,5},{5... | collective-permute-start | bytes 491528 | tf_op jit(solution)/shard_map/ppermute | solution.py:18
  18.7 3.2 %collective-permute-done.2.yu = f32[40,8,128]{2,1,0:T(8,128)S(1)} collective-permute-done((f32[40,8,128]{2,1,0:T(8,128)}, f32[40,8,128]{2,1,0:T(8,128)S(1)}, u32[]{:S(2)}, u32[]{:S(2)}) %collective-permute-start.2) | collective-permute-done | bytes 163872 | tf_op jit(solution)/shard_map/ppermute | solution.py:18
  21.8 0.0 collective-permute-done.3.yd
  21.8 0.6 copy-done.8
  22.5 0.7 copy-done.10
  23.1 5.7 %pack_lanes.1 = (f32[3,80,128]{2,1,0:T(8,128)}, f32[3,80,128]{2,1,0:T(8,128)}) custom-call(s32[32,64,128]{2,1,0:T(8,128)} %lab.3, f32[32,64,128]{2,1,0:T(8,128)} %b.3, f32[7,64,128]{2,1,0:T(8,128)} %copy-done.1, f32[7,64,128]{2,1,0:T(8,128)} %copy-done.3, f32[40,8,128]{2,1,0:T(8,128)} %copy-done.8, f32[40,8,128]{2,1,0:T(8,128)} %copy-done.10), custom_call_target="tpu_custom_call" | custom-call | tf_op jit(solution)/shard_map/pack_lanes/pallas_call | solution.py:472
  28.9 3.8 %collective-permute-start.4 = (f32[3,80,128]{2,1,0:T(8,128)}, f32[3,80,128]{2,1,0:T(8,128)S(1)}, u32[]{:S(2)}, u32[]{:S(2)}) collective-permute-start(f32[3,80,128]{2,1,0:T(8,128)} %get-tuple-element.15.zu_own), channel_id=1, source_target_pairs={{0,3},{1,0},{2,1},{3,2},{4,7},{5,4},{6,5},{7,6},{8,11},{9,8},{10,9... | collective-permute-start | bytes 368648 | tf_op jit(solution)/shard_map/ppermute | solution.py:18
  32.6 0.0 collective-permute-start.5
  32.6 2.2 %collective-permute-done.4.zu = f32[3,80,128]{2,1,0:T(8,128)S(1)} collective-permute-done((f32[3,80,128]{2,1,0:T(8,128)}, f32[3,80,128]{2,1,0:T(8,128)S(1)}, u32[]{:S(2)}, u32[]{:S(2)}) %collective-permute-start.4) | collective-permute-done | bytes 122912 | tf_op jit(solution)/shard_map/ppermute | solution.py:18
  34.8 3.0 %collective-permute-done.5.zd = f32[3,80,128]{2,1,0:T(8,128)S(1)} collective-permute-done((f32[3,80,128]{2,1,0:T(8,128)}, f32[3,80,128]{2,1,0:T(8,128)S(1)}, u32[]{:S(2)}, u32[]{:S(2)}) %collective-permute-start.5) | collective-permute-done | bytes 122912 | tf_op jit(solution)/shard_map/ppermute | solution.py:18
  37.8 0.0 copy-done.14
  37.8 0.0 copy-start.9
  37.8 0.9 copy-done.9
  38.7 0.9 copy-done.11
  39.6 0.9 copy-done.12
  40.5 0.9 copy-done.13
  41.4 46.1 %sweeps.1 = (f32[32,64,128]{2,1,0:T(8,128)S(1)}, f32[32,64,128]{2,1,0:T(8,128)S(1)}, f32[32,64,128]{2,1,0:T(8,128)S(1)}, f32[128,128]{1,0:T(8,128)S(1)}) custom-call(f32[7,8]{1,0:T(8,128)S(1)} %copy-done.14, s32[32,64,128]{2,1,0:T(8,128)S(1)} %copy-done, f32[32,64,128]{2,1,0:T(8,128)} %b.3, f32[7,64,128]{2,1,0:T(8,128)S(1)} %copy-done.2, ...), custom_call_target="tpu_custom_call" | custom-call | tf_op jit(solution)/shard_map/sweeps/pallas_call | solution.py:486
  87.6 1.0 copy-done.5
  88.6 1.0 copy-done.6
  89.5 1.0 copy-done.7
  90.5 17.5 %all_to_all.11 = f32[128,1,128]{2,1,0:T(1,128)} all-to-all(f32[128,1,128]{2,1,0:T(1,128)S(1)} %bitcast.4), channel_id=1, replica_groups=mesh['gx'=4,'gy'=8,'gz'=4] {'gx','gy','gz'}, dimensions={0} | all-to-all | bytes 131072 | tf_op jit(solution)/shard_map/all_to_all | solution.py:499
  108.0 3.3 %combine.1 = f32[32,64,128]{2,1,0:T(8,128)} custom-call(f32[128,128]{1,0:T(8,128)} %bitcast.5, f32[32,64,128]{2,1,0:T(8,128)} %copy-done.5, f32[32,64,128]{2,1,0:T(8,128)} %copy-done.6, f32[32,64,128]{2,1,0:T(8,128)} %copy-done.7), custom_call_target="tpu_custom_call" | custom-call | tf_op jit(solution)/shard_map/combine/pallas_call | solution.py:500
  (19 shorter events, 0.1 us)
Async XLA Ops:
  2.0 7.7 %collective-permute-start = (f32[7,64,128]{2,1,0:T(8,128)S(1)}, f32[7,64,128]{2,1,0:T(8,128)S(1)}, u32[]{:S(2)}, u32[]{:S(2)}) collective-permute-start(f32[7,64,128]{2,1,0:T(8,128)S(1)} %pad_maximum_fusion), channel_id=1, source_target_pairs={{0,96},{32,0},{64,32},{96,64},{1,97},{33,1},{65,33},{97,65},{2,98}... | collective-permute-start | bytes 688136 | tf_op jit(solution)/shard_map/ppermute | solution.py:18
  5.4 7.5 %collective-permute-start.1 = (f32[7,64,128]{2,1,0:T(8,128)S(1)}, f32[7,64,128]{2,1,0:T(8,128)S(1)}, u32[]{:S(2)}, u32[]{:S(2)}) collective-permute-start(f32[7,64,128]{2,1,0:T(8,128)S(1)} %pad_maximum_fusion.1), channel_id=1, source_target_pairs={{0,32},{32,64},{64,96},{96,0},{1,33},{33,65},{65,97},{97,1},{2,34}... | collective-permute-start | bytes 688136 | tf_op jit(solution)/shard_map/ppermute | solution.py:18
  9.6 3.2 %copy-start.1 = (f32[7,64,128]{2,1,0:T(8,128)}, f32[7,64,128]{2,1,0:T(8,128)S(1)}, u32[]{:S(2)}) copy-start(f32[7,64,128]{2,1,0:T(8,128)S(1)} %collective-permute-done.xu0.xu7.xu) | copy-start | bytes 688132
  12.9 0.7 copy-start.3
  15.6 6.2 %collective-permute-start.2 = (f32[40,8,128]{2,1,0:T(8,128)}, f32[40,8,128]{2,1,0:T(8,128)S(1)}, u32[]{:S(2)}, u32[]{:S(2)}) collective-permute-start(f32[40,8,128]{2,1,0:T(8,128)} %get-tuple-element.13), channel_id=1, source_target_pairs={{0,28},{4,0},{8,4},{12,8},{16,12},{20,16},{24,20},{28,24},{1,29},{... | collective-permute-start | bytes 491528 | tf_op jit(solution)/shard_map/ppermute | solution.py:18
  17.4 20.4 %copy-start = (s32[32,64,128]{2,1,0:T(8,128)S(1)}, s32[32,64,128]{2,1,0:T(8,128)}, u32[]{:S(2)}) copy-start(s32[32,64,128]{2,1,0:T(8,128)} %lab.3) | copy-start | bytes 3145732
  17.4 20.4 %copy-start.2 = (f32[7,64,128]{2,1,0:T(8,128)S(1)}, f32[7,64,128]{2,1,0:T(8,128)}, u32[]{:S(2)}) copy-start(f32[7,64,128]{2,1,0:T(8,128)} %copy-done.1) | copy-start | bytes 688132
  17.4 20.4 %copy-start.4 = (f32[7,64,128]{2,1,0:T(8,128)S(1)}, f32[7,64,128]{2,1,0:T(8,128)}, u32[]{:S(2)}) copy-start(f32[7,64,128]{2,1,0:T(8,128)} %copy-done.3) | copy-start | bytes 688132
  17.4 4.4 %collective-permute-start.3 = (f32[40,8,128]{2,1,0:T(8,128)}, f32[40,8,128]{2,1,0:T(8,128)S(1)}, u32[]{:S(2)}, u32[]{:S(2)}) collective-permute-start(f32[40,8,128]{2,1,0:T(8,128)} %get-tuple-element.14), channel_id=1, source_target_pairs={{0,4},{4,8},{8,12},{12,16},{16,20},{20,24},{24,28},{28,0},{1,5},{5... | collective-permute-start | bytes 491528 | tf_op jit(solution)/shard_map/ppermute | solution.py:18
  21.8 0.7 copy-start.8
  22.5 0.7 copy-start.10
  23.1 14.7 %copy-start.14 = (f32[7,8]{1,0:T(8,128)S(1)}, f32[7,8]{1,0:T(8,128)}, u32[]{:S(2)}) copy-start(f32[7,8]{1,0:T(8,128)} %cond.1) | copy-start | bytes 676
  28.9 5.9 %collective-permute-start.4 = (f32[3,80,128]{2,1,0:T(8,128)}, f32[3,80,128]{2,1,0:T(8,128)S(1)}, u32[]{:S(2)}, u32[]{:S(2)}) collective-permute-start(f32[3,80,128]{2,1,0:T(8,128)} %get-tuple-element.15.zu_own), channel_id=1, source_target_pairs={{0,3},{1,0},{2,1},{3,2},{4,7},{5,4},{6,5},{7,6},{8,11},{9,8},{10,9... | collective-permute-start | bytes 368648 | tf_op jit(solution)/shard_map/ppermute | solution.py:18
  32.6 5.2 %collective-permute-start.5 = (f32[3,80,128]{2,1,0:T(8,128)}, f32[3,80,128]{2,1,0:T(8,128)S(1)}, u32[]{:S(2)}, u32[]{:S(2)}) collective-permute-start(f32[3,80,128]{2,1,0:T(8,128)} %get-tuple-element.16.zd_own), channel_id=1, source_target_pairs={{0,1},{1,2},{2,3},{3,0},{4,5},{5,6},{6,7},{7,4},{8,9},{9,10},{10,1... | collective-permute-start | bytes 368648 | tf_op jit(solution)/shard_map/ppermute | solution.py:18
  37.8 0.9 copy-start.9
  38.7 0.9 copy-start.11
  39.6 0.9 copy-start.12
  40.5 0.9 copy-start.13
  87.5 1.0 copy-start.5
  88.6 1.0 copy-start.6
  89.5 1.0 copy-start.7

commit v2 on v1

v2 whole, which is shorter than its diff:
```python
import jax
import jax.numpy as jnp
from jax import lax
from jax.experimental import pallas as pl
from jax.experimental.pallas import tpu as pltpu
from jax.sharding import PartitionSpec as P

LABELS = 8
ALL = ("gx", "gy", "gz")
NX, NY, NZ = 32, 64, 128
XP, RW = NX + 8, NY + 24
OWN = slice(8, 8 + NY)
F32 = jnp.float32


def ring(arr, axis, step):
    count = lax.axis_size(axis)
    return lax.ppermute(arr, axis, [(i, (i + step) % count) for i in range(count)])


def iota(shape, dim):
    return lax.broadcasted_iota(jnp.int32, shape, dim)


def pack_rows(lab, b, xu, xl, up, down):
    low = iota((8, 128), 0) < 4
    head, tail = pl.ds(0, 8), pl.ds(NY - 8, 8)

    def put(xp, lab_first, lab_last, b_first, b_last):
        up[xp] = jnp.where(low, b_first, pltpu.roll(lab_first, 4, 0))
        down[xp] = jnp.where(low, pltpu.roll(lab_last, 4, 0), b_last)

    for x in range(NX):
        put(x + 4, lab[x, head].astype(F32), lab[x, tail].astype(F32), b[x, head], b[x, tail])
    zero = jnp.zeros((8, 128), F32)
    for k in range(4):
        bk = (xl[k - 1, head], xl[k - 1, tail]) if k else (zero, zero)
        put(k, xl[3 + k, head], xl[3 + k, tail], *bk)
        bk = (xu[k, head], xu[k, tail]) if k < 3 else (zero, zero)
        put(36 + k, xu[3 + k, head], xu[3 + k, tail], *bk)


def rows_lab(yu, yd, xp):
    low = iota((8, 128), 0) < 4
    return pltpu.roll(jnp.where(low, yd[xp], yu[xp]), 4, 0)


def rows_b(yu, yd, xp):
    low = iota((8, 128), 0) < 4
    return jnp.where(low, yu[xp], yd[xp])


def pack_lanes(lab, b, xu, xl, yu, yd, up, down):
    lane = iota((8, 128), 1)
    first = lane % 8 < 4
    zero = jnp.zeros((8, 128), F32)

    def pack(at, lab_of, b_of):
        for g in range(3):
            acc_lab, acc_b = zero, zero
            for k in range(16 if g < 2 else 8):
                hit = lane // 8 == k
                shift = (8 * k + 4) % 128
                turn = lambda t: pltpu.roll(t, shift, 1) if shift else t
                acc_lab = jnp.where(hit, turn(lab_of(16 * g + k)), acc_lab)
                acc_b = jnp.where(hit, turn(b_of(16 * g + k)), acc_b)
            for off in at:
                down[g, off] = jnp.where(first, acc_lab, pltpu.roll(acc_b, 4, 1))
                up[g, off] = jnp.where(first, pltpu.roll(acc_b, 124, 1), acc_lab)

    def rows(rg, carry):
        at = pl.ds(pl.multiple_of(8 * rg, 8), 8)

        def lab_of(xp):
            if xp < 4:
                return xl[3 + xp, at]
            if xp >= 36:
                return xu[xp - 33, at]
            return lab[xp - 4, at].astype(F32)

        def b_of(xp):
            if xp < 4:
                return xl[xp - 1, at] if xp else zero
            if xp >= 36:
                return xu[xp - 36, at] if xp < 39 else zero
            return b[xp - 4, at]

        pack((pl.ds(pl.multiple_of(8 * rg + 8, 8), 8),), lab_of, b_of)
        return carry

    lax.fori_loop(0, 8, rows, 0)
    pack(
        (pl.ds(0, 8), pl.ds(72, 8)),
        lambda xp: rows_lab(yu, yd, xp),
        lambda xp: rows_b(yu, yd, xp),
    )


def group(g):
    return pl.ds(8 + 8 * g, 8)


def sweeps(
    cond, lab, b, xu, xl, yu, yd, zu_own, zd_own, zu, zd,
    w0o, w1o, w2o, mom,
    f0, f1, f2, f2l, s3, s4, s5, inv, mid, v0, v1, v2, dz, ac, u3, u4, u5,
    q0, q1, q2, q3, q4, q5, qinv, qmid, qv0, qv1, qv2, qdz, qac, p3, p4, p5,
    wide, patch_v, patch_q, row_v, row_q,
):
    s0, s1, s2 = u3, u4, dz
    sig = (s0, s1, s2, s3, s4, s5)
    qsig = (q0, q1, q2, q3, q4, q5)
    gx, gy, gz = (lax.axis_index(a) for a in ALL)
    not_first_x = (gx > 0).astype(F32)
    not_last_x = (gx < lax.axis_size("gx") - 1).astype(F32)
    not_first_y = (gy > 0).astype(F32)
    not_last_y = (gy < lax.axis_size("gy") - 1).astype(F32)
    not_first_z = (gz > 0).astype(F32)
    not_last_z = (gz < lax.axis_size("gz") - 1).astype(F32)

    sub8 = iota((8, 128), 0)
    ln = iota((8, 128), 1)
    tables = []
    for c in range(7):
        t = jnp.zeros((8, 128), F32)
        scale = 0.5 if c < 3 else (0.25 if c < 6 else 1.0)
        for l in range(LABELS):
            t = jnp.where(sub8 == l, cond[c, l] * scale, t)
        tables.append(t)

    mass = sum(cond[6, l] for l in range(LABELS))
    faces = sum(cond[c, l] for c in range(3) for l in range(LABELS)) * 2.0
    theta = jnp.full((1, 128), faces, F32) / jnp.full((1, 128), faces + mass, F32)

    def look(c, idx):
        return jnp.take_along_axis(tables[c], idx, axis=0, mode="promise_in_bounds")

    def entries(idx, on):
        vals = [look(c, idx) for c in range(7)]
        if on is not None:
            vals = [v * on for v in vals]
        centre = vals[6] + 2.0 * (vals[0] + vals[1] + vals[2])
        return vals[:6], centre

    row_on = jnp.where(sub8 < 4, not_last_y, not_first_y)

    def put(ref, xp, g, value):
        ref[xp, group(g)] = value
        if g == 8:
            ref[xp, pl.ds(0, 8)] = value
        if g == 0:
            ref[xp, pl.ds(80, 8)] = value

    def table_plane(xp, labels_of, b_of, on):
        for g in range(9):
            if g < 8:
                vals, centre = entries(labels_of(g), on)
                v0[xp, group(g)] = b_of(g)
            else:
                vals, centre = entries(
                    rows_lab(yu, yd, xp).astype(jnp.int32),
                    row_on if on is None else row_on * on,
                )
                v0[xp, group(g)] = rows_b(yu, yd, xp)
            for c in range(6):
                if c == 1:
                    put(s1, xp, g, vals[1])
                else:
                    sig[c][xp, group(g)] = vals[c]
            inv[xp, group(g)] = centre

    def own_plane(x, carry):
        table_plane(
            x + 4, lambda g: lab[x, pl.ds(8 * g, 8)], lambda g: b[x, pl.ds(8 * g, 8)], None
        )
        return carry

    lax.fori_loop(0, NX, own_plane, 0)

    def low_plane(k, carry):
        table_plane(
            k,
            lambda g: xl[3 + k, pl.ds(8 * g, 8)].astype(jnp.int32),
            lambda g: xl[jnp.maximum(k - 1, 0), pl.ds(8 * g, 8)],
            not_first_x,
        )
        return carry

    def high_plane(k, carry):
        table_plane(
            36 + k,
            lambda g: xu[3 + k, pl.ds(8 * g, 8)].astype(jnp.int32),
            lambda g: xu[jnp.minimum(k, 2), pl.ds(8 * g, 8)],
            not_last_x,
        )
        return carry

    lax.fori_loop(0, 4, low_plane, 0)
    lax.fori_loop(0, 4, high_plane, 0)

    first = iota((80, 128), 1) % 8 < 4
    wide[...] = jnp.zeros((128, 128), F32)
    lane_on = jnp.where(ln < 8, not_first_y, jnp.where(ln >= 72, not_last_y, 1.0))
    low_on = jnp.where(sub8 < 4, not_first_z, 1.0) * lane_on
    high_on = jnp.where(sub8 < 4, 1.0, not_last_z) * lane_on

    def turned(arr):
        wide[pl.ds(0, 80)] = arr
        return wide[...].T

    for g in range(3):
        count = 16 if g < 2 else 8
        parts = (
            (0, low_on, turned(jnp.where(first, zd[g], zu_own[g])),
             turned(jnp.where(first, zu_own[g], zd[g]))),
            (8, high_on, turned(jnp.where(first, zd_own[g], zu[g])),
             turned(jnp.where(first, zu[g], zd_own[g]))),
        )
        for off, on, labs, bs in parts:
            for k in range(count):
                xp = 16 * g + k
                here = on
                if xp < 4:
                    here = on * not_first_x
                if xp >= 36:
                    here = on * not_last_x
                idx = jnp.clip(labs[8 * k : 8 * k + 8].astype(jnp.int32), 0, LABELS - 1)
                vals, centre = entries(idx, here)
                for c in range(6):
                    qsig[c][xp + 1, pl.ds(off, 8)] = vals[c]
                qinv[xp + 1, pl.ds(off, 8)] = centre
                qv0[xp + 1, pl.ds(off, 8)] = pltpu.roll(bs[8 * k : 8 * k + 8], 4, 0)

    def set_rows(ref, xp, values):
        for k in range(values.shape[0]):
            ref[pl.ds(2 * (xp + k) + 1, 1)] = values[k, 3:4]
            ref[pl.ds(2 * (xp + k), 1)] = values[k, 12:13]

    def set_patch(patch, rows):
        t = rows[...].T
        patch[...] = t[:80]
        patch[pl.ds(72, 8)] = jnp.where(sub8 < 4, t[72:80], t[:8])

    def sides(value, patch, xp, g):
        p = pltpu.roll(patch[group(g)], 127 - 2 * xp, 1)
        left = jnp.where(ln == 0, p, pltpu.roll(value, 1, 1))
        right = jnp.where(ln == 127, p, pltpu.roll(value, 127, 1))
        return left, right

    QB = 8

    def q_loop(body):
        lax.fori_loop(0, XP // QB, lambda i, c: body(QB * i) or c, 0)

    def lanes(x, step):
        return pltpu.roll(x, step % 128, 2)

    def subs(x, step):
        return pltpu.roll(x, step % 16, 1)

    row_v[...] = jnp.zeros((128, 128), F32)
    row_q[...] = jnp.zeros((128, 128), F32)

    def reciprocal(centre, total):
        return jnp.where(centre > 0, 1.0 / jnp.where(centre > 0, total, 1.0), 0.0)

    def q_diag(xp):
        at = pl.ds(xp + 1, QB)
        c = qinv[at]
        b1 = q1[at]
        b2 = q2[at]
        total = c + (q0[pl.ds(xp + 2, QB)] + q0[pl.ds(xp, QB)])
        total = total + (lanes(b1, 1) + lanes(b1, -1))
        total = total + (subs(b2, 1) + subs(b2, -1))
        r = reciprocal(c, total)
        qinv[at] = r
        qmid[at] = theta * total
        w = qv0[at] * r
        qv0[at] = w
        set_rows(row_q, xp, b2)
        set_rows(row_v, xp, w)

    q_loop(q_diag)
    set_patch(patch_q, row_q)
    set_patch(patch_v, row_v)

    def add(acc, value):
        total, lost = acc
        value = value - lost
        new = total + value
        return new, (new - total) - value

    def tree(values):
        while len(values) > 1:
            values = [sum(values[i : i + 2]) for i in range(0, len(values), 2)]
        return values[0]

    zero8 = jnp.zeros((8, 128), F32)
    none = (zero8, zero8)

    def blocks(body, extra, sums):
        if extra:
            lax.fori_loop(
                0, 2, lambda i, c: body(4 - extra + (32 + extra) * i, extra, None) or c, 0
            )
        return lax.fori_loop(0, NX // 4, lambda i, acc: body(4 * i + 4, 4, acc), sums)

    def diag_block(xp0, n, acc):
        for g in range(9):
            at, nxt, prv = group(g), pl.ds(9 + 8 * g, 8), pl.ds(7 + 8 * g, 8)
            faces_x = [s0[xp0 - 1 + i, at] for i in range(n + 2)]
            parts = []
            for i in range(n):
                xp = xp0 + i
                c = inv[xp, at]
                a1, a1n = s1[xp, at], s1[xp, nxt]
                a2 = s2[xp, at]
                left, right = sides(a2, patch_q, xp, g)
                total = c + (faces_x[i + 2] + faces_x[i])
                total = total + (a1n + s1[xp, prv])
                total = total + (left + right)
                r = reciprocal(c, total)
                rhs = v0[xp, at]
                w = rhs * r
                inv[xp, at] = r
                mid[xp, at] = theta * total
                put(v0, xp, g, w)
                f0[xp, at] = faces_x[i + 1] + faces_x[i + 2]
                put(f1, xp, g, a1 + a1n)
                f2[xp, at] = a2 + right
                f2l[xp, at] = a2 + left
                parts.append(rhs * w)
            if acc is not None and g < 8:
                acc = add(acc, tree(parts))
        return acc

    nu0 = blocks(diag_block, 3, none)

    def apply(v, w, qv, qw, extra, last):
        def q_first(xp):
            at = pl.ds(xp + 1, QB)
            x = qv[at]
            left = subs(x, 1)
            right = subs(x, -1)
            qdz[at] = right - left
            qac[at] = q2[at] * (left + right)
            p3[at] = q3[at] * x
            p4[at] = q4[at] * x
            p5[at] = q5[at] * x

        q_loop(q_first)

        def q_second(xp):
            at, nx, pr = pl.ds(xp + 1, QB), pl.ds(xp + 2, QB), pl.ds(xp, QB)

            def dy(x):
                return lanes(x, -1) - lanes(x, 1)

            q = (p4[nx] - p4[pr]) + dy(p5[at])
            set_rows(row_q, xp, q)
            if not last:
                x = qv[at]
                u2 = q2[at] * x
                b0 = q0[at]
                xa, xb = qv[nx], qv[pr]
                r = (qac[at] - qmid[at] * x) + (b0 + q0[nx]) * xa + (b0 + q0[pr]) * xb
                u1 = q1[at] * x
                t = p3[nx] - p3[pr]
                r = r + q1[at] * (lanes(x, -1) + lanes(x, 1))
                r = r + lanes(u1 + t, -1) + lanes(u1 - t, 1)
                r = r + q3[at] * dy(xa - xb)
                r = r + q4[at] * (qdz[nx] - qdz[pr])
                r = r + q5[at] * dy(qdz[at])
                r = r + subs(u2 + q, -1) + subs(u2 - q, 1)
                out = r * qinv[at]
                qw[at] = out
                set_rows(row_v, xp, out)

        q_loop(q_second)
        set_patch(patch_q, row_q)

        def first_block(xp0, n, acc):
            for g in range(9):
                at = group(g)
                for xp in [xp0 + i for i in range(n)]:
                    x = v[xp, at]
                    left, right = sides(x, patch_v, xp, g)
                    put(dz, xp, g, right - left)
                    ac[xp, at] = f2[xp, at] * right + f2l[xp, at] * left
                    put(u3, xp, g, s3[xp, at] * x)
                    u4[xp, at] = s4[xp, at] * x
                    put(u5, xp, g, s5[xp, at] * x)
            return acc

        blocks(first_block, extra + 1, 0)

        def second_block(xp0, n, acc):
            def start(g):
                at, nxt, prv = group(g), pl.ds(9 + 8 * g, 8), pl.ds(7 + 8 * g, 8)
                a4 = [u4[xp0 - 1 + i, at] for i in range(n + 2)]
                out = []
                for i in range(n):
                    xp = xp0 + i
                    q = (a4[i + 2] - a4[i]) + (u5[xp, nxt] - u5[xp, prv])
                    left, right = sides(q, patch_q, xp, g)
                    out.append(right - left)
                return out

            def finish(g, qs, acc):
                at, nxt, prv = group(g), pl.ds(9 + 8 * g, 8), pl.ds(7 + 8 * g, 8)
                vh = [v[xp0 - 1 + i, at] for i in range(n + 2)]
                vn = [v[xp0 - 1 + i, nxt] for i in range(n + 2)]
                vp = [v[xp0 - 1 + i, prv] for i in range(n + 2)]
                un = [u3[xp0 - 1 + i, nxt] for i in range(n + 2)]
                up = [u3[xp0 - 1 + i, prv] for i in range(n + 2)]
                zh = [dz[xp0 - 1 + i, at] for i in range(n + 2)]
                fx = [f0[xp0 - 1 + i, at] for i in range(n + 1)]
                dots, norms = [], []
                for i in range(n):
                    xp = xp0 + i
                    x = vh[i + 1]
                    r = ac[xp, at] - mid[xp, at] * x
                    r = r + (fx[i + 1] * vh[i + 2] + fx[i] * vh[i])
                    r = r + (f1[xp, at] * vn[i + 1] + f1[xp, prv] * vp[i + 1])
                    r = r + s3[xp, at] * ((vn[i + 2] - vn[i]) - (vp[i + 2] - vp[i]))
                    r = r + ((un[i + 2] - un[i]) - (up[i + 2] - up[i]))
                    r = r + s4[xp, at] * (zh[i + 2] - zh[i])
                    r = r + s5[xp, at] * (dz[xp, nxt] - dz[xp, prv])
                    r = r + qs[i]
                    dots.append(x * r)
                    if not last:
                        out = r * inv[xp, at]
                        put(w, xp, g, out)
                        norms.append(out * r)
                if acc is None or g == 8:
                    return acc
                if last:
                    return add(acc[0], tree(dots)), acc[1]
                return add(acc[0], tree(dots)), add(acc[1], tree(norms))

            count = 8 if last else 9
            ahead = 2
            pending = [start(g) for g in range(ahead)]
            for g in range(count):
                if g + ahead < count:
                    pending.append(start(g + ahead))
                acc = finish(g, pending.pop(0), acc)
            return acc

        out = blocks(second_block, extra, (none, none))
        if not last:
            set_patch(patch_v, row_v)
        return out

    nu1, nu2 = apply(v0, v1, qv0, qv1, 2, False)
    nu3, nu4 = apply(v1, v2, qv1, qv2, 1, False)
    nu5, _ = apply(v2, None, qv2, None, 0, True)

    def store(x, carry):
        w0o[x] = v0[x + 4, OWN]
        w1o[x] = v1[x + 4, OWN]
        w2o[x] = v2[x + 4, OWN]
        return carry

    lax.fori_loop(0, NX, store, 0)
    line = jnp.zeros((1, 128), F32)
    at = iota((1, 128), 1)
    line = jnp.where(at == 6, theta, line)
    for k, (nu, _) in enumerate((nu0, nu1, nu2, nu3, nu4, nu5)):
        part = jnp.sum(jnp.sum(nu, axis=0, keepdims=True), axis=1, keepdims=True)
        line = jnp.where(at == k, part, line)
    mom[...] = jnp.broadcast_to(line, mom.shape)


def combine(mom, w0, w1, w2, out):
    total = jnp.sum(mom[...], axis=0, keepdims=True)
    at = iota((1, 128), 1)
    m = [jnp.sum(jnp.where(at == k, total, 0.0), axis=1, keepdims=True) for k in range(7)]
    rest = 1.0 - m[6] * (1.0 / mom.shape[0])
    a = [rest * m[k] - m[k + 1] for k in range(5)]
    tiny = 1e-7

    def ratio(p, q, limit):
        ok = q > limit
        return jnp.where(ok, p / jnp.where(ok, q, 1.0), 0.0)

    l10 = a[1] / a[0]
    l20 = a[2] / a[0]
    d1 = a[2] - l10 * a[1]
    e12 = a[3] - l10 * a[2]
    g1 = m[1] - l10 * m[0]
    l21 = ratio(e12, d1, tiny * a[2])
    d2 = a[4] - l20 * a[2] - l21 * e12
    g2 = m[2] - l20 * m[0] - l21 * g1
    c2 = ratio(g2, d2, tiny * a[4])
    c1 = ratio(g1, d1, tiny * a[2]) - l21 * c2
    c0 = (m[0] - a[1] * c1 - a[2] * c2) / a[0]

    def plane(x, carry):
        out[x] = c0 * w0[x] + c1 * w1[x] + c2 * w2[x]
        return carry

    lax.fori_loop(0, NX, plane, 0)


def vmem():
    return pl.BlockSpec(memory_space=pltpu.VMEM)


def local(labels, conductivity, right_side):
    xu_own = jnp.concatenate([right_side[:3], labels[:4].astype(F32)], 0)
    xl_own = jnp.concatenate([right_side[NX - 3 :], labels[NX - 4 :].astype(F32)], 0)
    xu = ring(xu_own, "gx", -1)
    xl = ring(xl_own, "gx", 1)

    packet = jax.ShapeDtypeStruct((XP, 8, 128), F32)
    yu_own, yd_own = call(pack_rows, 4, [packet] * 2, 4)(labels, right_side, xu, xl)
    yu = ring(yu_own, "gy", -1)
    yd = ring(yd_own, "gy", 1)

    packet = jax.ShapeDtypeStruct((3, 80, 128), F32)
    zu_own, zd_own = call(pack_lanes, 6, [packet] * 2, 6)(labels, right_side, xu, xl, yu, yd)
    zu = ring(zu_own, "gz", -1)
    zd = ring(zd_own, "gz", 1)

    block = jax.ShapeDtypeStruct((NX, NY, NZ), F32)
    square = pltpu.VMEM((128, 128), F32)
    patch = pltpu.VMEM((80, 128), F32)
    w0, w1, w2, mom = pl.pallas_call(
        sweeps,
        in_specs=[pl.BlockSpec(memory_space=pltpu.SMEM)] + [vmem()] * 10,
        out_specs=[vmem()] * 4,
        out_shape=[block, block, block, jax.ShapeDtypeStruct((128, 128), F32)],
        scratch_shapes=[pltpu.VMEM((XP, RW, 128), F32)] * 17
        + [pltpu.VMEM((XP + 2, 16, 128), F32)] * 16
        + [square, patch, patch, square, square],
        compiler_params=pltpu.CompilerParams(vmem_limit_bytes=48 * 2**20),
        name="sweeps",
    )(conductivity, labels, right_side, xu, xl, yu, yd, zu_own, zd_own, zu, zd)
    mom = lax.all_to_all(mom, ALL, 0, 0, tiled=True)
    return call(combine, 4, block, 6)(mom, w0, w1, w2)


def call(kernel, inputs, shapes, mib):
    many = isinstance(shapes, list)
    return pl.pallas_call(
        kernel,
        in_specs=[vmem()] * inputs,
        out_specs=[vmem()] * len(shapes) if many else vmem(),
        out_shape=shapes,
        compiler_params=pltpu.CompilerParams(vmem_limit_bytes=mib * 2**20),
        name=kernel.__name__,
    )


def solution(mesh):
    spec = P("gx", "gy", "gz")
    return jax.shard_map(
        local, mesh=mesh, in_specs=(spec, P(), spec), out_specs=spec, check_vma=False
    )
```

time: 112 us -> 70.2 us (0.63)
  Pallas kernels: 57.2 us -> 23.9 us
  local copies, waits for them, and re-layouts: 9.55 us -> 2.28 us
    pallas_call x1, Pallas kernels: 46.1 us -> 20.7 us  [local(): pl.pallas_call(sweeps, in_specs=[pl.BlockSpec(memory_space=pltpu.SMEM)] +...]
    pallas_call x3, Pallas kernels: 11.1 us -> 3.16 us  [the longest x1 1.68 us: local(): call(pack_lanes, 6, [packet] * 2, 6)(labels, right_side, xu, xl, yu, yd)]
    unnamed x30 -> x8, local copies, waits for them, and re-layouts: 8.59 us -> 1.24 us
where the time goes in v2:
time: 70.2 us; the launch traced here: 70 us
  Pallas kernels  23.9 us (34%)
  blocking collectives  17.1 us (24%)
  waiting for transfers between devices  15.3 us (22%)
  starting transfers between devices  10.3 us (15%)
  local copies, waits for them, and re-layouts  2.28 us (3%)
  other arithmetic  1.02 us (1%)
    pallas_call x1, Pallas kernels, local(): pl.pallas_call(sweeps, in_specs=[pl.BlockSpec(memory_space=pltpu.SMEM)] +...  20.7 us
    all_to_all x1, blocking collectives, local(): mom = lax.all_to_all(mom, ALL, 0, 0, tiled=True)  17.1 us
    ppermute x6, waiting for transfers between devices, ring(): lax.ppermute(arr, axis, [(i, (i + step) % count) for i in range(count)])  15.3 us
    ppermute x6, starting transfers between devices, ring(): lax.ppermute(arr, axis, [(i, (i + step) % count) for i in range(count)])  10.3 us
    pallas_call x1, Pallas kernels, local(): call(pack_lanes, 6, [packet] * 2, 6)(labels, right_side, xu, xl, yu, yd)  1.68 us
    pallas_call x1, Pallas kernels, local(): return call(combine, 4, block, 6)(mom, w0, w1, w2)  1.44 us
  transfers between devices with their start and end apart: 6, of which 5 were waited for; matrix products, arithmetic and copies ran while one was open for 0% of the time, Pallas kernels for 0%

profile of v2, /device:TPU:1, one launch (start us, length us, event | category | flops | bytes accessed | tf_op | source)
XLA Modules:
  0.0 70.0 jit_solution(2460242316561424538)
XLA Ops:
  0.0 0.0 copy-start
  0.0 1.0 %fusion = (f32[3,64,128]{2,1,0:T(8,128)S(1)}, f32[3,64,128]{2,1,0:T(8,128)S(1)}) fusion(f32[32,64,128]{2,1,0:T(8,128)} %b.5), kind=kLoop, calls=%fused_computation.4 | loop fusion | bytes 393216 | tf_op jit(solution)/shard_map/slice | solution.py:512
  1.0 1.0 %slice_convert_fusion = (f32[4,64,128]{2,1,0:T(8,128)S(1)}, f32[4,64,128]{2,1,0:T(8,128)S(1)}) fusion(s32[32,64,128]{2,1,0:T(8,128)} %lab.5), kind=kLoop, calls=%fused_computation.2 | loop fusion | flops 65536 | bytes 524288 | tf_op jit(solution)/shard_map/convert_element_type | solution.py:512
  2.1 3.4 %collective-permute-start = (f32[7,64,128]{2,1,0:T(8,128)S(1)}, f32[7,64,128]{2,1,0:T(8,128)S(1)}, u32[]{:S(2)}, u32[]{:S(2)}) collective-permute-start(f32[7,64,128]{2,1,0:T(8,128)S(1)} %pad_maximum_fusion), channel_id=1, source_target_pairs={{0,96},{32,0},{64,32},{96,64},{1,97},{33,1},{65,33},{97,65},{2,98}... | collective-permute-start | bytes 688136 | tf_op jit(solution)/shard_map/ppermute | solution.py:18
  5.5 0.1 collective-permute-start.1
  5.5 4.2 %collective-permute-done.xu = f32[7,64,128]{2,1,0:T(8,128)S(1)} collective-permute-done((f32[7,64,128]{2,1,0:T(8,128)S(1)}, f32[7,64,128]{2,1,0:T(8,128)S(1)}, u32[]{:S(2)}, u32[]{:S(2)}) %collective-permute-start) | collective-permute-done | bytes 229408 | tf_op jit(solution)/shard_map/ppermute | solution.py:18
  9.7 3.2 %collective-permute-done.1.xl = f32[7,64,128]{2,1,0:T(8,128)S(1)} collective-permute-done((f32[7,64,128]{2,1,0:T(8,128)S(1)}, f32[7,64,128]{2,1,0:T(8,128)S(1)}, u32[]{:S(2)}, u32[]{:S(2)}) %collective-permute-start.1) | collective-permute-done | bytes 229408 | tf_op jit(solution)/shard_map/ppermute | solution.py:18
  12.9 0.0 copy-done
  12.9 0.0 copy-start.1
  12.9 1.2 %copy-done.1 = f32[32,64,128]{2,1,0:T(8,128)S(1)} copy-done((f32[32,64,128]{2,1,0:T(8,128)S(1)}, f32[32,64,128]{2,1,0:T(8,128)}, u32[]{:S(2)}) %copy-start.1) | copy-done | bytes 1048600
  14.2 0.0 copy-start.2
  14.2 1.8 %collective-permute-start.2 = (f32[40,8,128]{2,1,0:T(8,128)S(1)}, f32[40,8,128]{2,1,0:T(8,128)S(1)}, u32[]{:S(2)}, u32[]{:S(2)}) collective-permute-start(f32[40,8,128]{2,1,0:T(8,128)S(1)} %get-tuple-element.13), channel_id=1, source_target_pairs={{0,28},{4,0},{8,4},{12,8},{16,12},{20,16},{24,20},{28,24},{1,29},{... | collective-permute-start | bytes 491528 | tf_op jit(solution)/shard_map/ppermute | solution.py:18
  16.0 1.2 %collective-permute-start.3 = (f32[40,8,128]{2,1,0:T(8,128)S(1)}, f32[40,8,128]{2,1,0:T(8,128)S(1)}, u32[]{:S(2)}, u32[]{:S(2)}) collective-permute-start(f32[40,8,128]{2,1,0:T(8,128)S(1)} %get-tuple-element.14), channel_id=1, source_target_pairs={{0,4},{4,8},{8,12},{12,16},{16,20},{20,24},{24,28},{28,0},{1,5},{5... | collective-permute-start | bytes 491528 | tf_op jit(solution)/shard_map/ppermute | solution.py:18
  17.3 3.0 %collective-permute-done.2.yu = f32[40,8,128]{2,1,0:T(8,128)S(1)} collective-permute-done((f32[40,8,128]{2,1,0:T(8,128)S(1)}, f32[40,8,128]{2,1,0:T(8,128)S(1)}, u32[]{:S(2)}, u32[]{:S(2)}) %collective-permute-start.2) | collective-permute-done | bytes 163872 | tf_op jit(solution)/shard_map/ppermute | solution.py:18
  20.2 0.0 collective-permute-done.3.yd
  20.2 0.0 copy-done.2
  20.2 0.0 copy-start.3
  20.2 1.7 %pack_lanes.1 = (f32[3,80,128]{2,1,0:T(8,128)S(1)}, f32[3,80,128]{2,1,0:T(8,128)S(1)}) custom-call(s32[32,64,128]{2,1,0:T(8,128)S(1)} %copy-done, f32[32,64,128]{2,1,0:T(8,128)S(1)} %copy-done.2, f32[7,64,128]{2,1,0:T(8,128)S(1)} %collective-permute-done.xu, f32[7,64,128]{2,1,0:T(8,128)S(1)} %collective-permute-done.1.xl, ...), custom_call_target="tpu_custom_call" | custom-call | tf_op jit(solution)/shard_map/pack_lanes/pallas_call | solution.py:522
  21.9 3.8 %collective-permute-start.4 = (f32[3,80,128]{2,1,0:T(8,128)S(1)}, f32[3,80,128]{2,1,0:T(8,128)S(1)}, u32[]{:S(2)}, u32[]{:S(2)}) collective-permute-start(f32[3,80,128]{2,1,0:T(8,128)S(1)} %get-tuple-element.15.zu_own), channel_id=1, source_target_pairs={{0,3},{1,0},{2,1},{3,2},{4,7},{5,4},{6,5},{7,6},{8,11},{9,8},{10,9... | collective-permute-start | bytes 368648 | tf_op jit(solution)/shard_map/ppermute | solution.py:18
  25.7 0.0 collective-permute-start.5
  25.7 1.9 %collective-permute-done.4.zu = f32[3,80,128]{2,1,0:T(8,128)S(1)} collective-permute-done((f32[3,80,128]{2,1,0:T(8,128)S(1)}, f32[3,80,128]{2,1,0:T(8,128)S(1)}, u32[]{:S(2)}, u32[]{:S(2)}) %collective-permute-start.4) | collective-permute-done | bytes 122912 | tf_op jit(solution)/shard_map/ppermute | solution.py:18
  27.6 3.1 %collective-permute-done.5.zd = f32[3,80,128]{2,1,0:T(8,128)S(1)} collective-permute-done((f32[3,80,128]{2,1,0:T(8,128)S(1)}, f32[3,80,128]{2,1,0:T(8,128)S(1)}, u32[]{:S(2)}, u32[]{:S(2)}) %collective-permute-start.5) | collective-permute-done | bytes 122912 | tf_op jit(solution)/shard_map/ppermute | solution.py:18
  30.7 0.0 copy-done.3
  30.7 20.7 %sweeps.1 = (f32[32,64,128]{2,1,0:T(8,128)S(1)}, f32[32,64,128]{2,1,0:T(8,128)S(1)}, f32[32,64,128]{2,1,0:T(8,128)S(1)}, f32[128,128]{1,0:T(8,128)S(1)}) custom-call(f32[7,8]{1,0:T(8,128)S(1)} %copy-done.3, s32[32,64,128]{2,1,0:T(8,128)S(1)} %copy-done, f32[32,64,128]{2,1,0:T(8,128)} %b.5, f32[7,64,128]{2,1,0:T(8,128)S(1)} %collective-permute-done.xu, ...), custom_call_target="tpu_custom_call" | custom-call | tf_op jit(solution)/shard_map/sweeps/pallas_call | solution.py:529
  51.4 17.1 %all_to_all.11 = f32[128,1,128]{2,1,0:T(1,128)S(1)} all-to-all(f32[128,1,128]{2,1,0:T(1,128)S(1)} %bitcast.5), channel_id=1, replica_groups=mesh['gx'=4,'gy'=8,'gz'=4] {'gx','gy','gz'}, dimensions={0} | all-to-all | bytes 131072 | tf_op jit(solution)/shard_map/all_to_all | solution.py:540
  68.5 1.4 %combine.1 = f32[32,64,128]{2,1,0:T(8,128)} custom-call(f32[128,128]{1,0:T(8,128)S(1)} %bitcast.4, f32[32,64,128]{2,1,0:T(8,128)S(1)} %get-tuple-element.18.w0, f32[32,64,128]{2,1,0:T(8,128)S(1)} %get-tuple-element.19.w1, f32[32,64,128]{2,1,0:T(8,128)S(1)} %get-tuple-element.20.w2), custom_call_target="tpu_custom_call" | custom-call | tf_op jit(solution)/shard_map/combine/pallas_call | solution.py:541
  (3 shorter events, 0.1 us)
Async XLA Ops:
  0.0 12.9 %copy-start = (s32[32,64,128]{2,1,0:T(8,128)S(1)}, s32[32,64,128]{2,1,0:T(8,128)}, u32[]{:S(2)}) copy-start(s32[32,64,128]{2,1,0:T(8,128)} %lab.5) | copy-start | bytes 3145732
  2.1 7.7 %collective-permute-start = (f32[7,64,128]{2,1,0:T(8,128)S(1)}, f32[7,64,128]{2,1,0:T(8,128)S(1)}, u32[]{:S(2)}, u32[]{:S(2)}) collective-permute-start(f32[7,64,128]{2,1,0:T(8,128)S(1)} %pad_maximum_fusion), channel_id=1, source_target_pairs={{0,96},{32,0},{64,32},{96,64},{1,97},{33,1},{65,33},{97,65},{2,98}... | collective-permute-start | bytes 688136 | tf_op jit(solution)/shard_map/ppermute | solution.py:18
  5.5 7.5 %collective-permute-start.1 = (f32[7,64,128]{2,1,0:T(8,128)S(1)}, f32[7,64,128]{2,1,0:T(8,128)S(1)}, u32[]{:S(2)}, u32[]{:S(2)}) collective-permute-start(f32[7,64,128]{2,1,0:T(8,128)S(1)} %pad_maximum_fusion.1), channel_id=1, source_target_pairs={{0,32},{32,64},{64,96},{96,0},{1,33},{33,65},{65,97},{97,1},{2,34}... | collective-permute-start | bytes 688136 | tf_op jit(solution)/shard_map/ppermute | solution.py:18
  12.9 1.2 %copy-start.1 = (f32[32,64,128]{2,1,0:T(8,128)S(1)}, f32[32,64,128]{2,1,0:T(8,128)}, u32[]{:S(2)}) copy-start(f32[32,64,128]{2,1,0:T(8,128)} %b.5) | copy-start | bytes 3145732
  14.2 6.1 %copy-start.2 = (f32[32,64,128]{2,1,0:T(8,128)S(1)}, f32[32,64,128]{2,1,0:T(8,128)}, u32[]{:S(2)}) copy-start(f32[32,64,128]{2,1,0:T(8,128)} %b.5) | copy-start | bytes 3145732
  14.2 6.0 %collective-permute-start.2 = (f32[40,8,128]{2,1,0:T(8,128)S(1)}, f32[40,8,128]{2,1,0:T(8,128)S(1)}, u32[]{:S(2)}, u32[]{:S(2)}) collective-permute-start(f32[40,8,128]{2,1,0:T(8,128)S(1)} %get-tuple-element.13), channel_id=1, source_target_pairs={{0,28},{4,0},{8,4},{12,8},{16,12},{20,16},{24,20},{28,24},{1,29},{... | collective-permute-start | bytes 491528 | tf_op jit(solution)/shard_map/ppermute | solution.py:18
  16.0 4.2 %collective-permute-start.3 = (f32[40,8,128]{2,1,0:T(8,128)S(1)}, f32[40,8,128]{2,1,0:T(8,128)S(1)}, u32[]{:S(2)}, u32[]{:S(2)}) collective-permute-start(f32[40,8,128]{2,1,0:T(8,128)S(1)} %get-tuple-element.14), channel_id=1, source_target_pairs={{0,4},{4,8},{8,12},{12,16},{16,20},{20,24},{24,28},{28,0},{1,5},{5... | collective-permute-start | bytes 491528 | tf_op jit(solution)/shard_map/ppermute | solution.py:18
  20.2 10.4 %copy-start.3 = (f32[7,8]{1,0:T(8,128)S(1)}, f32[7,8]{1,0:T(8,128)}, u32[]{:S(2)}) copy-start(f32[7,8]{1,0:T(8,128)} %cond.1) | copy-start | bytes 676
  21.9 5.7 %collective-permute-start.4 = (f32[3,80,128]{2,1,0:T(8,128)S(1)}, f32[3,80,128]{2,1,0:T(8,128)S(1)}, u32[]{:S(2)}, u32[]{:S(2)}) collective-permute-start(f32[3,80,128]{2,1,0:T(8,128)S(1)} %get-tuple-element.15.zu_own), channel_id=1, source_target_pairs={{0,3},{1,0},{2,1},{3,2},{4,7},{5,4},{6,5},{7,6},{8,11},{9,8},{10,9... | collective-permute-start | bytes 368648 | tf_op jit(solution)/shard_map/ppermute | solution.py:18
  25.7 4.9 %collective-permute-start.5 = (f32[3,80,128]{2,1,0:T(8,128)S(1)}, f32[3,80,128]{2,1,0:T(8,128)S(1)}, u32[]{:S(2)}, u32[]{:S(2)}) collective-permute-start(f32[3,80,128]{2,1,0:T(8,128)S(1)} %get-tuple-element.16.zd_own), channel_id=1, source_target_pairs={{0,1},{1,2},{2,3},{3,0},{4,5},{5,6},{6,7},{7,4},{8,9},{9,10},{10,1... | collective-permute-start | bytes 368648 | tf_op jit(solution)/shard_map/ppermute | solution.py:18

commit v3 on v2

--- a/solution.py
+++ b/solution.py
@@ -8,7 +8,7 @@
 LABELS = 8
 ALL = ("gx", "gy", "gz")
 NX, NY, NZ = 32, 64, 128
-XP, RW = NX + 8, NY + 24
+XP, RW = NX + 10, NY + 24
 OWN = slice(8, 8 + NY)
 F32 = jnp.float32
 
@@ -22,7 +22,7 @@
     return lax.broadcasted_iota(jnp.int32, shape, dim)
 
 
-def pack_rows(lab, b, xu, xl, up, down):
+def pack_rows(lab0, lab7, b0, b7, xu, xl, up, down):
     low = iota((8, 128), 0) < 4
     head, tail = pl.ds(0, 8), pl.ds(NY - 8, 8)
 
@@ -31,7 +31,7 @@
         down[xp] = jnp.where(low, pltpu.roll(lab_last, 4, 0), b_last)
 
     for x in range(NX):
-        put(x + 4, lab[x, head].astype(F32), lab[x, tail].astype(F32), b[x, head], b[x, tail])
+        put(x + 4, lab0[x].astype(F32), lab7[x].astype(F32), b0[x], b7[x])
     zero = jnp.zeros((8, 128), F32)
     for k in range(4):
         bk = (xl[k - 1, head], xl[k - 1, tail]) if k else (zero, zero)
@@ -104,8 +104,9 @@
     cond, lab, b, xu, xl, yu, yd, zu_own, zd_own, zu, zd,
     w0o, w1o, w2o, mom,
     f0, f1, f2, f2l, s3, s4, s5, inv, mid, v0, v1, v2, dz, ac, u3, u4, u5,
-    q0, q1, q2, q3, q4, q5, qinv, qmid, qv0, qv1, qv2, qdz, qac, p3, p4, p5,
-    wide, patch_v, patch_q, row_v, row_q,
+    q0, q1, q2, q3, q4, q5, qf1, qf1l, qf2, qf2l, qinv, qmid, qv0, qv1, qv2,
+    qdy, p3, p4, p5,
+    wide, patch_q, row_q,
 ):
     s0, s1, s2 = u3, u4, dz
     sig = (s0, s1, s2, s3, s4, s5)
@@ -231,10 +232,10 @@
                 qinv[xp + 1, pl.ds(off, 8)] = centre
                 qv0[xp + 1, pl.ds(off, 8)] = pltpu.roll(bs[8 * k : 8 * k + 8], 4, 0)
 
-    def set_rows(ref, xp, values):
-        for k in range(values.shape[0]):
-            ref[pl.ds(2 * (xp + k) + 1, 1)] = values[k, 3:4]
-            ref[pl.ds(2 * (xp + k), 1)] = values[k, 12:13]
+    def set_rows(ref, xp, for_first, for_last):
+        for k in range(QB):
+            ref[pl.ds(2 * (xp + k) + 1, 1)] = for_first[k]
+            ref[pl.ds(2 * (xp + k), 1)] = for_last[k]
 
     def set_patch(patch, rows):
         t = rows[...].T
@@ -250,7 +251,7 @@
     QB = 8
 
     def q_loop(body):
-        lax.fori_loop(0, XP // QB, lambda i, c: body(QB * i) or c, 0)
+        lax.fori_loop(0, (NX + 8) // QB, lambda i, c: body(QB * i) or c, 0)
 
     def lanes(x, step):
         return pltpu.roll(x, step % 128, 2)
@@ -258,7 +259,6 @@
     def subs(x, step):
         return pltpu.roll(x, step % 16, 1)
 
-    row_v[...] = jnp.zeros((128, 128), F32)
     row_q[...] = jnp.zeros((128, 128), F32)
 
     def reciprocal(centre, total):
@@ -269,20 +269,24 @@
         c = qinv[at]
         b1 = q1[at]
         b2 = q2[at]
+        r1, l1 = lanes(b1, -1), lanes(b1, 1)
+        r2, l2 = subs(b2, -1), subs(b2, 1)
         total = c + (q0[pl.ds(xp + 2, QB)] + q0[pl.ds(xp, QB)])
-        total = total + (lanes(b1, 1) + lanes(b1, -1))
-        total = total + (subs(b2, 1) + subs(b2, -1))
+        total = total + (l1 + r1)
+        total = total + (l2 + r2)
+        qf1[at] = b1 + r1
+        qf1l[at] = b1 + l1
+        qf2[at] = b2 + r2
+        qf2l[at] = b2 + l2
         r = reciprocal(c, total)
         qinv[at] = r
         qmid[at] = theta * total
         w = qv0[at] * r
         qv0[at] = w
-        set_rows(row_q, xp, b2)
-        set_rows(row_v, xp, w)
+        set_rows(row_q, xp, b2[:, 3:4], b2[:, 12:13])
 
     q_loop(q_diag)
     set_patch(patch_q, row_q)
-    set_patch(patch_v, row_v)
 
     def add(acc, value):
         total, lost = acc
@@ -340,73 +344,106 @@
         def q_first(xp):
             at = pl.ds(xp + 1, QB)
             x = qv[at]
-            left = subs(x, 1)
-            right = subs(x, -1)
-            qdz[at] = right - left
-            qac[at] = q2[at] * (left + right)
-            p3[at] = q3[at] * x
             p4[at] = q4[at] * x
             p5[at] = q5[at] * x
+            if not last:
+                right, left = lanes(x, -1), lanes(x, 1)
+                qdy[at] = right - left
+                p3[at] = q3[at] * x
+                r = qf2[at] * subs(x, -1) + qf2l[at] * subs(x, 1)
+                r = r + (qf1[at] * right + qf1l[at] * left)
+                qw[at] = r - qmid[at] * x
 
         q_loop(q_first)
 
         def q_second(xp):
             at, nx, pr = pl.ds(xp + 1, QB), pl.ds(xp + 2, QB), pl.ds(xp, QB)
-
-            def dy(x):
-                return lanes(x, -1) - lanes(x, 1)
-
-            q = (p4[nx] - p4[pr]) + dy(p5[at])
-            set_rows(row_q, xp, q)
+            xa, x5 = qv[nx], p5[at]
             if not last:
-                x = qv[at]
-                u2 = q2[at] * x
+                xb = qv[pr]
+                dx = xa - xb
+                dx4 = p4[nx] - p4[pr]
+                y = qdy[at]
+            x = qv[at]
+            if last:
+                q = p4[nx] + lanes(x5, -1)
+                e, ex, eq = (t[:, :8] - t[:, 8:] for t in (x, xa, q))
+                ey = pltpu.roll(e, 127, 2)
+            else:
+                q = dx4 + (lanes(x5, -1) - lanes(x5, 1))
+                e, ex, ey, eq = (t[:, :8] - t[:, 8:] for t in (x, dx, y, q))
+
+            def turn(t, step):
+                return pltpu.roll(t, step % 8, 1)
+
+            b4, b5 = q4[at], q5[at]
+            first = -(b4[:, :8] * turn(ex, 1) + b5[:, :8] * turn(ey, 1)) - turn(eq, 1)
+            if not last:
+                first = first + qf2l[at][:, :8] * turn(e, 1)
+            final = qf2[at][:, 8:] * turn(e, -1) + b4[:, 8:] * turn(ex, -1)
+            final = final + b5[:, 8:] * turn(ey, -1) + turn(eq, -1)
+            set_rows(row_q, xp, first[:, 4:5], -final[:, 3:4])
+            if not last:
                 b0 = q0[at]
-                xa, xb = qv[nx], qv[pr]
-                r = (qac[at] - qmid[at] * x) + (b0 + q0[nx]) * xa + (b0 + q0[pr]) * xb
-                u1 = q1[at] * x
-                t = p3[nx] - p3[pr]
-                r = r + q1[at] * (lanes(x, -1) + lanes(x, 1))
-                r = r + lanes(u1 + t, -1) + lanes(u1 - t, 1)
-                r = r + q3[at] * dy(xa - xb)
-                r = r + q4[at] * (qdz[nx] - qdz[pr])
-                r = r + q5[at] * dy(qdz[at])
-                r = r + subs(u2 + q, -1) + subs(u2 - q, 1)
-                out = r * qinv[at]
-                qw[at] = out
-                set_rows(row_v, xp, out)
+                t = (p3[nx] - p3[pr]) + (subs(x5, -1) - subs(x5, 1))
+                r = qw[at] + (b0 + q0[nx]) * xa + (b0 + q0[pr]) * xb
+                r = r + (lanes(t, -1) - lanes(t, 1))
+                r = r + q3[at] * (qdy[nx] - qdy[pr])
+                r = r + b4 * (subs(dx, -1) - subs(dx, 1))
+                r = r + b5 * (subs(y, -1) - subs(y, 1))
+                r = r + (subs(dx4, -1) - subs(dx4, 1))
+                qw[at] = r * qinv[at]
 
         q_loop(q_second)
         set_patch(patch_q, row_q)
 
-        def first_block(xp0, n, acc):
-            for g in range(9):
-                at = group(g)
-                for xp in [xp0 + i for i in range(n)]:
-                    x = v[xp, at]
-                    left, right = sides(x, patch_v, xp, g)
-                    put(dz, xp, g, right - left)
+        def first(g, xps):
+            at = group(g)
+            for xp in xps:
+                x = v[xp, at]
+                left, right = pltpu.roll(x, 1, 1), pltpu.roll(x, 127, 1)
+                put(dz, xp, g, right - left)
+                if last:
+                    ac[xp, at] = f2[xp, at] * right
+                else:
                     ac[xp, at] = f2[xp, at] * right + f2l[xp, at] * left
-                    put(u3, xp, g, s3[xp, at] * x)
-                    u4[xp, at] = s4[xp, at] * x
-                    put(u5, xp, g, s5[xp, at] * x)
-            return acc
-
-        blocks(first_block, extra + 1, 0)
-
-        def second_block(xp0, n, acc):
+                put(u3, xp, g, s3[xp, at] * x)
+                u4[xp, at] = s4[xp, at] * x
+                put(u5, xp, g, s5[xp, at] * x)
+
+        def second_block(xp0, n, acc, then=None):
             def start(g):
                 at, nxt, prv = group(g), pl.ds(9 + 8 * g, 8), pl.ds(7 + 8 * g, 8)
                 a4 = [u4[xp0 - 1 + i, at] for i in range(n + 2)]
                 out = []
                 for i in range(n):
                     xp = xp0 + i
-                    q = (a4[i + 2] - a4[i]) + (u5[xp, nxt] - u5[xp, prv])
-                    left, right = sides(q, patch_q, xp, g)
-                    out.append(right - left)
+                    if last:
+                        q = a4[i + 2] + u5[xp, nxt]
+                    else:
+                        q = (a4[i + 2] - a4[i]) + (u5[xp, nxt] - u5[xp, prv])
+                    p = pltpu.roll(patch_q[at], 127 - 2 * xp, 1)
+                    p = jnp.where((ln == 0) | (ln == 127), p, 0.0)
+                    out.append((pltpu.roll(q, 127, 1) - pltpu.roll(q, 1, 1)) + p)
                 return out
 
+            def finish_half(g, qs, acc):
+                at, nxt, prv = group(g), pl.ds(9 + 8 * g, 8), pl.ds(7 + 8 * g, 8)
+                dots = []
+                for i in range(n):
+                    xp = xp0 + i
+                    x = v[xp, at]
+                    r = ac[xp, at] - (0.5 * mid[xp, at]) * x
+                    r = r + (f0[xp, at] * v[xp + 1, at] + f1[xp, at] * v[xp, nxt])
+                    r = r + s3[xp, at] * (v[xp + 1, nxt] - v[xp + 1, prv])
+                    r = r + (u3[xp + 1, nxt] - u3[xp + 1, prv])
+                    r = r + (s4[xp, at] * dz[xp + 1, at] + s5[xp, at] * dz[xp, nxt])
+                    dots.append((2.0 * x) * (r + qs[i]))
+                return add(acc[0], tree(dots)), acc[1]
+
             def finish(g, qs, acc):
+                if last:
+                    return finish_half(g, qs, acc)
                 at, nxt, prv = group(g), pl.ds(9 + 8 * g, 8), pl.ds(7 + 8 * g, 8)
                 vh = [v[xp0 - 1 + i, at] for i in range(n + 2)]
                 vn = [v[xp0 - 1 + i, nxt] for i in range(n + 2)]
@@ -428,28 +465,44 @@
                     r = r + s5[xp, at] * (dz[xp, nxt] - dz[xp, prv])
                     r = r + qs[i]
                     dots.append(x * r)
-                    if not last:
-                        out = r * inv[xp, at]
-                        put(w, xp, g, out)
-                        norms.append(out * r)
+                    out = r * inv[xp, at]
+                    put(w, xp, g, out)
+                    norms.append(out * r)
                 if acc is None or g == 8:
                     return acc
-                if last:
-                    return add(acc[0], tree(dots)), acc[1]
                 return add(acc[0], tree(dots)), add(acc[1], tree(norms))
 
             count = 8 if last else 9
             ahead = 2
             pending = [start(g) for g in range(ahead)]
-            for g in range(count):
+            for g in range(9):
                 if g + ahead < count:
                     pending.append(start(g + ahead))
-                acc = finish(g, pending.pop(0), acc)
+                if then is not None:
+                    first(g, [then + i for i in range(4)])
+                if g < count:
+                    acc = finish(g, pending.pop(0), acc)
             return acc
 
-        out = blocks(second_block, extra, (none, none))
-        if not last:
-            set_patch(patch_v, row_v)
+        def lead(i, carry):
+            for g in range(9):
+                first(g, [4 * i + 1 + k for k in range(4)])
+            return carry
+
+        lax.fori_loop(0, 2, lead, 0)
+        out = lax.fori_loop(
+            1,
+            1 + NX // 4,
+            lambda i, acc: second_block(4 * i, 4, acc, 4 * i + 5),
+            (none, none),
+        )
+        if extra:
+            lax.fori_loop(
+                0,
+                2,
+                lambda i, c: second_block(4 - extra + (32 + extra) * i, extra, None) or c,
+                0,
+            )
         return out
 
     nu1, nu2 = apply(v0, v1, qv0, qv1, 2, False)
@@ -507,14 +560,26 @@
     return pl.BlockSpec(memory_space=pltpu.VMEM)
 
 
+def pack_planes(lab_head, lab_tail, b_head, b_tail, up, down):
+    up[pl.ds(0, 3)] = b_head[...]
+    up[pl.ds(3, 4)] = lab_head[...].astype(F32)
+    down[pl.ds(0, 3)] = b_tail[...]
+    down[pl.ds(3, 4)] = lab_tail[...].astype(F32)
+
+
 def local(labels, conductivity, right_side):
-    xu_own = jnp.concatenate([right_side[:3], labels[:4].astype(F32)], 0)
-    xl_own = jnp.concatenate([right_side[NX - 3 :], labels[NX - 4 :].astype(F32)], 0)
+    packet = jax.ShapeDtypeStruct((7, NY, NZ), F32)
+    block = jax.ShapeDtypeStruct((NX, NY, NZ), F32)
+    xu_own, xl_own = call(pack_planes, 4, [packet] * 2, 4)(
+        labels[:4], labels[NX - 4 :], right_side[:3], right_side[NX - 3 :]
+    )
     xu = ring(xu_own, "gx", -1)
     xl = ring(xl_own, "gx", 1)
 
-    packet = jax.ShapeDtypeStruct((XP, 8, 128), F32)
-    yu_own, yd_own = call(pack_rows, 4, [packet] * 2, 4)(labels, right_side, xu, xl)
+    packet = jax.ShapeDtypeStruct((NX + 8, 8, 128), F32)
+    yu_own, yd_own = call(pack_rows, 6, [packet] * 2, 4)(
+        labels[:, :8], labels[:, NY - 8 :], right_side[:, :8], right_side[:, NY - 8 :], xu, xl
+    )
     yu = ring(yu_own, "gy", -1)
     yd = ring(yd_own, "gy", 1)
 
@@ -523,7 +588,6 @@
     zu = ring(zu_own, "gz", -1)
     zd = ring(zd_own, "gz", 1)
 
-    block = jax.ShapeDtypeStruct((NX, NY, NZ), F32)
     square = pltpu.VMEM((128, 128), F32)
     patch = pltpu.VMEM((80, 128), F32)
     w0, w1, w2, mom = pl.pallas_call(
@@ -532,8 +596,8 @@
         out_specs=[vmem()] * 4,
         out_shape=[block, block, block, jax.ShapeDtypeStruct((128, 128), F32)],
         scratch_shapes=[pltpu.VMEM((XP, RW, 128), F32)] * 17
-        + [pltpu.VMEM((XP + 2, 16, 128), F32)] * 16
-        + [square, patch, patch, square, square],
+        + [pltpu.VMEM((XP, 16, 128), F32)] * 19
+        + [square, patch, square],
         compiler_params=pltpu.CompilerParams(vmem_limit_bytes=48 * 2**20),
         name="sweeps",
     )(conductivity, labels, right_side, xu, xl, yu, yd, zu_own, zd_own, zu, zd)

time: 70.2 us -> 68.4 us (0.974)
  other arithmetic: 1.02 us -> 0 us
  waiting for transfers between devices: 15.3 us -> 14.3 us
  local copies, waits for them, and re-layouts: 2.28 us -> 3.06 us
    slice x0 -> x3, local copies, waits for them, and re-layouts: none -> 2 us  [the longest x1 0.99 us: local(): right_side[:, NY - 8:]]
    unnamed x8 -> x6, local copies, waits for them, and re-layouts: 1.24 us -> 0.01 us
    ppermute x6, waiting for transfers between devices: 15.3 us -> 14.3 us  [ring(): lax.ppermute(arr, axis, [(i, (i + step) % count) for i in range(count)])]
    convert_element_type x1 -> x0, other arithmetic: 0.99 us -> none  [local(): labels[NX - 4:].astype(F32)]
  transfers between devices with their start and end apart: 6 -> 6, of which waited for: 5 -> 5; matrix products, arithmetic and copies ran while one was open for 0% -> 1% of each run, Pallas kernels for 0% -> 0%
where the time goes in v3:
time: 68.4 us; the launch traced here: 68.2 us
  Pallas kernels  23.5 us (34%)
  blocking collectives  17.1 us (25%)
  waiting for transfers between devices  14.3 us (21%)
  starting transfers between devices  10.2 us (15%)
  local copies, waits for them, and re-layouts  3.06 us (4%)
    pallas_call x1, Pallas kernels, local(): pl.pallas_call(sweeps, in_specs=[pl.BlockSpec(memory_space=pltpu.SMEM)] +...  20.3 us
    all_to_all x1, blocking collectives, local(): mom = lax.all_to_all(mom, ALL, 0, 0, tiled=True)  17.1 us
    ppermute x6, waiting for transfers between devices, ring(): lax.ppermute(arr, axis, [(i, (i + step) % count) for i in range(count)])  14.3 us
    ppermute x6, starting transfers between devices, ring(): lax.ppermute(arr, axis, [(i, (i + step) % count) for i in range(count)])  10.2 us
    pallas_call x1, Pallas kernels, local(): call(pack_lanes, 6, [packet] * 2, 6)(labels, right_side, xu, xl, yu, yd)  1.68 us
    pallas_call x1, Pallas kernels, local(): return call(combine, 4, block, 6)(mom, w0, w1, w2)  1.44 us
  transfers between devices with their start and end apart: 6, of which 5 were waited for; matrix products, arithmetic and copies ran while one was open for 1% of the time, Pallas kernels for 0%

profile of v3, /device:TPU:1, one launch (start us, length us, event | category | flops | bytes accessed | tf_op | source)
XLA Modules:
  0.0 68.2 jit_solution(17876623043502907305)
XLA Ops:
  0.0 0.0 copy-start
  0.0 1.0 %fusion.2 = (f32[3,64,128]{2,1,0:T(8,128)S(1)}, f32[3,64,128]{2,1,0:T(8,128)S(1)}) fusion(f32[32,64,128]{2,1,0:T(8,128)} %b.3), kind=kLoop, calls=%fused_computation.2 | loop fusion | bytes 393216 | tf_op jit(solution)/shard_map/slice | solution.py:574
  1.0 1.0 %fusion.3 = (s32[4,64,128]{2,1,0:T(8,128)S(1)}, s32[4,64,128]{2,1,0:T(8,128)S(1)}) fusion(s32[32,64,128]{2,1,0:T(8,128)} %lab.3), kind=kLoop, calls=%fused_computation.3 | loop fusion | bytes 524288 | tf_op jit(solution)/shard_map/slice | solution.py:574
  2.1 0.0 copy-start.1
  2.1 3.4 %collective-permute-start = (f32[7,64,128]{2,1,0:T(8,128)S(1)}, f32[7,64,128]{2,1,0:T(8,128)S(1)}, u32[]{:S(2)}, u32[]{:S(2)}) collective-permute-start(f32[7,64,128]{2,1,0:T(8,128)S(1)} %get-tuple-element.15), channel_id=1, source_target_pairs={{0,96},{32,0},{64,32},{96,64},{1,97},{33,1},{65,33},{97,65},{2,98}... | collective-permute-start | bytes 688136 | tf_op jit(solution)/shard_map/ppermute | solution.py:18
  5.5 0.0 collective-permute-start.1
  5.5 0.0 copy-done
  5.5 1.0 %fusion = (f32[32,8,128]{2,1,0:T(8,128)S(1)}, f32[32,8,128]{2,1,0:T(8,128)S(1)}) fusion(f32[32,64,128]{2,1,0:T(8,128)} %b.3), kind=kLoop, calls=%fused_computation | loop fusion | bytes 524288 | tf_op jit(solution)/shard_map/slice | solution.py:581
  6.5 3.3 %collective-permute-done.xu = f32[7,64,128]{2,1,0:T(8,128)S(1)} collective-permute-done((f32[7,64,128]{2,1,0:T(8,128)S(1)}, f32[7,64,128]{2,1,0:T(8,128)S(1)}, u32[]{:S(2)}, u32[]{:S(2)}) %collective-permute-start) | collective-permute-done | bytes 229408 | tf_op jit(solution)/shard_map/ppermute | solution.py:18
  9.7 3.1 %collective-permute-done.1.xl = f32[7,64,128]{2,1,0:T(8,128)S(1)} collective-permute-done((f32[7,64,128]{2,1,0:T(8,128)S(1)}, f32[7,64,128]{2,1,0:T(8,128)S(1)}, u32[]{:S(2)}, u32[]{:S(2)}) %collective-permute-start.1) | collective-permute-done | bytes 229408 | tf_op jit(solution)/shard_map/ppermute | solution.py:18
  12.9 1.8 %collective-permute-start.2 = (f32[40,8,128]{2,1,0:T(8,128)S(1)}, f32[40,8,128]{2,1,0:T(8,128)S(1)}, u32[]{:S(2)}, u32[]{:S(2)}) collective-permute-start(f32[40,8,128]{2,1,0:T(8,128)S(1)} %get-tuple-element.17), channel_id=1, source_target_pairs={{0,28},{4,0},{8,4},{12,8},{16,12},{20,16},{24,20},{28,24},{1,29},{... | collective-permute-start | bytes 491528 | tf_op jit(solution)/shard_map/ppermute | solution.py:18
  14.7 1.2 %collective-permute-start.3 = (f32[40,8,128]{2,1,0:T(8,128)S(1)}, f32[40,8,128]{2,1,0:T(8,128)S(1)}, u32[]{:S(2)}, u32[]{:S(2)}) collective-permute-start(f32[40,8,128]{2,1,0:T(8,128)S(1)} %get-tuple-element.18), channel_id=1, source_target_pairs={{0,4},{4,8},{8,12},{12,16},{16,20},{20,24},{24,28},{28,0},{1,5},{5... | collective-permute-start | bytes 491528 | tf_op jit(solution)/shard_map/ppermute | solution.py:18
  16.0 3.0 %collective-permute-done.2.yu = f32[40,8,128]{2,1,0:T(8,128)S(1)} collective-permute-done((f32[40,8,128]{2,1,0:T(8,128)S(1)}, f32[40,8,128]{2,1,0:T(8,128)S(1)}, u32[]{:S(2)}, u32[]{:S(2)}) %collective-permute-start.2) | collective-permute-done | bytes 163872 | tf_op jit(solution)/shard_map/ppermute | solution.py:18
  18.9 0.0 collective-permute-done.3.yd
  18.9 0.0 copy-done.1
  18.9 0.0 copy-start.2
  18.9 1.7 %pack_lanes.1 = (f32[3,80,128]{2,1,0:T(8,128)S(1)}, f32[3,80,128]{2,1,0:T(8,128)S(1)}) custom-call(s32[32,64,128]{2,1,0:T(8,128)S(1)} %copy-done, f32[32,64,128]{2,1,0:T(8,128)S(1)} %copy-done.1, f32[7,64,128]{2,1,0:T(8,128)S(1)} %collective-permute-done.xu, f32[7,64,128]{2,1,0:T(8,128)S(1)} %collective-permute-done.1.xl, ...), custom_call_target="tpu_custom_call" | custom-call | tf_op jit(solution)/shard_map/pack_lanes/pallas_call | solution.py:587
  20.6 3.8 %collective-permute-start.4 = (f32[3,80,128]{2,1,0:T(8,128)S(1)}, f32[3,80,128]{2,1,0:T(8,128)S(1)}, u32[]{:S(2)}, u32[]{:S(2)}) collective-permute-start(f32[3,80,128]{2,1,0:T(8,128)S(1)} %get-tuple-element.19.zu_own), channel_id=1, source_target_pairs={{0,3},{1,0},{2,1},{3,2},{4,7},{5,4},{6,5},{7,6},{8,11},{9,8},{10,9... | collective-permute-start | bytes 368648 | tf_op jit(solution)/shard_map/ppermute | solution.py:18
  24.4 0.0 collective-permute-start.5
  24.4 1.9 %collective-permute-done.4.zu = f32[3,80,128]{2,1,0:T(8,128)S(1)} collective-permute-done((f32[3,80,128]{2,1,0:T(8,128)S(1)}, f32[3,80,128]{2,1,0:T(8,128)S(1)}, u32[]{:S(2)}, u32[]{:S(2)}) %collective-permute-start.4) | collective-permute-done | bytes 122912 | tf_op jit(solution)/shard_map/ppermute | solution.py:18
  26.3 3.1 %collective-permute-done.5.zd = f32[3,80,128]{2,1,0:T(8,128)S(1)} collective-permute-done((f32[3,80,128]{2,1,0:T(8,128)S(1)}, f32[3,80,128]{2,1,0:T(8,128)S(1)}, u32[]{:S(2)}, u32[]{:S(2)}) %collective-permute-start.5) | collective-permute-done | bytes 122912 | tf_op jit(solution)/shard_map/ppermute | solution.py:18
  29.4 0.0 copy-done.2
  29.4 20.3 %sweeps.1 = (f32[32,64,128]{2,1,0:T(8,128)S(1)}, f32[32,64,128]{2,1,0:T(8,128)S(1)}, f32[32,64,128]{2,1,0:T(8,128)S(1)}, f32[128,128]{1,0:T(8,128)S(1)}) custom-call(f32[7,8]{1,0:T(8,128)S(1)} %copy-done.2, s32[32,64,128]{2,1,0:T(8,128)S(1)} %copy-done, f32[32,64,128]{2,1,0:T(8,128)} %b.3, f32[7,64,128]{2,1,0:T(8,128)S(1)} %collective-permute-done.xu, ...), custom_call_target="tpu_custom_call" | custom-call | tf_op jit(solution)/shard_map/sweeps/pallas_call | solution.py:593
  49.7 17.1 %all_to_all.11 = f32[128,1,128]{2,1,0:T(1,128)S(1)} all-to-all(f32[128,1,128]{2,1,0:T(1,128)S(1)} %bitcast.5), channel_id=1, replica_groups=mesh['gx'=4,'gy'=8,'gz'=4] {'gx','gy','gz'}, dimensions={0} | all-to-all | bytes 131072 | tf_op jit(solution)/shard_map/all_to_all | solution.py:604
  66.8 1.4 %combine.1 = f32[32,64,128]{2,1,0:T(8,128)} custom-call(f32[128,128]{1,0:T(8,128)S(1)} %bitcast.4, f32[32,64,128]{2,1,0:T(8,128)S(1)} %get-tuple-element.22.w0, f32[32,64,128]{2,1,0:T(8,128)S(1)} %get-tuple-element.23.w1, f32[32,64,128]{2,1,0:T(8,128)S(1)} %get-tuple-element.24.w2), custom_call_target="tpu_custom_call" | custom-call | tf_op jit(solution)/shard_map/combine/pallas_call | solution.py:605
  (3 shorter events, 0.1 us)
Async XLA Ops:
  0.0 5.5 %copy-start = (s32[32,64,128]{2,1,0:T(8,128)S(1)}, s32[32,64,128]{2,1,0:T(8,128)}, u32[]{:S(2)}) copy-start(s32[32,64,128]{2,1,0:T(8,128)} %lab.3) | copy-start | bytes 3145732
  2.1 16.9 %copy-start.1 = (f32[32,64,128]{2,1,0:T(8,128)S(1)}, f32[32,64,128]{2,1,0:T(8,128)}, u32[]{:S(2)}) copy-start(f32[32,64,128]{2,1,0:T(8,128)} %b.3) | copy-start | bytes 3145732
  2.1 7.7 %collective-permute-start = (f32[7,64,128]{2,1,0:T(8,128)S(1)}, f32[7,64,128]{2,1,0:T(8,128)S(1)}, u32[]{:S(2)}, u32[]{:S(2)}) collective-permute-start(f32[7,64,128]{2,1,0:T(8,128)S(1)} %get-tuple-element.15), channel_id=1, source_target_pairs={{0,96},{32,0},{64,32},{96,64},{1,97},{33,1},{65,33},{97,65},{2,98}... | collective-permute-start | bytes 688136 | tf_op jit(solution)/shard_map/ppermute | solution.py:18
  5.5 7.4 %collective-permute-start.1 = (f32[7,64,128]{2,1,0:T(8,128)S(1)}, f32[7,64,128]{2,1,0:T(8,128)S(1)}, u32[]{:S(2)}, u32[]{:S(2)}) collective-permute-start(f32[7,64,128]{2,1,0:T(8,128)S(1)} %get-tuple-element.16), channel_id=1, source_target_pairs={{0,32},{32,64},{64,96},{96,0},{1,33},{33,65},{65,97},{97,1},{2,34}... | collective-permute-start | bytes 688136 | tf_op jit(solution)/shard_map/ppermute | solution.py:18
  12.9 6.0 %collective-permute-start.2 = (f32[40,8,128]{2,1,0:T(8,128)S(1)}, f32[40,8,128]{2,1,0:T(8,128)S(1)}, u32[]{:S(2)}, u32[]{:S(2)}) collective-permute-start(f32[40,8,128]{2,1,0:T(8,128)S(1)} %get-tuple-element.17), channel_id=1, source_target_pairs={{0,28},{4,0},{8,4},{12,8},{16,12},{20,16},{24,20},{28,24},{1,29},{... | collective-permute-start | bytes 491528 | tf_op jit(solution)/shard_map/ppermute | solution.py:18
  14.7 4.2 %collective-permute-start.3 = (f32[40,8,128]{2,1,0:T(8,128)S(1)}, f32[40,8,128]{2,1,0:T(8,128)S(1)}, u32[]{:S(2)}, u32[]{:S(2)}) collective-permute-start(f32[40,8,128]{2,1,0:T(8,128)S(1)} %get-tuple-element.18), channel_id=1, source_target_pairs={{0,4},{4,8},{8,12},{12,16},{16,20},{20,24},{24,28},{28,0},{1,5},{5... | collective-permute-start | bytes 491528 | tf_op jit(solution)/shard_map/ppermute | solution.py:18
  18.9 10.4 %copy-start.2 = (f32[7,8]{1,0:T(8,128)S(1)}, f32[7,8]{1,0:T(8,128)}, u32[]{:S(2)}) copy-start(f32[7,8]{1,0:T(8,128)} %cond.1) | copy-start | bytes 676
  20.6 5.7 %collective-permute-start.4 = (f32[3,80,128]{2,1,0:T(8,128)S(1)}, f32[3,80,128]{2,1,0:T(8,128)S(1)}, u32[]{:S(2)}, u32[]{:S(2)}) collective-permute-start(f32[3,80,128]{2,1,0:T(8,128)S(1)} %get-tuple-element.19.zu_own), channel_id=1, source_target_pairs={{0,3},{1,0},{2,1},{3,2},{4,7},{5,4},{6,5},{7,6},{8,11},{9,8},{10,9... | collective-permute-start | bytes 368648 | tf_op jit(solution)/shard_map/ppermute | solution.py:18
  24.4 4.9 %collective-permute-start.5 = (f32[3,80,128]{2,1,0:T(8,128)S(1)}, f32[3,80,128]{2,1,0:T(8,128)S(1)}, u32[]{:S(2)}, u32[]{:S(2)}) collective-permute-start(f32[3,80,128]{2,1,0:T(8,128)S(1)} %get-tuple-element.20.zd_own), channel_id=1, source_target_pairs={{0,1},{1,2},{2,3},{3,0},{4,5},{5,6},{6,7},{7,4},{8,9},{9,10},{10,1... | collective-permute-start | bytes 368648 | tf_op jit(solution)/shard_map/ppermute | solution.py:18

commit v4 on v3

--- a/solution.py
+++ b/solution.py
@@ -100,27 +100,17 @@
     return pl.ds(8 + 8 * g, 8)
 
 
-def sweeps(
-    cond, lab, b, xu, xl, yu, yd, zu_own, zd_own, zu, zd,
-    w0o, w1o, w2o, mom,
-    f0, f1, f2, f2l, s3, s4, s5, inv, mid, v0, v1, v2, dz, ac, u3, u4, u5,
-    q0, q1, q2, q3, q4, q5, qf1, qf1l, qf2, qf2l, qinv, qmid, qv0, qv1, qv2,
-    qdy, p3, p4, p5,
-    wide, patch_q, row_q,
-):
-    s0, s1, s2 = u3, u4, dz
-    sig = (s0, s1, s2, s3, s4, s5)
-    qsig = (q0, q1, q2, q3, q4, q5)
-    gx, gy, gz = (lax.axis_index(a) for a in ALL)
-    not_first_x = (gx > 0).astype(F32)
-    not_last_x = (gx < lax.axis_size("gx") - 1).astype(F32)
-    not_first_y = (gy > 0).astype(F32)
-    not_last_y = (gy < lax.axis_size("gy") - 1).astype(F32)
-    not_first_z = (gz > 0).astype(F32)
-    not_last_z = (gz < lax.axis_size("gz") - 1).astype(F32)
-
+def grid_flags():
+    first, last = [], []
+    for axis in ALL:
+        at = lax.axis_index(axis)
+        first.append((at > 0).astype(F32))
+        last.append((at < lax.axis_size(axis) - 1).astype(F32))
+    return first, last
+
+
+def entries_of(cond):
     sub8 = iota((8, 128), 0)
-    ln = iota((8, 128), 1)
     tables = []
     for c in range(7):
         t = jnp.zeros((8, 128), F32)
@@ -129,10 +119,6 @@
             t = jnp.where(sub8 == l, cond[c, l] * scale, t)
         tables.append(t)
 
-    mass = sum(cond[6, l] for l in range(LABELS))
-    faces = sum(cond[c, l] for c in range(3) for l in range(LABELS)) * 2.0
-    theta = jnp.full((1, 128), faces, F32) / jnp.full((1, 128), faces + mass, F32)
-
     def look(c, idx):
         return jnp.take_along_axis(tables[c], idx, axis=0, mode="promise_in_bounds")
 
@@ -143,14 +129,34 @@
         centre = vals[6] + 2.0 * (vals[0] + vals[1] + vals[2])
         return vals[:6], centre
 
+    return entries
+
+
+def put(ref, xp, g, value):
+    ref[xp, group(g)] = value
+    if g == 8:
+        ref[xp, pl.ds(0, 8)] = value
+    if g == 0:
+        ref[xp, pl.ds(80, 8)] = value
+
+
+def blocks(body, extra, sums):
+    if extra:
+        lax.fori_loop(
+            0, 2, lambda i, c: body(4 - extra + (32 + extra) * i, extra, None) or c, 0
+        )
+    return lax.fori_loop(0, NX // 4, lambda i, acc: body(4 * i + 4, 4, acc), sums)
+
+
+OUTSIDE = 1e30
+
+
+def faces(cond, lab, b, xu, xl, yu, yd, f0, f1, diag, s2, s3, s4, s5, v0, s0, s1):
+    sig = (s0, s1, s2, s3, s4, s5)
+    (not_first_x, not_first_y, _), (not_last_x, not_last_y, _) = grid_flags()
+    entries = entries_of(cond)
+    sub8 = iota((8, 128), 0)
     row_on = jnp.where(sub8 < 4, not_last_y, not_first_y)
-
-    def put(ref, xp, g, value):
-        ref[xp, group(g)] = value
-        if g == 8:
-            ref[xp, pl.ds(0, 8)] = value
-        if g == 0:
-            ref[xp, pl.ds(80, 8)] = value
 
     def table_plane(xp, labels_of, b_of, on):
         for g in range(9):
@@ -168,7 +174,7 @@
                     put(s1, xp, g, vals[1])
                 else:
                     sig[c][xp, group(g)] = vals[c]
-            inv[xp, group(g)] = centre
+            diag[xp, group(g)] = centre
 
     def own_plane(x, carry):
         table_plane(
@@ -198,6 +204,41 @@
 
     lax.fori_loop(0, 4, low_plane, 0)
     lax.fori_loop(0, 4, high_plane, 0)
+
+    def sums(xp0, n, acc):
+        for g in range(9):
+            at, nxt, prv = group(g), pl.ds(9 + 8 * g, 8), pl.ds(7 + 8 * g, 8)
+            across = [s0[xp0 - 1 + i, at] for i in range(n + 2)]
+            for i in range(n):
+                xp = xp0 + i
+                c = diag[xp, at]
+                up = s1[xp, nxt]
+                total = c + (across[i + 2] + across[i]) + (up + s1[xp, prv])
+                diag[xp, at] = jnp.where(c > 0, total, OUTSIDE)
+                f0[xp, at] = across[i + 1] + across[i + 2]
+                put(f1, xp, g, s1[xp, at] + up)
+        return acc
+
+    blocks(sums, 3, 0)
+
+
+def sweeps(
+    cond, f0, f1, diag, s2, s3, s4, s5, rhs, zu_own, zd_own, zu, zd,
+    w0o, w1o, w2o, mom,
+    f2, f2l, inv, mid, v0, v1, v2, dz, ac, u3, u4, u5,
+    q0, q1, q2, q3, q4, q5, qf1, qf1l, qf2, qf2l, qinv, qmid, qv0, qv1, qv2,
+    qdy, p3, p4, p5,
+    wide, patch_q, row_q,
+):
+    qsig = (q0, q1, q2, q3, q4, q5)
+    (not_first_x, not_first_y, not_first_z), (not_last_x, not_last_y, not_last_z) = grid_flags()
+    entries = entries_of(cond)
+    sub8 = iota((8, 128), 0)
+    ln = iota((8, 128), 1)
+
+    mass = sum(cond[6, l] for l in range(LABELS))
+    faces = sum(cond[c, l] for c in range(3) for l in range(LABELS)) * 2.0
+    theta = jnp.full((1, 128), faces, F32) / jnp.full((1, 128), faces + mass, F32)
 
     first = iota((80, 128), 1) % 8 < 4
     wide[...] = jnp.zeros((128, 128), F32)
@@ -302,38 +343,25 @@
     zero8 = jnp.zeros((8, 128), F32)
     none = (zero8, zero8)
 
-    def blocks(body, extra, sums):
-        if extra:
-            lax.fori_loop(
-                0, 2, lambda i, c: body(4 - extra + (32 + extra) * i, extra, None) or c, 0
-            )
-        return lax.fori_loop(0, NX // 4, lambda i, acc: body(4 * i + 4, 4, acc), sums)
-
     def diag_block(xp0, n, acc):
         for g in range(9):
-            at, nxt, prv = group(g), pl.ds(9 + 8 * g, 8), pl.ds(7 + 8 * g, 8)
-            faces_x = [s0[xp0 - 1 + i, at] for i in range(n + 2)]
+            at = group(g)
             parts = []
-            for i in range(n):
-                xp = xp0 + i
-                c = inv[xp, at]
-                a1, a1n = s1[xp, at], s1[xp, nxt]
+            for xp in [xp0 + i for i in range(n)]:
                 a2 = s2[xp, at]
                 left, right = sides(a2, patch_q, xp, g)
-                total = c + (faces_x[i + 2] + faces_x[i])
-                total = total + (a1n + s1[xp, prv])
+                total = diag[xp, at]
+                inside = total < 0.5 * OUTSIDE
                 total = total + (left + right)
-                r = reciprocal(c, total)
-                rhs = v0[xp, at]
-                w = rhs * r
+                r = jnp.where(inside, 1.0 / total, 0.0)
+                b = rhs[xp, at]
+                w = b * r
                 inv[xp, at] = r
-                mid[xp, at] = theta * total
+                mid[xp, at] = jnp.where(inside, theta * total, 0.0)
                 put(v0, xp, g, w)
-                f0[xp, at] = faces_x[i + 1] + faces_x[i + 2]
-                put(f1, xp, g, a1 + a1n)
                 f2[xp, at] = a2 + right
                 f2l[xp, at] = a2 + left
-                parts.append(rhs * w)
+                parts.append(b * w)
             if acc is not None and g < 8:
                 acc = add(acc, tree(parts))
         return acc
@@ -590,17 +618,28 @@
 
     square = pltpu.VMEM((128, 128), F32)
     patch = pltpu.VMEM((80, 128), F32)
+    main = (XP, RW, 128)
+    tables = pl.pallas_call(
+        faces,
+        in_specs=[pl.BlockSpec(memory_space=pltpu.SMEM)] + [vmem()] * 6,
+        out_specs=[vmem()] * 8,
+        out_shape=[jax.ShapeDtypeStruct(main, F32)] * 8,
+        scratch_shapes=[pltpu.VMEM(main, F32)] * 2,
+        compiler_params=pltpu.CompilerParams(vmem_limit_bytes=5 * 2**20),
+        cost_estimate=pl.CostEstimate(flops=8 * 10**6, bytes_accessed=0, transcendentals=0),
+        name="faces",
+    )(conductivity, labels, right_side, xu, xl, yu, yd)
     w0, w1, w2, mom = pl.pallas_call(
         sweeps,
-        in_specs=[pl.BlockSpec(memory_space=pltpu.SMEM)] + [vmem()] * 10,
+        in_specs=[pl.BlockSpec(memory_space=pltpu.SMEM)] + [vmem()] * 12,
         out_specs=[vmem()] * 4,
         out_shape=[block, block, block, jax.ShapeDtypeStruct((128, 128), F32)],
-        scratch_shapes=[pltpu.VMEM((XP, RW, 128), F32)] * 17
+        scratch_shapes=[pltpu.VMEM(main, F32)] * 12
         + [pltpu.VMEM((XP, 16, 128), F32)] * 19
         + [square, patch, square],
-        compiler_params=pltpu.CompilerParams(vmem_limit_bytes=48 * 2**20),
+        compiler_params=pltpu.CompilerParams(vmem_limit_bytes=33 * 2**20),
         name="sweeps",
-    )(conductivity, labels, right_side, xu, xl, yu, yd, zu_own, zd_own, zu, zd)
+    )(conductivity, *tables, zu_own, zd_own, zu, zd)
     mom = lax.all_to_all(mom, ALL, 0, 0, tiled=True)
     return call(combine, 4, block, 6)(mom, w0, w1, w2)
 

time: 68.4 us -> 67 us (0.980)
  waiting for transfers between devices: 14.3 us -> 11.7 us
  Pallas kernels: 23.5 us -> 24.5 us
    ppermute x6, waiting for transfers between devices: 14.3 us -> 11.7 us  [ring(): lax.ppermute(arr, axis, [(i, (i + step) % count) for i in range(count)])]
    pallas_call x0 -> x1, Pallas kernels: none -> 2.56 us  [local(): pl.pallas_call(faces, in_specs=[pl.BlockSpec(memory_space=pltpu.SMEM)] +...]
    pallas_call x1, Pallas kernels: 20.3 us -> 18.8 us  [local(): pl.pallas_call(sweeps, in_specs=[pl.BlockSpec(memory_space=pltpu.SMEM)] +...]
    slice x1, local copies, waits for them, and re-layouts: 0.99 us -> 0.02 us  [local(): right_side[:, NY - 8:]]
    slice x1, local copies, waits for them, and re-layouts: 0.02 us -> 0.99 us  [local(): labels[:, NY - 8:]]
  transfers between devices with their start and end apart: 6 -> 6, of which waited for: 5 -> 4; matrix products, arithmetic and copies ran while one was open for 1% -> 2% of each run, Pallas kernels for 0% -> 4%
where the time goes in v4:
time: 67 us; the launch traced here: 66.8 us
  Pallas kernels  24.5 us (37%)
  blocking collectives  17.1 us (26%)
  waiting for transfers between devices  11.7 us (17%)
  starting transfers between devices  10.2 us (15%)
  local copies, waits for them, and re-layouts  3.11 us (5%)
    pallas_call x1, Pallas kernels, local(): pl.pallas_call(sweeps, in_specs=[pl.BlockSpec(memory_space=pltpu.SMEM)] +...  18.8 us
    all_to_all x1, blocking collectives, local(): mom = lax.all_to_all(mom, ALL, 0, 0, tiled=True)  17.1 us
    ppermute x6, waiting for transfers between devices, ring(): lax.ppermute(arr, axis, [(i, (i + step) % count) for i in range(count)])  11.7 us
    ppermute x6, starting transfers between devices, ring(): lax.ppermute(arr, axis, [(i, (i + step) % count) for i in range(count)])  10.2 us
    pallas_call x1, Pallas kernels, local(): pl.pallas_call(faces, in_specs=[pl.BlockSpec(memory_space=pltpu.SMEM)] +...  2.56 us
    pallas_call x1, Pallas kernels, local(): call(pack_lanes, 6, [packet] * 2, 6)(labels, right_side, xu, xl, yu, yd)  1.68 us
    pallas_call x1, Pallas kernels, local(): return call(combine, 4, block, 6)(mom, w0, w1, w2)  1.44 us
  transfers between devices with their start and end apart: 6, of which 4 were waited for; matrix products, arithmetic and copies ran while one was open for 2% of the time, Pallas kernels for 4%

profile of v4, /device:TPU:1, one launch (start us, length us, event | category | flops | bytes accessed | tf_op | source)
XLA Modules:
  0.0 66.8 jit_solution(14462802337544650396)
XLA Ops:
  0.0 0.0 copy-start.1
  0.0 0.0 copy-start
  0.0 1.1 %fusion.2 = (f32[3,64,128]{2,1,0:T(8,128)S(1)}, f32[3,64,128]{2,1,0:T(8,128)S(1)}) fusion(f32[32,64,128]{2,1,0:T(8,128)} %b.3), kind=kLoop, calls=%fused_computation.2 | loop fusion | bytes 393216 | tf_op jit(solution)/shard_map/slice | solution.py:602
  1.1 1.0 %fusion.3 = (s32[4,64,128]{2,1,0:T(8,128)S(1)}, s32[4,64,128]{2,1,0:T(8,128)S(1)}) fusion(s32[32,64,128]{2,1,0:T(8,128)} %lab.3), kind=kLoop, calls=%fused_computation.3 | loop fusion | bytes 524288 | tf_op jit(solution)/shard_map/slice | solution.py:602
  2.1 3.4 %collective-permute-start = (f32[7,64,128]{2,1,0:T(8,128)S(1)}, f32[7,64,128]{2,1,0:T(8,128)S(1)}, u32[]{:S(2)}, u32[]{:S(2)}) collective-permute-start(f32[7,64,128]{2,1,0:T(8,128)S(1)} %get-tuple-element.23), channel_id=1, source_target_pairs={{0,96},{32,0},{64,32},{96,64},{1,97},{33,1},{65,33},{97,65},{2,98}... | collective-permute-start | bytes 688136 | tf_op jit(solution)/shard_map/ppermute | solution.py:18
  5.5 0.0 collective-permute-start.1
  5.5 1.0 %fusion.1 = (s32[32,8,128]{2,1,0:T(8,128)S(1)}, s32[32,8,128]{2,1,0:T(8,128)S(1)}) fusion(s32[32,64,128]{2,1,0:T(8,128)} %lab.3), kind=kLoop, calls=%fused_computation.1 | loop fusion | bytes 524288 | tf_op jit(solution)/shard_map/slice | solution.py:609
  6.5 0.0 copy-done.1
  6.5 3.3 %collective-permute-done.xu = f32[7,64,128]{2,1,0:T(8,128)S(1)} collective-permute-done((f32[7,64,128]{2,1,0:T(8,128)S(1)}, f32[7,64,128]{2,1,0:T(8,128)S(1)}, u32[]{:S(2)}, u32[]{:S(2)}) %collective-permute-start) | collective-permute-done | bytes 229408 | tf_op jit(solution)/shard_map/ppermute | solution.py:18
  9.8 3.1 %collective-permute-done.1.xl = f32[7,64,128]{2,1,0:T(8,128)S(1)} collective-permute-done((f32[7,64,128]{2,1,0:T(8,128)S(1)}, f32[7,64,128]{2,1,0:T(8,128)S(1)}, u32[]{:S(2)}, u32[]{:S(2)}) %collective-permute-start.1) | collective-permute-done | bytes 229408 | tf_op jit(solution)/shard_map/ppermute | solution.py:18
  12.9 0.0 copy-start.2
  13.0 1.8 %collective-permute-start.2 = (f32[40,8,128]{2,1,0:T(8,128)S(1)}, f32[40,8,128]{2,1,0:T(8,128)S(1)}, u32[]{:S(2)}, u32[]{:S(2)}) collective-permute-start(f32[40,8,128]{2,1,0:T(8,128)S(1)} %get-tuple-element.25), channel_id=1, source_target_pairs={{0,28},{4,0},{8,4},{12,8},{16,12},{20,16},{24,20},{28,24},{1,29},{... | collective-permute-start | bytes 491528 | tf_op jit(solution)/shard_map/ppermute | solution.py:18
  14.8 1.2 %collective-permute-start.3 = (f32[40,8,128]{2,1,0:T(8,128)S(1)}, f32[40,8,128]{2,1,0:T(8,128)S(1)}, u32[]{:S(2)}, u32[]{:S(2)}) collective-permute-start(f32[40,8,128]{2,1,0:T(8,128)S(1)} %get-tuple-element.26), channel_id=1, source_target_pairs={{0,4},{4,8},{8,12},{12,16},{16,20},{20,24},{24,28},{28,0},{1,5},{5... | collective-permute-start | bytes 491528 | tf_op jit(solution)/shard_map/ppermute | solution.py:18
  16.0 3.0 %collective-permute-done.2.yu = f32[40,8,128]{2,1,0:T(8,128)S(1)} collective-permute-done((f32[40,8,128]{2,1,0:T(8,128)S(1)}, f32[40,8,128]{2,1,0:T(8,128)S(1)}, u32[]{:S(2)}, u32[]{:S(2)}) %collective-permute-start.2) | collective-permute-done | bytes 163872 | tf_op jit(solution)/shard_map/ppermute | solution.py:18
  19.0 0.0 collective-permute-done.3.yd
  19.0 0.0 copy-done
  19.0 1.7 %pack_lanes.1 = (f32[3,80,128]{2,1,0:T(8,128)S(1)}, f32[3,80,128]{2,1,0:T(8,128)S(1)}) custom-call(s32[32,64,128]{2,1,0:T(8,128)S(1)} %copy-done, f32[32,64,128]{2,1,0:T(8,128)S(1)} %copy-done.1, f32[7,64,128]{2,1,0:T(8,128)S(1)} %collective-permute-done.xu, f32[7,64,128]{2,1,0:T(8,128)S(1)} %collective-permute-done.1.xl, ...), custom_call_target="tpu_custom_call" | custom-call | tf_op jit(solution)/shard_map/pack_lanes/pallas_call | solution.py:615
  20.7 3.8 %collective-permute-start.4 = (f32[3,80,128]{2,1,0:T(8,128)S(1)}, f32[3,80,128]{2,1,0:T(8,128)S(1)}, u32[]{:S(2)}, u32[]{:S(2)}) collective-permute-start(f32[3,80,128]{2,1,0:T(8,128)S(1)} %get-tuple-element.35.zu_own), channel_id=1, source_target_pairs={{0,3},{1,0},{2,1},{3,2},{4,7},{5,4},{6,5},{7,6},{8,11},{9,8},{10,9... | collective-permute-start | bytes 368648 | tf_op jit(solution)/shard_map/ppermute | solution.py:18
  24.5 0.0 collective-permute-start.5
  24.5 0.0 copy-done.2
  24.5 2.6 %faces.1 = (f32[42,88,128]{2,1,0:T(8,128)S(1)}, f32[42,88,128]{2,1,0:T(8,128)S(1)}, f32[42,88,128]{2,1,0:T(8,128)S(1)}, f32[42,88,128]{2,1,0:T(8,128)S(1)}, f32[...) custom-call(f32[7,8]{1,0:T(8,128)S(1)} %copy-done.2, ...), custom_call_target="tpu_custom_call" | custom-call | flops 8000000 | tf_op jit(solution)/shard_map/faces/pallas_call | solution.py:622
  27.0 0.0 collective-permute-done.4.zu
  27.0 2.4 %collective-permute-done.5.zd = f32[3,80,128]{2,1,0:T(8,128)S(1)} collective-permute-done((f32[3,80,128]{2,1,0:T(8,128)S(1)}, f32[3,80,128]{2,1,0:T(8,128)S(1)}, u32[]{:S(2)}, u32[]{:S(2)}) %collective-permute-start.5) | collective-permute-done | bytes 122912 | tf_op jit(solution)/shard_map/ppermute | solution.py:18
  29.4 18.8 %sweeps.1 = (f32[32,64,128]{2,1,0:T(8,128)S(1)}, f32[32,64,128]{2,1,0:T(8,128)S(1)}, f32[32,64,128]{2,1,0:T(8,128)S(1)}, f32[128,128]{1,0:T(8,128)S(1)}) custom-call(f32[7,8]{1,0:T(8,128)S(1)} %copy-done.2, f32[42,88,128]{2,1,0:T(8,128)S(1)} %get-tuple-element.27.f0, f32[42,88,128]{2,1,0:T(8,128)S(1)} %get-tuple-element.28.f1, ...), custom_call_target="tpu_custom_call" | custom-call | tf_op jit(solution)/shard_map/sweeps/pallas_call | solution.py:632
  48.2 17.1 %all_to_all.11 = f32[128,1,128]{2,1,0:T(1,128)S(1)} all-to-all(f32[128,1,128]{2,1,0:T(1,128)S(1)} %bitcast.5), channel_id=1, replica_groups=mesh['gx'=4,'gy'=8,'gz'=4] {'gx','gy','gz'}, dimensions={0} | all-to-all | bytes 131072 | tf_op jit(solution)/shard_map/all_to_all | solution.py:643
  65.3 1.4 %combine.1 = f32[32,64,128]{2,1,0:T(8,128)} custom-call(f32[128,128]{1,0:T(8,128)S(1)} %bitcast.4, f32[32,64,128]{2,1,0:T(8,128)S(1)} %get-tuple-element.38.w0, f32[32,64,128]{2,1,0:T(8,128)S(1)} %get-tuple-element.39.w1, f32[32,64,128]{2,1,0:T(8,128)S(1)} %get-tuple-element.40.w2), custom_call_target="tpu_custom_call" | custom-call | tf_op jit(solution)/shard_map/combine/pallas_call | solution.py:644
  (3 shorter events, 0.1 us)
Async XLA Ops:
  0.0 6.5 %copy-start.1 = (f32[32,64,128]{2,1,0:T(8,128)S(1)}, f32[32,64,128]{2,1,0:T(8,128)}, u32[]{:S(2)}) copy-start(f32[32,64,128]{2,1,0:T(8,128)} %b.3) | copy-start | bytes 3145732
  0.0 19.0 %copy-start = (s32[32,64,128]{2,1,0:T(8,128)S(1)}, s32[32,64,128]{2,1,0:T(8,128)}, u32[]{:S(2)}) copy-start(s32[32,64,128]{2,1,0:T(8,128)} %lab.3) | copy-start | bytes 3145732
  2.1 7.7 %collective-permute-start = (f32[7,64,128]{2,1,0:T(8,128)S(1)}, f32[7,64,128]{2,1,0:T(8,128)S(1)}, u32[]{:S(2)}, u32[]{:S(2)}) collective-permute-start(f32[7,64,128]{2,1,0:T(8,128)S(1)} %get-tuple-element.23), channel_id=1, source_target_pairs={{0,96},{32,0},{64,32},{96,64},{1,97},{33,1},{65,33},{97,65},{2,98}... | collective-permute-start | bytes 688136 | tf_op jit(solution)/shard_map/ppermute | solution.py:18
  5.5 7.4 %collective-permute-start.1 = (f32[7,64,128]{2,1,0:T(8,128)S(1)}, f32[7,64,128]{2,1,0:T(8,128)S(1)}, u32[]{:S(2)}, u32[]{:S(2)}) collective-permute-start(f32[7,64,128]{2,1,0:T(8,128)S(1)} %get-tuple-element.24), channel_id=1, source_target_pairs={{0,32},{32,64},{64,96},{96,0},{1,33},{33,65},{65,97},{97,1},{2,34}... | collective-permute-start | bytes 688136 | tf_op jit(solution)/shard_map/ppermute | solution.py:18
  12.9 11.5 %copy-start.2 = (f32[7,8]{1,0:T(8,128)S(1)}, f32[7,8]{1,0:T(8,128)}, u32[]{:S(2)}) copy-start(f32[7,8]{1,0:T(8,128)} %cond.3) | copy-start | bytes 676
  13.0 6.0 %collective-permute-start.2 = (f32[40,8,128]{2,1,0:T(8,128)S(1)}, f32[40,8,128]{2,1,0:T(8,128)S(1)}, u32[]{:S(2)}, u32[]{:S(2)}) collective-permute-start(f32[40,8,128]{2,1,0:T(8,128)S(1)} %get-tuple-element.25), channel_id=1, source_target_pairs={{0,28},{4,0},{8,4},{12,8},{16,12},{20,16},{24,20},{28,24},{1,29},{... | collective-permute-start | bytes 491528 | tf_op jit(solution)/shard_map/ppermute | solution.py:18
  14.8 4.2 %collective-permute-start.3 = (f32[40,8,128]{2,1,0:T(8,128)S(1)}, f32[40,8,128]{2,1,0:T(8,128)S(1)}, u32[]{:S(2)}, u32[]{:S(2)}) collective-permute-start(f32[40,8,128]{2,1,0:T(8,128)S(1)} %get-tuple-element.26), channel_id=1, source_target_pairs={{0,4},{4,8},{8,12},{12,16},{16,20},{20,24},{24,28},{28,0},{1,5},{5... | collective-permute-start | bytes 491528 | tf_op jit(solution)/shard_map/ppermute | solution.py:18
  20.7 6.4 %collective-permute-start.4 = (f32[3,80,128]{2,1,0:T(8,128)S(1)}, f32[3,80,128]{2,1,0:T(8,128)S(1)}, u32[]{:S(2)}, u32[]{:S(2)}) collective-permute-start(f32[3,80,128]{2,1,0:T(8,128)S(1)} %get-tuple-element.35.zu_own), channel_id=1, source_target_pairs={{0,3},{1,0},{2,1},{3,2},{4,7},{5,4},{6,5},{7,6},{8,11},{9,8},{10,9... | collective-permute-start | bytes 368648 | tf_op jit(solution)/shard_map/ppermute | solution.py:18
  24.5 4.9 %collective-permute-start.5 = (f32[3,80,128]{2,1,0:T(8,128)S(1)}, f32[3,80,128]{2,1,0:T(8,128)S(1)}, u32[]{:S(2)}, u32[]{:S(2)}) collective-permute-start(f32[3,80,128]{2,1,0:T(8,128)S(1)} %get-tuple-element.36.zd_own), channel_id=1, source_target_pairs={{0,1},{1,2},{2,3},{3,0},{4,5},{5,6},{6,7},{7,4},{8,9},{9,10},{10,1... | collective-permute-start | bytes 368648 | tf_op jit(solution)/shard_map/ppermute | solution.py:18

commit v5 on v4

--- a/solution.py
+++ b/solution.py
@@ -50,50 +50,62 @@
     return jnp.where(low, yu[xp], yd[xp])
 
 
-def pack_lanes(lab, b, xu, xl, yu, yd, up, down):
+def gather(lane, planes, of, g, acc):
+    for xp in planes:
+        if xp // 16 != g:
+            continue
+        k = xp % 16
+        shift = (8 * k + 4) % 128
+        value = of(xp)
+        acc = jnp.where(lane // 8 == k, pltpu.roll(value, shift, 1) if shift else value, acc)
+    return acc
+
+
+def pack_own(lab, b, lab_part, b_part):
+    lane = iota((8, 128), 1)
+    zero = jnp.zeros((8, 128), F32)
+
+    def rows(rg, carry):
+        at = pl.ds(pl.multiple_of(8 * rg, 8), 8)
+        own = range(4, NX + 4)
+        for g in range(3):
+            lab_part[g, at] = gather(lane, own, lambda xp: lab[xp - 4, at].astype(F32), g, zero)
+            b_part[g, at] = gather(lane, own, lambda xp: b[xp - 4, at], g, zero)
+        return carry
+
+    lax.fori_loop(0, NY // 8, rows, 0)
+
+
+def pack_lanes(lab_part, b_part, xu, xl, yu, yd, up, down):
     lane = iota((8, 128), 1)
     first = lane % 8 < 4
     zero = jnp.zeros((8, 128), F32)
 
-    def pack(at, lab_of, b_of):
-        for g in range(3):
-            acc_lab, acc_b = zero, zero
-            for k in range(16 if g < 2 else 8):
-                hit = lane // 8 == k
-                shift = (8 * k + 4) % 128
-                turn = lambda t: pltpu.roll(t, shift, 1) if shift else t
-                acc_lab = jnp.where(hit, turn(lab_of(16 * g + k)), acc_lab)
-                acc_b = jnp.where(hit, turn(b_of(16 * g + k)), acc_b)
-            for off in at:
-                down[g, off] = jnp.where(first, acc_lab, pltpu.roll(acc_b, 4, 1))
-                up[g, off] = jnp.where(first, pltpu.roll(acc_b, 124, 1), acc_lab)
-
-    def rows(rg, carry):
-        at = pl.ds(pl.multiple_of(8 * rg, 8), 8)
-
-        def lab_of(xp):
-            if xp < 4:
-                return xl[3 + xp, at]
-            if xp >= 36:
-                return xu[xp - 33, at]
-            return lab[xp - 4, at].astype(F32)
-
-        def b_of(xp):
-            if xp < 4:
-                return xl[xp - 1, at] if xp else zero
-            if xp >= 36:
+    def send(g, at, lab, b):
+        down[g, at] = jnp.where(first, lab, pltpu.roll(b, 4, 1))
+        up[g, at] = jnp.where(first, pltpu.roll(b, 124, 1), lab)
+
+    everything = range(NX + 8)
+    beside = [xp for xp in everything if xp < 4 or xp >= NX + 4]
+    for g in range(3):
+        lab = gather(lane, everything, lambda xp: rows_lab(yu, yd, xp), g, zero)
+        b = gather(lane, everything, lambda xp: rows_b(yu, yd, xp), g, zero)
+        send(g, pl.ds(0, 8), lab, b)
+        send(g, pl.ds(72, 8), lab, b)
+        for rg in range(NY // 8):
+            at = pl.ds(8 * rg, 8)
+
+            def lab_of(xp):
+                return xl[3 + xp, at] if xp < 4 else xu[xp - 33, at]
+
+            def b_of(xp):
+                if xp < 4:
+                    return xl[xp - 1, at] if xp else zero
                 return xu[xp - 36, at] if xp < 39 else zero
-            return b[xp - 4, at]
-
-        pack((pl.ds(pl.multiple_of(8 * rg + 8, 8), 8),), lab_of, b_of)
-        return carry
-
-    lax.fori_loop(0, 8, rows, 0)
-    pack(
-        (pl.ds(0, 8), pl.ds(72, 8)),
-        lambda xp: rows_lab(yu, yd, xp),
-        lambda xp: rows_b(yu, yd, xp),
-    )
+
+            lab = gather(lane, beside, lab_of, g, lab_part[g, at])
+            b = gather(lane, beside, b_of, g, b_part[g, at])
+            send(g, group(rg), lab, b)
 
 
 def group(g):
@@ -289,7 +301,7 @@
         right = jnp.where(ln == 127, p, pltpu.roll(value, 127, 1))
         return left, right
 
-    QB = 8
+    QB = 40
 
     def q_loop(body):
         lax.fori_loop(0, (NX + 8) // QB, lambda i, c: body(QB * i) or c, 0)
@@ -604,6 +616,17 @@
     xu = ring(xu_own, "gx", -1)
     xl = ring(xl_own, "gx", 1)
 
+    packet = jax.ShapeDtypeStruct((3, NY, 128), F32)
+    lab_part, b_part = pl.pallas_call(
+        pack_own,
+        in_specs=[vmem()] * 2,
+        out_specs=[vmem()] * 2,
+        out_shape=[packet] * 2,
+        compiler_params=pltpu.CompilerParams(vmem_limit_bytes=4 * 2**20),
+        cost_estimate=pl.CostEstimate(flops=4 * 10**6, bytes_accessed=0, transcendentals=0),
+        name="pack_own",
+    )(labels, right_side)
+
     packet = jax.ShapeDtypeStruct((NX + 8, 8, 128), F32)
     yu_own, yd_own = call(pack_rows, 6, [packet] * 2, 4)(
         labels[:, :8], labels[:, NY - 8 :], right_side[:, :8], right_side[:, NY - 8 :], xu, xl
@@ -612,7 +635,7 @@
     yd = ring(yd_own, "gy", 1)
 
     packet = jax.ShapeDtypeStruct((3, 80, 128), F32)
-    zu_own, zd_own = call(pack_lanes, 6, [packet] * 2, 6)(labels, right_side, xu, xl, yu, yd)
+    zu_own, zd_own = call(pack_lanes, 6, [packet] * 2, 4)(lab_part, b_part, xu, xl, yu, yd)
     zu = ring(zu_own, "gz", -1)
     zd = ring(zd_own, "gz", 1)
 

time: 67 us -> 64.7 us (0.966)
  Pallas kernels: 24.5 us -> 23.3 us
  waiting for transfers between devices: 11.7 us -> 10.6 us
    pallas_call x1, Pallas kernels: 18.8 us -> 17.3 us  [local(): pl.pallas_call(sweeps, in_specs=[pl.BlockSpec(memory_space=pltpu.SMEM)] +...]
    ppermute x6, waiting for transfers between devices: 11.7 us -> 10.6 us  [ring(): lax.ppermute(arr, axis, [(i, (i + step) % count) for i in range(count)])]
    pallas_call x1 -> x2, Pallas kernels: 1.68 us -> 1.94 us  [the longest x1 1.09 us: local(): pl.pallas_call(pack_own, in_specs=[vmem()] * 2, out_specs=[vmem()] * 2, o...]
  transfers between devices with their start and end apart: 6 -> 6, of which waited for: 4 -> 4; matrix products, arithmetic and copies ran while one was open for 2% -> 2% of each run, Pallas kernels for 4% -> 6%
where the time goes in v5:
time: 64.7 us; the launch traced here: 64.5 us
  Pallas kernels  23.3 us (36%)
  blocking collectives  17.1 us (26%)
  waiting for transfers between devices  10.6 us (16%)
  starting transfers between devices  10.2 us (16%)
  local copies, waits for them, and re-layouts  3.11 us (5%)
    pallas_call x1, Pallas kernels, local(): pl.pallas_call(sweeps, in_specs=[pl.BlockSpec(memory_space=pltpu.SMEM)] +...  17.3 us
    all_to_all x1, blocking collectives, local(): mom = lax.all_to_all(mom, ALL, 0, 0, tiled=True)  17.1 us
    ppermute x6, waiting for transfers between devices, ring(): lax.ppermute(arr, axis, [(i, (i + step) % count) for i in range(count)])  10.6 us
    ppermute x6, starting transfers between devices, ring(): lax.ppermute(arr, axis, [(i, (i + step) % count) for i in range(count)])  10.2 us
    pallas_call x1, Pallas kernels, local(): pl.pallas_call(faces, in_specs=[pl.BlockSpec(memory_space=pltpu.SMEM)] +...  2.56 us
    pallas_call x1, Pallas kernels, local(): return call(combine, 4, block, 6)(mom, w0, w1, w2)  1.44 us
  transfers between devices with their start and end apart: 6, of which 4 were waited for; matrix products, arithmetic and copies ran while one was open for 2% of the time, Pallas kernels for 6%

profile of v5, /device:TPU:1, one launch (start us, length us, event | category | flops | bytes accessed | tf_op | source)
XLA Modules:
  0.0 64.5 jit_solution(8337068614083316661)
XLA Ops:
  0.0 0.0 copy-start.1
  0.0 0.0 copy-start
  0.0 1.1 %fusion.2 = (f32[3,64,128]{2,1,0:T(8,128)S(1)}, f32[3,64,128]{2,1,0:T(8,128)S(1)}) fusion(f32[32,64,128]{2,1,0:T(8,128)} %b.3), kind=kLoop, calls=%fused_computation.2 | loop fusion | bytes 393216 | tf_op jit(solution)/shard_map/slice | solution.py:614
  1.1 1.0 %fusion.3 = (s32[4,64,128]{2,1,0:T(8,128)S(1)}, s32[4,64,128]{2,1,0:T(8,128)S(1)}) fusion(s32[32,64,128]{2,1,0:T(8,128)} %lab.3), kind=kLoop, calls=%fused_computation.3 | loop fusion | bytes 524288 | tf_op jit(solution)/shard_map/slice | solution.py:614
  2.1 3.4 %collective-permute-start = (f32[7,64,128]{2,1,0:T(8,128)S(1)}, f32[7,64,128]{2,1,0:T(8,128)S(1)}, u32[]{:S(2)}, u32[]{:S(2)}) collective-permute-start(f32[7,64,128]{2,1,0:T(8,128)S(1)} %get-tuple-element.25), channel_id=1, source_target_pairs={{0,96},{32,0},{64,32},{96,64},{1,97},{33,1},{65,33},{97,65},{2,98}... | collective-permute-start | bytes 688136 | tf_op jit(solution)/shard_map/ppermute | solution.py:18
  5.5 0.0 collective-permute-start.1
  5.5 1.0 %fusion.1 = (s32[32,8,128]{2,1,0:T(8,128)S(1)}, s32[32,8,128]{2,1,0:T(8,128)S(1)}) fusion(s32[32,64,128]{2,1,0:T(8,128)} %lab.3), kind=kLoop, calls=%fused_computation.1 | loop fusion | bytes 524288 | tf_op jit(solution)/shard_map/slice | solution.py:632
  6.5 0.0 copy-done.1
  6.5 3.3 %collective-permute-done.xu = f32[7,64,128]{2,1,0:T(8,128)S(1)} collective-permute-done((f32[7,64,128]{2,1,0:T(8,128)S(1)}, f32[7,64,128]{2,1,0:T(8,128)S(1)}, u32[]{:S(2)}, u32[]{:S(2)}) %collective-permute-start) | collective-permute-done | bytes 229408 | tf_op jit(solution)/shard_map/ppermute | solution.py:18
  9.8 3.1 %collective-permute-done.1.xl = f32[7,64,128]{2,1,0:T(8,128)S(1)} collective-permute-done((f32[7,64,128]{2,1,0:T(8,128)S(1)}, f32[7,64,128]{2,1,0:T(8,128)S(1)}, u32[]{:S(2)}, u32[]{:S(2)}) %collective-permute-start.1) | collective-permute-done | bytes 229408 | tf_op jit(solution)/shard_map/ppermute | solution.py:18
  12.9 0.0 copy-start.2
  13.0 1.8 %collective-permute-start.2 = (f32[40,8,128]{2,1,0:T(8,128)S(1)}, f32[40,8,128]{2,1,0:T(8,128)S(1)}, u32[]{:S(2)}, u32[]{:S(2)}) collective-permute-start(f32[40,8,128]{2,1,0:T(8,128)S(1)} %get-tuple-element.27), channel_id=1, source_target_pairs={{0,28},{4,0},{8,4},{12,8},{16,12},{20,16},{24,20},{28,24},{1,29},{... | collective-permute-start | bytes 491528 | tf_op jit(solution)/shard_map/ppermute | solution.py:18
  14.8 1.2 %collective-permute-start.3 = (f32[40,8,128]{2,1,0:T(8,128)S(1)}, f32[40,8,128]{2,1,0:T(8,128)S(1)}, u32[]{:S(2)}, u32[]{:S(2)}) collective-permute-start(f32[40,8,128]{2,1,0:T(8,128)S(1)} %get-tuple-element.28), channel_id=1, source_target_pairs={{0,4},{4,8},{8,12},{12,16},{16,20},{20,24},{24,28},{28,0},{1,5},{5... | collective-permute-start | bytes 491528 | tf_op jit(solution)/shard_map/ppermute | solution.py:18
  16.0 0.0 copy-done
  16.0 1.1 %pack_own.1 = (f32[3,64,128]{2,1,0:T(8,128)S(1)}, f32[3,64,128]{2,1,0:T(8,128)S(1)}) custom-call(s32[32,64,128]{2,1,0:T(8,128)S(1)} %copy-done, f32[32,64,128]{2,1,0:T(8,128)S(1)} %copy-done.1), custom_call_target="tpu_custom_call" | custom-call | flops 4000000 | tf_op jit(solution)/shard_map/pack_own/pallas_call | solution.py:620
  17.1 1.9 %collective-permute-done.2.yu = f32[40,8,128]{2,1,0:T(8,128)S(1)} collective-permute-done((f32[40,8,128]{2,1,0:T(8,128)S(1)}, f32[40,8,128]{2,1,0:T(8,128)S(1)}, u32[]{:S(2)}, u32[]{:S(2)}) %collective-permute-start.2) | collective-permute-done | bytes 163872 | tf_op jit(solution)/shard_map/ppermute | solution.py:18
  19.0 0.0 collective-permute-done.3.yd
  19.0 0.9 %pack_lanes.1 = (f32[3,80,128]{2,1,0:T(8,128)S(1)}, f32[3,80,128]{2,1,0:T(8,128)S(1)}) custom-call(f32[3,64,128]{2,1,0:T(8,128)S(1)} %get-tuple-element.37.lab_part, f32[3,64,128]{2,1,0:T(8,128)S(1)} %get-tuple-element.38.b_part, f32[7,64,128]{2,1,0:T(8,128)S(1)} %collective-permute-done.xu, f32[7,64,128]{2,1,0:T(8,128)S(1)} %collective-permute-done.1.xl, ...), custom_call_target="tpu_custom_call" | custom-call | tf_op jit(solution)/shard_map/pack_lanes/pallas_call | solution.py:638
  19.8 3.8 %collective-permute-start.4 = (f32[3,80,128]{2,1,0:T(8,128)S(1)}, f32[3,80,128]{2,1,0:T(8,128)S(1)}, u32[]{:S(2)}, u32[]{:S(2)}) collective-permute-start(f32[3,80,128]{2,1,0:T(8,128)S(1)} %get-tuple-element.39.zu_own), channel_id=1, source_target_pairs={{0,3},{1,0},{2,1},{3,2},{4,7},{5,4},{6,5},{7,6},{8,11},{9,8},{10,9... | collective-permute-start | bytes 368648 | tf_op jit(solution)/shard_map/ppermute | solution.py:18
  23.7 0.0 collective-permute-start.5
  23.7 0.0 copy-done.2
  23.7 2.6 %faces.1 = (f32[42,88,128]{2,1,0:T(8,128)S(1)}, f32[42,88,128]{2,1,0:T(8,128)S(1)}, f32[42,88,128]{2,1,0:T(8,128)S(1)}, f32[42,88,128]{2,1,0:T(8,128)S(1)}, f32[...) custom-call(f32[7,8]{1,0:T(8,128)S(1)} %copy-done.2, ...), custom_call_target="tpu_custom_call" | custom-call | flops 8000000 | tf_op jit(solution)/shard_map/faces/pallas_call | solution.py:645
  26.2 0.0 collective-permute-done.4.zu
  26.3 2.4 %collective-permute-done.5.zd = f32[3,80,128]{2,1,0:T(8,128)S(1)} collective-permute-done((f32[3,80,128]{2,1,0:T(8,128)S(1)}, f32[3,80,128]{2,1,0:T(8,128)S(1)}, u32[]{:S(2)}, u32[]{:S(2)}) %collective-permute-start.5) | collective-permute-done | bytes 122912 | tf_op jit(solution)/shard_map/ppermute | solution.py:18
  28.6 17.3 %sweeps.1 = (f32[32,64,128]{2,1,0:T(8,128)S(1)}, f32[32,64,128]{2,1,0:T(8,128)S(1)}, f32[32,64,128]{2,1,0:T(8,128)S(1)}, f32[128,128]{1,0:T(8,128)S(1)}) custom-call(f32[7,8]{1,0:T(8,128)S(1)} %copy-done.2, f32[42,88,128]{2,1,0:T(8,128)S(1)} %get-tuple-element.29.f0, f32[42,88,128]{2,1,0:T(8,128)S(1)} %get-tuple-element.30.f1, ...), custom_call_target="tpu_custom_call" | custom-call | tf_op jit(solution)/shard_map/sweeps/pallas_call | solution.py:655
  45.9 17.1 %all_to_all.11 = f32[128,1,128]{2,1,0:T(1,128)S(1)} all-to-all(f32[128,1,128]{2,1,0:T(1,128)S(1)} %bitcast.5), channel_id=1, replica_groups=mesh['gx'=4,'gy'=8,'gz'=4] {'gx','gy','gz'}, dimensions={0} | all-to-all | bytes 131072 | tf_op jit(solution)/shard_map/all_to_all | solution.py:666
  63.1 1.4 %combine.1 = f32[32,64,128]{2,1,0:T(8,128)} custom-call(f32[128,128]{1,0:T(8,128)S(1)} %bitcast.4, f32[32,64,128]{2,1,0:T(8,128)S(1)} %get-tuple-element.42.w0, f32[32,64,128]{2,1,0:T(8,128)S(1)} %get-tuple-element.43.w1, f32[32,64,128]{2,1,0:T(8,128)S(1)} %get-tuple-element.44.w2), custom_call_target="tpu_custom_call" | custom-call | tf_op jit(solution)/shard_map/combine/pallas_call | solution.py:667
  (3 shorter events, 0.1 us)
Async XLA Ops:
  0.0 6.5 %copy-start.1 = (f32[32,64,128]{2,1,0:T(8,128)S(1)}, f32[32,64,128]{2,1,0:T(8,128)}, u32[]{:S(2)}) copy-start(f32[32,64,128]{2,1,0:T(8,128)} %b.3) | copy-start | bytes 3145732
  0.0 16.0 %copy-start = (s32[32,64,128]{2,1,0:T(8,128)S(1)}, s32[32,64,128]{2,1,0:T(8,128)}, u32[]{:S(2)}) copy-start(s32[32,64,128]{2,1,0:T(8,128)} %lab.3) | copy-start | bytes 3145732
  2.1 7.7 %collective-permute-start = (f32[7,64,128]{2,1,0:T(8,128)S(1)}, f32[7,64,128]{2,1,0:T(8,128)S(1)}, u32[]{:S(2)}, u32[]{:S(2)}) collective-permute-start(f32[7,64,128]{2,1,0:T(8,128)S(1)} %get-tuple-element.25), channel_id=1, source_target_pairs={{0,96},{32,0},{64,32},{96,64},{1,97},{33,1},{65,33},{97,65},{2,98}... | collective-permute-start | bytes 688136 | tf_op jit(solution)/shard_map/ppermute | solution.py:18
  5.5 7.4 %collective-permute-start.1 = (f32[7,64,128]{2,1,0:T(8,128)S(1)}, f32[7,64,128]{2,1,0:T(8,128)S(1)}, u32[]{:S(2)}, u32[]{:S(2)}) collective-permute-start(f32[7,64,128]{2,1,0:T(8,128)S(1)} %get-tuple-element.26), channel_id=1, source_target_pairs={{0,32},{32,64},{64,96},{96,0},{1,33},{33,65},{65,97},{97,1},{2,34}... | collective-permute-start | bytes 688136 | tf_op jit(solution)/shard_map/ppermute | solution.py:18
  12.9 10.7 %copy-start.2 = (f32[7,8]{1,0:T(8,128)S(1)}, f32[7,8]{1,0:T(8,128)}, u32[]{:S(2)}) copy-start(f32[7,8]{1,0:T(8,128)} %cond.3) | copy-start | bytes 676
  13.0 6.0 %collective-permute-start.2 = (f32[40,8,128]{2,1,0:T(8,128)S(1)}, f32[40,8,128]{2,1,0:T(8,128)S(1)}, u32[]{:S(2)}, u32[]{:S(2)}) collective-permute-start(f32[40,8,128]{2,1,0:T(8,128)S(1)} %get-tuple-element.27), channel_id=1, source_target_pairs={{0,28},{4,0},{8,4},{12,8},{16,12},{20,16},{24,20},{28,24},{1,29},{... | collective-permute-start | bytes 491528 | tf_op jit(solution)/shard_map/ppermute | solution.py:18
  14.8 4.2 %collective-permute-start.3 = (f32[40,8,128]{2,1,0:T(8,128)S(1)}, f32[40,8,128]{2,1,0:T(8,128)S(1)}, u32[]{:S(2)}, u32[]{:S(2)}) collective-permute-start(f32[40,8,128]{2,1,0:T(8,128)S(1)} %get-tuple-element.28), channel_id=1, source_target_pairs={{0,4},{4,8},{8,12},{12,16},{16,20},{20,24},{24,28},{28,0},{1,5},{5... | collective-permute-start | bytes 491528 | tf_op jit(solution)/shard_map/ppermute | solution.py:18
  19.8 6.4 %collective-permute-start.4 = (f32[3,80,128]{2,1,0:T(8,128)S(1)}, f32[3,80,128]{2,1,0:T(8,128)S(1)}, u32[]{:S(2)}, u32[]{:S(2)}) collective-permute-start(f32[3,80,128]{2,1,0:T(8,128)S(1)} %get-tuple-element.39.zu_own), channel_id=1, source_target_pairs={{0,3},{1,0},{2,1},{3,2},{4,7},{5,4},{6,5},{7,6},{8,11},{9,8},{10,9... | collective-permute-start | bytes 368648 | tf_op jit(solution)/shard_map/ppermute | solution.py:18
  23.7 4.9 %collective-permute-start.5 = (f32[3,80,128]{2,1,0:T(8,128)S(1)}, f32[3,80,128]{2,1,0:T(8,128)S(1)}, u32[]{:S(2)}, u32[]{:S(2)}) collective-permute-start(f32[3,80,128]{2,1,0:T(8,128)S(1)} %get-tuple-element.40.zd_own), channel_id=1, source_target_pairs={{0,1},{1,2},{2,3},{3,0},{4,5},{5,6},{6,7},{7,4},{8,9},{9,10},{10,1... | collective-permute-start | bytes 368648 | tf_op jit(solution)/shard_map/ppermute | solution.py:18

commit v6 on v5

--- a/solution.py
+++ b/solution.py
@@ -565,7 +565,7 @@
     mom[...] = jnp.broadcast_to(line, mom.shape)
 
 
-def combine(mom, w0, w1, w2, out):
+def combine(mom, w0, w1, w2, out, held, sems):
     total = jnp.sum(mom[...], axis=0, keepdims=True)
     at = iota((1, 128), 1)
     m = [jnp.sum(jnp.where(at == k, total, 0.0), axis=1, keepdims=True) for k in range(7)]
@@ -589,11 +589,18 @@
     c1 = ratio(g1, d1, tiny * a[2]) - l21 * c2
     c0 = (m[0] - a[1] * c1 - a[2] * c2) / a[0]
 
-    def plane(x, carry):
-        out[x] = c0 * w0[x] + c1 * w1[x] + c2 * w2[x]
-        return carry
-
-    lax.fori_loop(0, NX, plane, 0)
+    step = NX // 4
+
+    def send(i):
+        part = pl.ds(step * i, step)
+        return pltpu.make_async_copy(held.at[part], out.at[part], sems.at[i])
+
+    for i in range(4):
+        part = pl.ds(step * i, step)
+        held[part] = c0 * w0[part] + c1 * w1[part] + c2 * w2[part]
+        send(i).start()
+    for i in range(4):
+        send(i).wait()
 
 
 def vmem():
@@ -664,7 +671,15 @@
         name="sweeps",
     )(conductivity, *tables, zu_own, zd_own, zu, zd)
     mom = lax.all_to_all(mom, ALL, 0, 0, tiled=True)
-    return call(combine, 4, block, 6)(mom, w0, w1, w2)
+    return pl.pallas_call(
+        combine,
+        in_specs=[vmem()] * 4,
+        out_specs=pl.BlockSpec(memory_space=pl.ANY),
+        out_shape=block,
+        scratch_shapes=[pltpu.VMEM((NX, NY, NZ), F32), pltpu.SemaphoreType.DMA((4,))],
+        compiler_params=pltpu.CompilerParams(vmem_limit_bytes=6 * 2**20),
+        name="combine",
+    )(mom, w0, w1, w2)
 
 
 def call(kernel, inputs, shapes, mib):

time: 64.7 us -> 64.5 us (level)
  no operation moved by 1% of the time
where the time goes in v6:
time: 64.5 us; the launch traced here: 64.3 us
  Pallas kernels  23.1 us (36%)
  blocking collectives  17.1 us (27%)
  waiting for transfers between devices  10.6 us (16%)
  starting transfers between devices  10.2 us (16%)
  local copies, waits for them, and re-layouts  3.11 us (5%)
    pallas_call x1, Pallas kernels, local(): pl.pallas_call(sweeps, in_specs=[pl.BlockSpec(memory_space=pltpu.SMEM)] +...  17.3 us
    all_to_all x1, blocking collectives, local(): mom = lax.all_to_all(mom, ALL, 0, 0, tiled=True)  17.1 us
    ppermute x6, waiting for transfers between devices, ring(): lax.ppermute(arr, axis, [(i, (i + step) % count) for i in range(count)])  10.6 us
    ppermute x6, starting transfers between devices, ring(): lax.ppermute(arr, axis, [(i, (i + step) % count) for i in range(count)])  10.2 us
    pallas_call x1, Pallas kernels, local(): pl.pallas_call(faces, in_specs=[pl.BlockSpec(memory_space=pltpu.SMEM)] +...  2.56 us
  transfers between devices with their start and end apart: 6, of which 4 were waited for; matrix products, arithmetic and copies ran while one was open for 2% of the time, Pallas kernels for 6%

profile of v6, /device:TPU:1, one launch (start us, length us, event | category | flops | bytes accessed | tf_op | source)
XLA Modules:
  0.0 64.3 jit_solution(2998220705902635270)
XLA Ops:
  0.0 0.0 copy-start.1
  0.0 0.0 copy-start
  0.0 1.1 %fusion.2 = (f32[3,64,128]{2,1,0:T(8,128)S(1)}, f32[3,64,128]{2,1,0:T(8,128)S(1)}) fusion(f32[32,64,128]{2,1,0:T(8,128)} %b.3), kind=kLoop, calls=%fused_computation.2 | loop fusion | bytes 393216 | tf_op jit(solution)/shard_map/slice | solution.py:621
  1.1 1.0 %fusion.3 = (s32[4,64,128]{2,1,0:T(8,128)S(1)}, s32[4,64,128]{2,1,0:T(8,128)S(1)}) fusion(s32[32,64,128]{2,1,0:T(8,128)} %lab.3), kind=kLoop, calls=%fused_computation.3 | loop fusion | bytes 524288 | tf_op jit(solution)/shard_map/slice | solution.py:621
  2.1 3.4 %collective-permute-start = (f32[7,64,128]{2,1,0:T(8,128)S(1)}, f32[7,64,128]{2,1,0:T(8,128)S(1)}, u32[]{:S(2)}, u32[]{:S(2)}) collective-permute-start(f32[7,64,128]{2,1,0:T(8,128)S(1)} %get-tuple-element.25), channel_id=1, source_target_pairs={{0,96},{32,0},{64,32},{96,64},{1,97},{33,1},{65,33},{97,65},{2,98}... | collective-permute-start | bytes 688136 | tf_op jit(solution)/shard_map/ppermute | solution.py:18
  5.5 0.0 collective-permute-start.1
  5.5 1.0 %fusion.1 = (s32[32,8,128]{2,1,0:T(8,128)S(1)}, s32[32,8,128]{2,1,0:T(8,128)S(1)}) fusion(s32[32,64,128]{2,1,0:T(8,128)} %lab.3), kind=kLoop, calls=%fused_computation.1 | loop fusion | bytes 524288 | tf_op jit(solution)/shard_map/slice | solution.py:639
  6.5 0.0 copy-done.1
  6.5 3.3 %collective-permute-done.xu = f32[7,64,128]{2,1,0:T(8,128)S(1)} collective-permute-done((f32[7,64,128]{2,1,0:T(8,128)S(1)}, f32[7,64,128]{2,1,0:T(8,128)S(1)}, u32[]{:S(2)}, u32[]{:S(2)}) %collective-permute-start) | collective-permute-done | bytes 229408 | tf_op jit(solution)/shard_map/ppermute | solution.py:18
  9.8 3.1 %collective-permute-done.1.xl = f32[7,64,128]{2,1,0:T(8,128)S(1)} collective-permute-done((f32[7,64,128]{2,1,0:T(8,128)S(1)}, f32[7,64,128]{2,1,0:T(8,128)S(1)}, u32[]{:S(2)}, u32[]{:S(2)}) %collective-permute-start.1) | collective-permute-done | bytes 229408 | tf_op jit(solution)/shard_map/ppermute | solution.py:18
  12.9 0.0 copy-start.2
  13.0 1.8 %collective-permute-start.2 = (f32[40,8,128]{2,1,0:T(8,128)S(1)}, f32[40,8,128]{2,1,0:T(8,128)S(1)}, u32[]{:S(2)}, u32[]{:S(2)}) collective-permute-start(f32[40,8,128]{2,1,0:T(8,128)S(1)} %get-tuple-element.27), channel_id=1, source_target_pairs={{0,28},{4,0},{8,4},{12,8},{16,12},{20,16},{24,20},{28,24},{1,29},{... | collective-permute-start | bytes 491528 | tf_op jit(solution)/shard_map/ppermute | solution.py:18
  14.8 1.2 %collective-permute-start.3 = (f32[40,8,128]{2,1,0:T(8,128)S(1)}, f32[40,8,128]{2,1,0:T(8,128)S(1)}, u32[]{:S(2)}, u32[]{:S(2)}) collective-permute-start(f32[40,8,128]{2,1,0:T(8,128)S(1)} %get-tuple-element.28), channel_id=1, source_target_pairs={{0,4},{4,8},{8,12},{12,16},{16,20},{20,24},{24,28},{28,0},{1,5},{5... | collective-permute-start | bytes 491528 | tf_op jit(solution)/shard_map/ppermute | solution.py:18
  16.0 0.0 copy-done
  16.0 1.1 %pack_own.1 = (f32[3,64,128]{2,1,0:T(8,128)S(1)}, f32[3,64,128]{2,1,0:T(8,128)S(1)}) custom-call(s32[32,64,128]{2,1,0:T(8,128)S(1)} %copy-done, f32[32,64,128]{2,1,0:T(8,128)S(1)} %copy-done.1), custom_call_target="tpu_custom_call" | custom-call | flops 4000000 | tf_op jit(solution)/shard_map/pack_own/pallas_call | solution.py:627
  17.1 1.9 %collective-permute-done.2.yu = f32[40,8,128]{2,1,0:T(8,128)S(1)} collective-permute-done((f32[40,8,128]{2,1,0:T(8,128)S(1)}, f32[40,8,128]{2,1,0:T(8,128)S(1)}, u32[]{:S(2)}, u32[]{:S(2)}) %collective-permute-start.2) | collective-permute-done | bytes 163872 | tf_op jit(solution)/shard_map/ppermute | solution.py:18
  19.0 0.0 collective-permute-done.3.yd
  19.0 0.9 %pack_lanes.1 = (f32[3,80,128]{2,1,0:T(8,128)S(1)}, f32[3,80,128]{2,1,0:T(8,128)S(1)}) custom-call(f32[3,64,128]{2,1,0:T(8,128)S(1)} %get-tuple-element.37.lab_part, f32[3,64,128]{2,1,0:T(8,128)S(1)} %get-tuple-element.38.b_part, f32[7,64,128]{2,1,0:T(8,128)S(1)} %collective-permute-done.xu, f32[7,64,128]{2,1,0:T(8,128)S(1)} %collective-permute-done.1.xl, ...), custom_call_target="tpu_custom_call" | custom-call | tf_op jit(solution)/shard_map/pack_lanes/pallas_call | solution.py:645
  19.8 3.8 %collective-permute-start.4 = (f32[3,80,128]{2,1,0:T(8,128)S(1)}, f32[3,80,128]{2,1,0:T(8,128)S(1)}, u32[]{:S(2)}, u32[]{:S(2)}) collective-permute-start(f32[3,80,128]{2,1,0:T(8,128)S(1)} %get-tuple-element.39.zu_own), channel_id=1, source_target_pairs={{0,3},{1,0},{2,1},{3,2},{4,7},{5,4},{6,5},{7,6},{8,11},{9,8},{10,9... | collective-permute-start | bytes 368648 | tf_op jit(solution)/shard_map/ppermute | solution.py:18
  23.7 0.0 collective-permute-start.5
  23.7 0.0 copy-done.2
  23.7 2.6 %faces.1 = (f32[42,88,128]{2,1,0:T(8,128)S(1)}, f32[42,88,128]{2,1,0:T(8,128)S(1)}, f32[42,88,128]{2,1,0:T(8,128)S(1)}, f32[42,88,128]{2,1,0:T(8,128)S(1)}, f32[...) custom-call(f32[7,8]{1,0:T(8,128)S(1)} %copy-done.2, ...), custom_call_target="tpu_custom_call" | custom-call | flops 8000000 | tf_op jit(solution)/shard_map/faces/pallas_call | solution.py:652
  26.2 0.0 collective-permute-done.4.zu
  26.3 2.4 %collective-permute-done.5.zd = f32[3,80,128]{2,1,0:T(8,128)S(1)} collective-permute-done((f32[3,80,128]{2,1,0:T(8,128)S(1)}, f32[3,80,128]{2,1,0:T(8,128)S(1)}, u32[]{:S(2)}, u32[]{:S(2)}) %collective-permute-start.5) | collective-permute-done | bytes 122912 | tf_op jit(solution)/shard_map/ppermute | solution.py:18
  28.6 17.3 %sweeps.1 = (f32[32,64,128]{2,1,0:T(8,128)S(1)}, f32[32,64,128]{2,1,0:T(8,128)S(1)}, f32[32,64,128]{2,1,0:T(8,128)S(1)}, f32[128,128]{1,0:T(8,128)S(1)}) custom-call(f32[7,8]{1,0:T(8,128)S(1)} %copy-done.2, f32[42,88,128]{2,1,0:T(8,128)S(1)} %get-tuple-element.29.f0, f32[42,88,128]{2,1,0:T(8,128)S(1)} %get-tuple-element.30.f1, ...), custom_call_target="tpu_custom_call" | custom-call | tf_op jit(solution)/shard_map/sweeps/pallas_call | solution.py:662
  45.9 17.1 %all_to_all.11 = f32[128,1,128]{2,1,0:T(1,128)S(1)} all-to-all(f32[128,1,128]{2,1,0:T(1,128)S(1)} %bitcast.5), channel_id=1, replica_groups=mesh['gx'=4,'gy'=8,'gz'=4] {'gx','gy','gz'}, dimensions={0} | all-to-all | bytes 131072 | tf_op jit(solution)/shard_map/all_to_all | solution.py:673
  63.1 1.2 %combine.1 = f32[32,64,128]{2,1,0:T(8,128)} custom-call(f32[128,128]{1,0:T(8,128)S(1)} %bitcast.4, f32[32,64,128]{2,1,0:T(8,128)S(1)} %get-tuple-element.42.w0, f32[32,64,128]{2,1,0:T(8,128)S(1)} %get-tuple-element.43.w1, f32[32,64,128]{2,1,0:T(8,128)S(1)} %get-tuple-element.44.w2), custom_call_target="tpu_custom_call" | custom-call | tf_op jit(solution)/shard_map/combine/pallas_call | solution.py:674
  (3 shorter events, 0.1 us)
Async XLA Ops:
  0.0 6.5 %copy-start.1 = (f32[32,64,128]{2,1,0:T(8,128)S(1)}, f32[32,64,128]{2,1,0:T(8,128)}, u32[]{:S(2)}) copy-start(f32[32,64,128]{2,1,0:T(8,128)} %b.3) | copy-start | bytes 3145732
  0.0 16.0 %copy-start = (s32[32,64,128]{2,1,0:T(8,128)S(1)}, s32[32,64,128]{2,1,0:T(8,128)}, u32[]{:S(2)}) copy-start(s32[32,64,128]{2,1,0:T(8,128)} %lab.3) | copy-start | bytes 3145732
  2.1 7.7 %collective-permute-start = (f32[7,64,128]{2,1,0:T(8,128)S(1)}, f32[7,64,128]{2,1,0:T(8,128)S(1)}, u32[]{:S(2)}, u32[]{:S(2)}) collective-permute-start(f32[7,64,128]{2,1,0:T(8,128)S(1)} %get-tuple-element.25), channel_id=1, source_target_pairs={{0,96},{32,0},{64,32},{96,64},{1,97},{33,1},{65,33},{97,65},{2,98}... | collective-permute-start | bytes 688136 | tf_op jit(solution)/shard_map/ppermute | solution.py:18
  5.5 7.4 %collective-permute-start.1 = (f32[7,64,128]{2,1,0:T(8,128)S(1)}, f32[7,64,128]{2,1,0:T(8,128)S(1)}, u32[]{:S(2)}, u32[]{:S(2)}) collective-permute-start(f32[7,64,128]{2,1,0:T(8,128)S(1)} %get-tuple-element.26), channel_id=1, source_target_pairs={{0,32},{32,64},{64,96},{96,0},{1,33},{33,65},{65,97},{97,1},{2,34}... | collective-permute-start | bytes 688136 | tf_op jit(solution)/shard_map/ppermute | solution.py:18
  12.9 10.7 %copy-start.2 = (f32[7,8]{1,0:T(8,128)S(1)}, f32[7,8]{1,0:T(8,128)}, u32[]{:S(2)}) copy-start(f32[7,8]{1,0:T(8,128)} %cond.3) | copy-start | bytes 676
  13.0 6.0 %collective-permute-start.2 = (f32[40,8,128]{2,1,0:T(8,128)S(1)}, f32[40,8,128]{2,1,0:T(8,128)S(1)}, u32[]{:S(2)}, u32[]{:S(2)}) collective-permute-start(f32[40,8,128]{2,1,0:T(8,128)S(1)} %get-tuple-element.27), channel_id=1, source_target_pairs={{0,28},{4,0},{8,4},{12,8},{16,12},{20,16},{24,20},{28,24},{1,29},{... | collective-permute-start | bytes 491528 | tf_op jit(solution)/shard_map/ppermute | solution.py:18
  14.8 4.2 %collective-permute-start.3 = (f32[40,8,128]{2,1,0:T(8,128)S(1)}, f32[40,8,128]{2,1,0:T(8,128)S(1)}, u32[]{:S(2)}, u32[]{:S(2)}) collective-permute-start(f32[40,8,128]{2,1,0:T(8,128)S(1)} %get-tuple-element.28), channel_id=1, source_target_pairs={{0,4},{4,8},{8,12},{12,16},{16,20},{20,24},{24,28},{28,0},{1,5},{5... | collective-permute-start | bytes 491528 | tf_op jit(solution)/shard_map/ppermute | solution.py:18
  19.8 6.4 %collective-permute-start.4 = (f32[3,80,128]{2,1,0:T(8,128)S(1)}, f32[3,80,128]{2,1,0:T(8,128)S(1)}, u32[]{:S(2)}, u32[]{:S(2)}) collective-permute-start(f32[3,80,128]{2,1,0:T(8,128)S(1)} %get-tuple-element.39.zu_own), channel_id=1, source_target_pairs={{0,3},{1,0},{2,1},{3,2},{4,7},{5,4},{6,5},{7,6},{8,11},{9,8},{10,9... | collective-permute-start | bytes 368648 | tf_op jit(solution)/shard_map/ppermute | solution.py:18
  23.7 4.9 %collective-permute-start.5 = (f32[3,80,128]{2,1,0:T(8,128)S(1)}, f32[3,80,128]{2,1,0:T(8,128)S(1)}, u32[]{:S(2)}, u32[]{:S(2)}) collective-permute-start(f32[3,80,128]{2,1,0:T(8,128)S(1)} %get-tuple-element.40.zd_own), channel_id=1, source_target_pairs={{0,1},{1,2},{2,3},{3,0},{4,5},{5,6},{6,7},{7,4},{8,9},{9,10},{10,1... | collective-permute-start | bytes 368648 | tf_op jit(solution)/shard_map/ppermute | solution.py:18

commit v7 on v5

--- a/solution.py
+++ b/solution.py
@@ -371,6 +371,8 @@
                 inv[xp, at] = r
                 mid[xp, at] = jnp.where(inside, theta * total, 0.0)
                 put(v0, xp, g, w)
+                if acc is not None and g < 8:
+                    w0o[xp - 4, pl.ds(8 * g, 8)] = w
                 f2[xp, at] = a2 + right
                 f2l[xp, at] = a2 + left
                 parts.append(b * w)
@@ -380,7 +382,7 @@
 
     nu0 = blocks(diag_block, 3, none)
 
-    def apply(v, w, qv, qw, extra, last):
+    def apply(v, w, wo, qv, qw, extra, last):
         def q_first(xp):
             at = pl.ds(xp + 1, QB)
             x = qv[at]
@@ -507,6 +509,8 @@
                     dots.append(x * r)
                     out = r * inv[xp, at]
                     put(w, xp, g, out)
+                    if acc is not None and g < 8:
+                        wo[xp - 4, pl.ds(8 * g, 8)] = out
                     norms.append(out * r)
                 if acc is None or g == 8:
                     return acc
@@ -545,17 +549,10 @@
             )
         return out
 
-    nu1, nu2 = apply(v0, v1, qv0, qv1, 2, False)
-    nu3, nu4 = apply(v1, v2, qv1, qv2, 1, False)
-    nu5, _ = apply(v2, None, qv2, None, 0, True)
-
-    def store(x, carry):
-        w0o[x] = v0[x + 4, OWN]
-        w1o[x] = v1[x + 4, OWN]
-        w2o[x] = v2[x + 4, OWN]
-        return carry
-
-    lax.fori_loop(0, NX, store, 0)
+    nu1, nu2 = apply(v0, v1, w1o, qv0, qv1, 2, False)
+    nu3, nu4 = apply(v1, v2, w2o, qv1, qv2, 1, False)
+    nu5, _ = apply(v2, None, None, qv2, None, 0, True)
+
     line = jnp.zeros((1, 128), F32)
     at = iota((1, 128), 1)
     line = jnp.where(at == 6, theta, line)

time: 64.7 us -> 64.1 us (level)
  no operation moved by 1% of the time
where the time goes in v7:
time: 64.1 us; the launch traced here: 63.9 us
  Pallas kernels  22.7 us (35%)
  blocking collectives  17.1 us (27%)
  waiting for transfers between devices  10.6 us (17%)
  starting transfers between devices  10.2 us (16%)
  local copies, waits for them, and re-layouts  3.11 us (5%)
    all_to_all x1, blocking collectives, local(): mom = lax.all_to_all(mom, ALL, 0, 0, tiled=True)  17.1 us
    pallas_call x1, Pallas kernels, local(): pl.pallas_call(sweeps, in_specs=[pl.BlockSpec(memory_space=pltpu.SMEM)] +...  16.7 us
    ppermute x6, waiting for transfers between devices, ring(): lax.ppermute(arr, axis, [(i, (i + step) % count) for i in range(count)])  10.6 us
    ppermute x6, starting transfers between devices, ring(): lax.ppermute(arr, axis, [(i, (i + step) % count) for i in range(count)])  10.2 us
    pallas_call x1, Pallas kernels, local(): pl.pallas_call(faces, in_specs=[pl.BlockSpec(memory_space=pltpu.SMEM)] +...  2.56 us
    pallas_call x1, Pallas kernels, local(): return call(combine, 4, block, 6)(mom, w0, w1, w2)  1.44 us
  transfers between devices with their start and end apart: 6, of which 4 were waited for; matrix products, arithmetic and copies ran while one was open for 2% of the time, Pallas kernels for 6%

profile of v7, /device:TPU:1, one launch (start us, length us, event | category | flops | bytes accessed | tf_op | source)
XLA Modules:
  0.0 63.9 jit_solution(6518945462107046548)
XLA Ops:
  0.0 0.0 copy-start.1
  0.0 0.0 copy-start
  0.0 1.1 %fusion.2 = (f32[3,64,128]{2,1,0:T(8,128)S(1)}, f32[3,64,128]{2,1,0:T(8,128)S(1)}) fusion(f32[32,64,128]{2,1,0:T(8,128)} %b.3), kind=kLoop, calls=%fused_computation.2 | loop fusion | bytes 393216 | tf_op jit(solution)/shard_map/slice | solution.py:611
  1.1 1.0 %fusion.3 = (s32[4,64,128]{2,1,0:T(8,128)S(1)}, s32[4,64,128]{2,1,0:T(8,128)S(1)}) fusion(s32[32,64,128]{2,1,0:T(8,128)} %lab.3), kind=kLoop, calls=%fused_computation.3 | loop fusion | bytes 524288 | tf_op jit(solution)/shard_map/slice | solution.py:611
  2.1 3.4 %collective-permute-start = (f32[7,64,128]{2,1,0:T(8,128)S(1)}, f32[7,64,128]{2,1,0:T(8,128)S(1)}, u32[]{:S(2)}, u32[]{:S(2)}) collective-permute-start(f32[7,64,128]{2,1,0:T(8,128)S(1)} %get-tuple-element.25), channel_id=1, source_target_pairs={{0,96},{32,0},{64,32},{96,64},{1,97},{33,1},{65,33},{97,65},{2,98}... | collective-permute-start | bytes 688136 | tf_op jit(solution)/shard_map/ppermute | solution.py:18
  5.5 0.0 collective-permute-start.1
  5.5 1.0 %fusion.1 = (s32[32,8,128]{2,1,0:T(8,128)S(1)}, s32[32,8,128]{2,1,0:T(8,128)S(1)}) fusion(s32[32,64,128]{2,1,0:T(8,128)} %lab.3), kind=kLoop, calls=%fused_computation.1 | loop fusion | bytes 524288 | tf_op jit(solution)/shard_map/slice | solution.py:629
  6.5 0.0 copy-done.1
  6.5 3.3 %collective-permute-done.xu = f32[7,64,128]{2,1,0:T(8,128)S(1)} collective-permute-done((f32[7,64,128]{2,1,0:T(8,128)S(1)}, f32[7,64,128]{2,1,0:T(8,128)S(1)}, u32[]{:S(2)}, u32[]{:S(2)}) %collective-permute-start) | collective-permute-done | bytes 229408 | tf_op jit(solution)/shard_map/ppermute | solution.py:18
  9.8 3.1 %collective-permute-done.1.xl = f32[7,64,128]{2,1,0:T(8,128)S(1)} collective-permute-done((f32[7,64,128]{2,1,0:T(8,128)S(1)}, f32[7,64,128]{2,1,0:T(8,128)S(1)}, u32[]{:S(2)}, u32[]{:S(2)}) %collective-permute-start.1) | collective-permute-done | bytes 229408 | tf_op jit(solution)/shard_map/ppermute | solution.py:18
  12.9 0.0 copy-start.2
  13.0 1.8 %collective-permute-start.2 = (f32[40,8,128]{2,1,0:T(8,128)S(1)}, f32[40,8,128]{2,1,0:T(8,128)S(1)}, u32[]{:S(2)}, u32[]{:S(2)}) collective-permute-start(f32[40,8,128]{2,1,0:T(8,128)S(1)} %get-tuple-element.27), channel_id=1, source_target_pairs={{0,28},{4,0},{8,4},{12,8},{16,12},{20,16},{24,20},{28,24},{1,29},{... | collective-permute-start | bytes 491528 | tf_op jit(solution)/shard_map/ppermute | solution.py:18
  14.8 1.2 %collective-permute-start.3 = (f32[40,8,128]{2,1,0:T(8,128)S(1)}, f32[40,8,128]{2,1,0:T(8,128)S(1)}, u32[]{:S(2)}, u32[]{:S(2)}) collective-permute-start(f32[40,8,128]{2,1,0:T(8,128)S(1)} %get-tuple-element.28), channel_id=1, source_target_pairs={{0,4},{4,8},{8,12},{12,16},{16,20},{20,24},{24,28},{28,0},{1,5},{5... | collective-permute-start | bytes 491528 | tf_op jit(solution)/shard_map/ppermute | solution.py:18
  16.0 0.0 copy-done
  16.0 1.1 %pack_own.1 = (f32[3,64,128]{2,1,0:T(8,128)S(1)}, f32[3,64,128]{2,1,0:T(8,128)S(1)}) custom-call(s32[32,64,128]{2,1,0:T(8,128)S(1)} %copy-done, f32[32,64,128]{2,1,0:T(8,128)S(1)} %copy-done.1), custom_call_target="tpu_custom_call" | custom-call | flops 4000000 | tf_op jit(solution)/shard_map/pack_own/pallas_call | solution.py:617
  17.1 1.9 %collective-permute-done.2.yu = f32[40,8,128]{2,1,0:T(8,128)S(1)} collective-permute-done((f32[40,8,128]{2,1,0:T(8,128)S(1)}, f32[40,8,128]{2,1,0:T(8,128)S(1)}, u32[]{:S(2)}, u32[]{:S(2)}) %collective-permute-start.2) | collective-permute-done | bytes 163872 | tf_op jit(solution)/shard_map/ppermute | solution.py:18
  19.0 0.0 collective-permute-done.3.yd
  19.0 0.9 %pack_lanes.1 = (f32[3,80,128]{2,1,0:T(8,128)S(1)}, f32[3,80,128]{2,1,0:T(8,128)S(1)}) custom-call(f32[3,64,128]{2,1,0:T(8,128)S(1)} %get-tuple-element.37.lab_part, f32[3,64,128]{2,1,0:T(8,128)S(1)} %get-tuple-element.38.b_part, f32[7,64,128]{2,1,0:T(8,128)S(1)} %collective-permute-done.xu, f32[7,64,128]{2,1,0:T(8,128)S(1)} %collective-permute-done.1.xl, ...), custom_call_target="tpu_custom_call" | custom-call | tf_op jit(solution)/shard_map/pack_lanes/pallas_call | solution.py:635
  19.8 3.8 %collective-permute-start.4 = (f32[3,80,128]{2,1,0:T(8,128)S(1)}, f32[3,80,128]{2,1,0:T(8,128)S(1)}, u32[]{:S(2)}, u32[]{:S(2)}) collective-permute-start(f32[3,80,128]{2,1,0:T(8,128)S(1)} %get-tuple-element.39.zu_own), channel_id=1, source_target_pairs={{0,3},{1,0},{2,1},{3,2},{4,7},{5,4},{6,5},{7,6},{8,11},{9,8},{10,9... | collective-permute-start | bytes 368648 | tf_op jit(solution)/shard_map/ppermute | solution.py:18
  23.7 0.0 collective-permute-start.5
  23.7 0.0 copy-done.2
  23.7 2.6 %faces.1 = (f32[42,88,128]{2,1,0:T(8,128)S(1)}, f32[42,88,128]{2,1,0:T(8,128)S(1)}, f32[42,88,128]{2,1,0:T(8,128)S(1)}, f32[42,88,128]{2,1,0:T(8,128)S(1)}, f32[...) custom-call(f32[7,8]{1,0:T(8,128)S(1)} %copy-done.2, ...), custom_call_target="tpu_custom_call" | custom-call | flops 8000000 | tf_op jit(solution)/shard_map/faces/pallas_call | solution.py:642
  26.2 0.0 collective-permute-done.4.zu
  26.3 2.4 %collective-permute-done.5.zd = f32[3,80,128]{2,1,0:T(8,128)S(1)} collective-permute-done((f32[3,80,128]{2,1,0:T(8,128)S(1)}, f32[3,80,128]{2,1,0:T(8,128)S(1)}, u32[]{:S(2)}, u32[]{:S(2)}) %collective-permute-start.5) | collective-permute-done | bytes 122912 | tf_op jit(solution)/shard_map/ppermute | solution.py:18
  28.6 16.7 %sweeps.1 = (f32[32,64,128]{2,1,0:T(8,128)S(1)}, f32[32,64,128]{2,1,0:T(8,128)S(1)}, f32[32,64,128]{2,1,0:T(8,128)S(1)}, f32[128,128]{1,0:T(8,128)S(1)}) custom-call(f32[7,8]{1,0:T(8,128)S(1)} %copy-done.2, f32[42,88,128]{2,1,0:T(8,128)S(1)} %get-tuple-element.29.f0, f32[42,88,128]{2,1,0:T(8,128)S(1)} %get-tuple-element.30.f1, ...), custom_call_target="tpu_custom_call" | custom-call | tf_op jit(solution)/shard_map/sweeps/pallas_call | solution.py:652
  45.4 17.1 %all_to_all.11 = f32[128,1,128]{2,1,0:T(1,128)S(1)} all-to-all(f32[128,1,128]{2,1,0:T(1,128)S(1)} %bitcast.5), channel_id=1, replica_groups=mesh['gx'=4,'gy'=8,'gz'=4] {'gx','gy','gz'}, dimensions={0} | all-to-all | bytes 131072 | tf_op jit(solution)/shard_map/all_to_all | solution.py:663
  62.5 1.4 %combine.1 = f32[32,64,128]{2,1,0:T(8,128)} custom-call(f32[128,128]{1,0:T(8,128)S(1)} %bitcast.4, f32[32,64,128]{2,1,0:T(8,128)S(1)} %get-tuple-element.42.w0, f32[32,64,128]{2,1,0:T(8,128)S(1)} %get-tuple-element.43.w1, f32[32,64,128]{2,1,0:T(8,128)S(1)} %get-tuple-element.44.w2), custom_call_target="tpu_custom_call" | custom-call | tf_op jit(solution)/shard_map/combine/pallas_call | solution.py:664
  (3 shorter events, 0.1 us)
Async XLA Ops:
  0.0 6.5 %copy-start.1 = (f32[32,64,128]{2,1,0:T(8,128)S(1)}, f32[32,64,128]{2,1,0:T(8,128)}, u32[]{:S(2)}) copy-start(f32[32,64,128]{2,1,0:T(8,128)} %b.3) | copy-start | bytes 3145732
  0.0 16.0 %copy-start = (s32[32,64,128]{2,1,0:T(8,128)S(1)}, s32[32,64,128]{2,1,0:T(8,128)}, u32[]{:S(2)}) copy-start(s32[32,64,128]{2,1,0:T(8,128)} %lab.3) | copy-start | bytes 3145732
  2.1 7.7 %collective-permute-start = (f32[7,64,128]{2,1,0:T(8,128)S(1)}, f32[7,64,128]{2,1,0:T(8,128)S(1)}, u32[]{:S(2)}, u32[]{:S(2)}) collective-permute-start(f32[7,64,128]{2,1,0:T(8,128)S(1)} %get-tuple-element.25), channel_id=1, source_target_pairs={{0,96},{32,0},{64,32},{96,64},{1,97},{33,1},{65,33},{97,65},{2,98}... | collective-permute-start | bytes 688136 | tf_op jit(solution)/shard_map/ppermute | solution.py:18
  5.5 7.4 %collective-permute-start.1 = (f32[7,64,128]{2,1,0:T(8,128)S(1)}, f32[7,64,128]{2,1,0:T(8,128)S(1)}, u32[]{:S(2)}, u32[]{:S(2)}) collective-permute-start(f32[7,64,128]{2,1,0:T(8,128)S(1)} %get-tuple-element.26), channel_id=1, source_target_pairs={{0,32},{32,64},{64,96},{96,0},{1,33},{33,65},{65,97},{97,1},{2,34}... | collective-permute-start | bytes 688136 | tf_op jit(solution)/shard_map/ppermute | solution.py:18
  12.9 10.7 %copy-start.2 = (f32[7,8]{1,0:T(8,128)S(1)}, f32[7,8]{1,0:T(8,128)}, u32[]{:S(2)}) copy-start(f32[7,8]{1,0:T(8,128)} %cond.3) | copy-start | bytes 676
  13.0 6.0 %collective-permute-start.2 = (f32[40,8,128]{2,1,0:T(8,128)S(1)}, f32[40,8,128]{2,1,0:T(8,128)S(1)}, u32[]{:S(2)}, u32[]{:S(2)}) collective-permute-start(f32[40,8,128]{2,1,0:T(8,128)S(1)} %get-tuple-element.27), channel_id=1, source_target_pairs={{0,28},{4,0},{8,4},{12,8},{16,12},{20,16},{24,20},{28,24},{1,29},{... | collective-permute-start | bytes 491528 | tf_op jit(solution)/shard_map/ppermute | solution.py:18
  14.8 4.2 %collective-permute-start.3 = (f32[40,8,128]{2,1,0:T(8,128)S(1)}, f32[40,8,128]{2,1,0:T(8,128)S(1)}, u32[]{:S(2)}, u32[]{:S(2)}) collective-permute-start(f32[40,8,128]{2,1,0:T(8,128)S(1)} %get-tuple-element.28), channel_id=1, source_target_pairs={{0,4},{4,8},{8,12},{12,16},{16,20},{20,24},{24,28},{28,0},{1,5},{5... | collective-permute-start | bytes 491528 | tf_op jit(solution)/shard_map/ppermute | solution.py:18
  19.8 6.4 %collective-permute-start.4 = (f32[3,80,128]{2,1,0:T(8,128)S(1)}, f32[3,80,128]{2,1,0:T(8,128)S(1)}, u32[]{:S(2)}, u32[]{:S(2)}) collective-permute-start(f32[3,80,128]{2,1,0:T(8,128)S(1)} %get-tuple-element.39.zu_own), channel_id=1, source_target_pairs={{0,3},{1,0},{2,1},{3,2},{4,7},{5,4},{6,5},{7,6},{8,11},{9,8},{10,9... | collective-permute-start | bytes 368648 | tf_op jit(solution)/shard_map/ppermute | solution.py:18
  23.7 4.9 %collective-permute-start.5 = (f32[3,80,128]{2,1,0:T(8,128)S(1)}, f32[3,80,128]{2,1,0:T(8,128)S(1)}, u32[]{:S(2)}, u32[]{:S(2)}) collective-permute-start(f32[3,80,128]{2,1,0:T(8,128)S(1)} %get-tuple-element.40.zd_own), channel_id=1, source_target_pairs={{0,1},{1,2},{2,3},{3,0},{4,5},{5,6},{6,7},{7,4},{8,9},{9,10},{10,1... | collective-permute-start | bytes 368648 | tf_op jit(solution)/shard_map/ppermute | solution.py:18
